TPU v7x, 256 devices: a whole 4x4x8 slice. The times are simulated.
256 devices in a mesh: maps: 16 (over z, y_hi), row: 4 (over y_lo, core), col: 4 (over x).
Axes of the slice: x: 4, y: 4 (y_hi: 2, y_lo: 2; y = y_hi * 2 + y_lo), z: 8, core: 2. Of those that a mesh axis runs over, the one named last changes fastest.
Arguments:
- shear: float32 [2, 16, 2048, 2048], P(None, 'maps', 'row', 'col'), parts along dimension 1, may hold values from -600 to 600
- smoothing: float32 [16], P('maps'), parts along dimension 0, may hold values from 0.6 to 1.2
- offsets: int32 [16, 128, 128], P('maps', ('row', 'col')), parts along dimension 0, may hold values from 0 to 255
- thresholds: int32 [16, 16], P('maps'), parts along dimension 0, may hold values from -4 to 19
Outputs:
- snr: float32 [16, 2048, 2048], P('maps', ('row', 'col')), parts along dimension 0
- heights: float32 [16, 128, 128], P('maps', ('row', 'col')), parts along dimension 0
- counts: float32 [16, 16], P('maps'), parts along dimension 0
There are 16 independent parts, one for each index of `maps`. A program takes and returns all parts, laid end to end along the dimension named above; each array names one. Nothing has to cross between parts.
All inputs are finite; a program needn't handle non-finite values.
Results may differ from a plain program's by a relative error of at most 0.00014.
Values sent between devices are 32-bit elements; how exact they have to be, the bound alone decides.
No kernel may reach another device: no remote copies, remote signals or barrier semaphores. Data moves between devices by JAX's collectives and lax.ppermute only.
A program may use at most 64 MiB of HBM per device.

v0:
```python
from functools import partial
import math

import jax
import jax.numpy as jnp
from jax import lax
from jax.sharding import PartitionSpec as P

NX = 2048
NY = 2048
RADIX = 16
CELL = 16


HIGH = lax.Precision.HIGHEST
peak_soft = 0.05
bin_soft = 0.1
bin_step = 0.25


def with_halo(x, sides, width):
    edges = {}
    for axis, dim in sides:
        size, length = (lax.axis_size(axis), x.shape[dim])
        up = [(i, (i + 1) % size) for i in range(size)]
        last = lax.slice_in_dim(x, length - width, length, axis=dim)
        initial = lax.slice_in_dim(x, 0, width, axis=dim)
        edges[dim] = (
            lax.ppermute(last, axis, up),
            lax.ppermute(initial, axis, [(b, a) for a, b in up]),
        )
    done = []
    for _, dim in sides:
        low, high = edges[dim]
        around = [(width, width) if d in done else (0, 0) for d in range(x.ndim)]
        x = jnp.concatenate([jnp.pad(low, around), x, jnp.pad(high, around)], axis=dim)
        done.append(dim)
    return x


def copy_for_each(x, axis):
    copies = jnp.broadcast_to(x, (lax.axis_size(axis), *x.shape))
    return lax.all_to_all(copies, axis, split_axis=0, concat_axis=0, tiled=True)


def taken_together(x, axis):
    everything = copy_for_each(x, axis)
    return jnp.sum(everything, axis=0)


def table(rows, cols, length, sign):
    left = jnp.arange(rows, dtype=jnp.int32)[:, None]
    right = jnp.arange(cols, dtype=jnp.int32)[None, :]
    angle = sign * 2.0 * math.pi / length * (left * right % length).astype(jnp.float32)
    return (jnp.cos(angle), jnp.sin(angle))


def cform(form, left, right):
    apply = partial(jnp.einsum, form, precision=HIGH)
    return (
        apply(left[0], right[0]) - apply(left[1], right[1]),
        apply(left[0], right[1]) + apply(left[1], right[0]),
    )


def cmul(left, right):
    return (left[0] * right[0] - left[1] * right[1], left[0] * right[1] + left[1] * right[0])


def forward_last(real_part, imag_part):
    lead = real_part.shape[:-1]
    length = real_part.shape[-1]
    inner = length // RADIX
    part = (real_part.reshape(lead + (RADIX, inner)), imag_part.reshape(lead + (RADIX, inner)))
    part = cform("kn,...ni->...ki", table(RADIX, RADIX, RADIX, -1), part)
    part = cmul(part, table(RADIX, inner, length, -1))
    part = cform("...ki,il->...kl", part, table(inner, inner, inner, -1))
    return (part[0].reshape(lead + (length,)), part[1].reshape(lead + (length,)))


def forward_middle(real_part, imag_part):
    maps, length, cols = real_part.shape
    inner = length // RADIX
    part = (
        real_part.reshape(maps, RADIX, inner, cols),
        imag_part.reshape(maps, RADIX, inner, cols),
    )
    part = cform("kn,mniy->mkiy", table(RADIX, RADIX, RADIX, -1), part)
    twist = table(RADIX, inner, length, -1)
    part = cmul(part, (twist[0][:, :, None], twist[1][:, :, None]))
    part = cform("mkiy,il->mkly", part, table(inner, inner, inner, -1))
    return (part[0].reshape(maps, length, cols), part[1].reshape(maps, length, cols))


def inverse_middle(real_part, imag_part):
    maps, length, cols = real_part.shape
    inner = length // RADIX
    part = (
        real_part.reshape(maps, RADIX, inner, cols),
        imag_part.reshape(maps, RADIX, inner, cols),
    )
    part = cform("mkjy,jn->mkny", part, table(inner, inner, inner, 1))
    twist = table(RADIX, inner, length, 1)
    part = cmul(part, (twist[0][:, :, None], twist[1][:, :, None]))
    part = cform("nk,mkiy->mniy", table(RADIX, RADIX, RADIX, 1), part)
    return (
        part[0].reshape(maps, length, cols) / length,
        part[1].reshape(maps, length, cols) / length,
    )


def inverse_last_real(real_part, imag_part):
    lead = real_part.shape[:-1]
    length = real_part.shape[-1]
    inner = length // RADIX
    part = (real_part.reshape(lead + (RADIX, inner)), imag_part.reshape(lead + (RADIX, inner)))
    part = cform("...kj,jn->...kn", part, table(inner, inner, inner, 1))
    part = cmul(part, table(RADIX, inner, length, 1))
    outer = table(RADIX, RADIX, RADIX, 1)
    real = jnp.einsum("nk,...ki->...ni", outer[0], part[0], precision=HIGH) - jnp.einsum(
        "nk,...ki->...ni", outer[1], part[1], precision=HIGH
    )
    return real.reshape(lead + (length,)) / length


def signed_frequency(flat, length):
    inner = length // RADIX
    freq = flat // inner + RADIX * (flat % inner)
    return jnp.where(freq < length // 2, freq, freq - length).astype(jnp.float32)


def apply_kernel(real_part, imag_part, smoothing):
    maps, length, cols = real_part.shape
    total = cols * lax.axis_size(("row", "col"))
    freq_x = signed_frequency(jnp.arange(length, dtype=jnp.int32), length)[:, None]
    freq_y = signed_frequency(
        lax.axis_index(("row", "col")) * cols + jnp.arange(cols, dtype=jnp.int32), total
    )[None, :]
    square = jnp.maximum(freq_x * freq_x + freq_y * freq_y, 1.0)
    width = smoothing[:, None, None]
    damp = jnp.exp(
        -2.0 * math.pi**2 * width * width * ((freq_x / length) ** 2 + (freq_y / total) ** 2)
    )
    kernel = (
        (freq_x * freq_x - freq_y * freq_y) / square * damp,
        -2.0 * freq_x * freq_y / square * damp,
    )
    return cmul((real_part, imag_part), kernel)


def spectral_pass(real_part, imag_part, smoothing):
    real_part, imag_part = (
        lax.all_to_all(real_part, "col", split_axis=1, concat_axis=2, tiled=True),
        lax.all_to_all(imag_part, "col", split_axis=1, concat_axis=2, tiled=True),
    )
    real_part, imag_part = forward_last(real_part, imag_part)
    real_part, imag_part = (
        lax.all_to_all(real_part, ("row", "col"), split_axis=2, concat_axis=1, tiled=True),
        lax.all_to_all(imag_part, ("row", "col"), split_axis=2, concat_axis=1, tiled=True),
    )
    real_part, imag_part = forward_middle(real_part, imag_part)
    real_part, imag_part = apply_kernel(real_part, imag_part, smoothing)
    real_part, imag_part = inverse_middle(real_part, imag_part)
    real_part, imag_part = (
        lax.all_to_all(real_part, ("row", "col"), split_axis=1, concat_axis=2, tiled=True),
        lax.all_to_all(imag_part, ("row", "col"), split_axis=1, concat_axis=2, tiled=True),
    )
    return inverse_last_real(real_part, imag_part)


def body(shear, smoothing, offsets, thresholds):
    kappa = spectral_pass(shear[0], shear[1], smoothing)
    maps, rows, width = kappa.shape
    padded = with_halo(kappa, ((("row", "col"), 1),), 1)
    nearest = None
    for step_row in range(3):
        band = padded[:, step_row : step_row + rows]
        for step_col in (-1, 0, 1):
            if step_row == 1 and step_col == 0:
                continue
            moved = jnp.roll(band, step_col, axis=2)
            nearest = moved if nearest is None else jnp.maximum(nearest, moved)
    height_map = kappa - nearest
    full = jnp.repeat(jnp.repeat(offsets, CELL, axis=1), CELL, axis=2)
    code = (jnp.arange(rows, dtype=jnp.int32) % CELL)[:, None] * CELL + (
        jnp.arange(width, dtype=jnp.int32) % CELL
    )[None, :]
    chosen = full == code[None]
    blocks = (
        jnp.arange(width, dtype=jnp.int32)[:, None] // CELL
        == jnp.arange(width // CELL, dtype=jnp.int32)[None, :]
    ).astype(jnp.float32)

    def pick(values):
        picked = jnp.where(chosen, values, 0.0)
        summed = picked.reshape(maps, rows // CELL, CELL, width).sum(axis=2)
        return jnp.einsum("mxy,yc->mxc", summed, blocks, precision=HIGH)

    total = taken_together(jnp.sum(kappa * kappa, axis=(1, 2)), ("row", "col"))
    rms = jnp.sqrt(total / (NX * NY) + 1e-06)
    snr = kappa / rms[:, None, None]
    heights = pick(height_map) / rms[:, None, None]
    values = pick(kappa) / rms[:, None, None]
    weight = jax.nn.sigmoid(heights / peak_soft)
    levels = bin_step * thresholds.astype(jnp.float32)
    above = jax.nn.sigmoid((values[..., None] - levels[:, None, None, :]) / bin_soft)
    local = jnp.sum(weight[..., None] * above, axis=(1, 2))
    counts = taken_together(local, ("row", "col"))
    return (snr, heights, counts)


def solution(mesh):
    return jax.shard_map(
        body,
        mesh=mesh,
        in_specs=(
            P(None, "maps", "row", "col"),
            P("maps"),
            P("maps", ("row", "col"), None),
            P("maps", None),
        ),
        out_specs=(
            P("maps", ("row", "col"), None),
            P("maps", ("row", "col"), None),
            P("maps", None),
        ),
        check_vma=False,
    )
```

profile of v0, /device:TPU:1, one launch (start us, length us, event | category | flops | bytes accessed | tf_op | source)
XLA Modules:
  0.0 206.1 jit_solution(32004106269578060)
XLA Ops:
  4.4 4.8 %all-to-all-start.1 = ((f32[1,512,512]{2,0,1:T(1,128)}), f32[1,512,512]{2,0,1:T(1,128)S(1)}, u32[]{:S(2)}, u32[]{:S(2)}) async-start(f32[1,512,512]{2,0,1:T(1,128)} %bitcast.245), calls=%async_computation.1 | async-start | bytes 2097152 | tf_op jit(solution)/shard_map/all_to_all | solution.py:154
  11.3 11.3 %all-to-all-done.1 = f32[1,512,512]{2,0,1:T(1,128)S(1)} async-done(((f32[1,512,512]{2,0,1:T(1,128)}), f32[1,512,512]{2,0,1:T(1,128)S(1)}, u32[]{:S(2)}, u32[]{:S(2)}) %all-to-all-start.1) | async-done | bytes 1048608 | tf_op jit(solution)/shard_map/all_to_all | solution.py:154
  22.6 3.7 %all-to-all-start = ((f32[1,512,512]{2,0,1:T(1,128)}), f32[1,512,512]{2,0,1:T(1,128)S(1)}, u32[]{:S(2)}, u32[]{:S(2)}) async-start(f32[1,512,512]{2,0,1:T(1,128)} %bitcast.246), calls=%async_computation | async-start | bytes 2097152 | tf_op jit(solution)/shard_map/all_to_all | solution.py:153
  28.5 9.9 %all-to-all-done = f32[1,512,512]{2,0,1:T(1,128)S(1)} async-done(((f32[1,512,512]{2,0,1:T(1,128)}), f32[1,512,512]{2,0,1:T(1,128)S(1)}, u32[]{:S(2)}, u32[]{:S(2)}) %all-to-all-start) | async-done | bytes 1048608 | tf_op jit(solution)/shard_map/all_to_all | solution.py:153
  46.6 2.6 %convolution_add_fusion.5 = f32[128,16,128]{0,2,1:T(8,128)} fusion(f32[128,16,128]{0,2,1:T(8,128)S(1)} %fusion.58, f32[128,16,128]{2,1,0:T(8,128)S(1)} %get-tuple-element.9), kind=kOutput, calls=%fused_computation.38 | convolution fusion | flops 403144704 | bytes 3145728 | tf_op jit(solution)/shard_map/...ki,il->...kl/dot_general | solution.py:62
  49.2 8.7 %all-to-all-start.3 = ((f32[1,128,2048]{1,0,2:T(1,128)}), f32[1,128,2048]{1,0,2:T(1,128)S(1)}, u32[]{:S(2)}, u32[]{:S(2)}) async-start(f32[1,128,2048]{1,0,2:T(1,128)} %bitcast.32), calls=%async_computation.3 | async-start | bytes 2097152 | tf_op jit(solution)/shard_map/all_to_all | solution.py:159
  59.6 2.6 %convolution_subtract_fusion.6 = f32[128,16,128]{0,2,1:T(8,128)} fusion(f32[128,16,128]{0,2,1:T(8,128)S(1)} %fusion.60, f32[128,16,128]{2,1,0:T(8,128)S(1)} %get-tuple-element.9), kind=kOutput, calls=%fused_computation.39 | convolution fusion | flops 403144704 | bytes 3145728 | tf_op jit(solution)/shard_map/...ki,il->...kl/dot_general | solution.py:61
  62.2 11.3 %all-to-all-done.3 = f32[1,128,2048]{1,0,2:T(1,128)S(1)} async-done(((f32[1,128,2048]{1,0,2:T(1,128)}), f32[1,128,2048]{1,0,2:T(1,128)S(1)}, u32[]{:S(2)}, u32[]{:S(2)}) %all-to-all-start.3) | async-done | bytes 1048608 | tf_op jit(solution)/shard_map/all_to_all | solution.py:159
  73.5 4.2 %all-to-all-start.2 = ((f32[1,128,2048]{1,0,2:T(1,128)}), f32[1,128,2048]{1,0,2:T(1,128)S(1)}, u32[]{:S(2)}, u32[]{:S(2)}) async-start(f32[1,128,2048]{1,0,2:T(1,128)} %bitcast.25), calls=%async_computation.2 | async-start | bytes 2097152 | tf_op jit(solution)/shard_map/all_to_all | solution.py:158
  81.5 11.8 %all-to-all-done.2 = f32[1,128,2048]{1,0,2:T(1,128)S(1)} async-done(((f32[1,128,2048]{1,0,2:T(1,128)}), f32[1,128,2048]{1,0,2:T(1,128)S(1)}, u32[]{:S(2)}, u32[]{:S(2)}) %all-to-all-start.2) | async-done | bytes 1048608 | tf_op jit(solution)/shard_map/all_to_all | solution.py:158
  105.8 2.2 %fusion.30 = f32[128,16,128]{2,0,1:T(8,128)S(1)} fusion(f32[1,16,128,128]{3,2,1,0:T(8,128)S(1)} %fusion.7, f32[1,16,128,128]{3,2,1,0:T(8,128)S(1)} %fusion.8, f32[128]{0:T(128)S(1)} %get-tuple-element.33, f32[16,128]{1,0:T(8,128)S(1)} %get-tuple-element.35, f32[]{:T(128)} %bitcast.50, f32[128]{0:T(128)S(1)} %get-tuple-element.34, ...), kind=kOutput, calls=%fused_computation.68 | convolution fusion | flops 406290432 | bytes 3171844 | tf_op jit(solution)/shard_map/mkjy,jn->mkny/dot_general | solution.py:62
  112.2 2.5 %add_bitcast_fusion = (f32[16,128,128]{2,1,0:T(8,128)S(1)}, f32[16,128,128]{2,1,0:T(8,128)S(1)}) fusion(f32[1,16,128,128]{3,2,1,0:T(8,128)S(1)} %fusion.5, f32[16,128]{1,0:T(8,128)S(1)} %get-tuple-element.37, f32[16,128]{1,0:T(8,128)S(1)} %get-tuple-element.38, f32[128,16,128]{2,0,1:T(8,128)S(1)} %fusion.32, f32[1,16,128,128]{3,2,1,0:T(8,128)S(1)} %fusion.7, ...), kind=kOutput, calls=%fused_computation.89 | convolution fusion | flops 408125440 | bytes 6333956 | tf_op jit(solution)/shard_map/mkjy,jn->mkny/dot_general | solution.py:61
  119.2 4.6 %all-to-all-start.4 = ((f32[1,2048,128]{2,0,1:T(1,128)}), f32[1,2048,128]{2,0,1:T(1,128)S(1)}, u32[]{:S(2)}, u32[]{:S(2)}) async-start(f32[1,2048,128]{2,0,1:T(1,128)} %bitcast.259), calls=%async_computation.4 | async-start | bytes 2097152 | tf_op jit(solution)/shard_map/all_to_all | solution.py:165
  125.1 5.9 %reshape.922 = s32[1,8,16,2048]{2,1,3,0:T(8,128)} reshape(s32[128,128,16]{0,2,1:T(8,128)} %broadcast_in_dim.26) | data formatting | bytes 2097152 | tf_op jit(solution)/shard_map/broadcast_in_dim | solution.py:184
  131.0 6.0 %copy.314 = s32[1,8,16,2048]{3,2,1,0:T(8,128)} copy(s32[1,8,16,2048]{2,1,3,0:T(8,128)} %reshape.922) | data formatting | bytes 2097152 | tf_op jit(solution)/shard_map/broadcast_in_dim | solution.py:184
  141.6 5.8 %all-to-all-start.5 = ((f32[1,2048,128]{2,0,1:T(1,128)}), f32[1,2048,128]{2,0,1:T(1,128)S(1)}, u32[]{:S(2)}, u32[]{:S(2)}) async-start(f32[1,2048,128]{2,0,1:T(1,128)} %bitcast.83), calls=%async_computation.5 | async-start | bytes 2097152 | tf_op jit(solution)/shard_map/all_to_all | solution.py:166
  150.9 12.1 %all-to-all-done.5 = f32[1,2048,128]{2,0,1:T(1,128)S(1)} async-done(((f32[1,2048,128]{2,0,1:T(1,128)}), f32[1,2048,128]{2,0,1:T(1,128)S(1)}, u32[]{:S(2)}, u32[]{:S(2)}) %all-to-all-start.5) | async-done | bytes 1048608 | tf_op jit(solution)/shard_map/all_to_all | solution.py:166
  163.0 2.5 %convolution_subtract_fusion.1 = f32[128,16,128]{2,0,1:T(8,128)S(1)} fusion(f32[128,16,128]{2,0,1:T(8,128)} %fusion.80, f32[128,16,128]{2,0,1:T(8,128)S(1)} %bitcast.251), kind=kOutput, calls=%fused_computation.19 | convolution fusion | flops 403144704 | bytes 3145728 | tf_op jit(solution)/shard_map/...kj,jn->...kn/dot_general | solution.py:61
  168.5 2.4 %multiply_reduce_fusion = (f32[]{:T(128)}, f32[128,128,16]{1,2,0:T(8,128)S(1)}) fusion(f32[128,128,16]{1,2,0:T(8,128)S(1)} %fusion.41, f32[128,16,128]{2,0,1:T(8,128)S(1)} %get-tuple-element.5), kind=kOutput, calls=%fused_computation.86 | convolution fusion | flops 51383808 | bytes 3145732 | tf_op jit(solution)/shard_map/nk,...ki->...ni/dot_general | solution.py:120
  173.8 4.0 %all-to-all-start.6 = ((f32[16,1,1]{2,1,0:T(1,128)}), f32[16,1,1]{2,1,0:T(1,128)S(1)}, u32[]{:S(2)}, u32[]{:S(2)}) async-start(f32[16,1,1]{2,1,0:T(1,128)} %broadcast_in_dim.23), calls=%async_computation.6 | async-start | bytes 16384 | tf_op jit(solution)/shard_map/all_to_all | solution.py:43
  177.8 2.8 %collective-permute-start.1 = (f32[1,1,2048]{2,1,0:T(1,128)S(1)}, f32[1,1,2048]{2,1,0:T(1,128)S(1)}, u32[]{:S(2)}, u32[]{:S(2)}) collective-permute-start(f32[1,1,2048]{2,1,0:T(1,128)S(1)} %get-tuple-element.26), channel_id=1, source_target_pairs={{1,0},{2,1},{3,2},{4,3},{5,4},{6,5},{7,6},{8,7},{9,8},{10,9},{11,1... | collective-permute-start | bytes 24584 | tf_op jit(solution)/shard_map/ppermute | solution.py:30
  187.1 3.2 %fusion.18 = f32[1,128,2048]{1,2,0:T(8,128)} fusion(f32[1,128,2048]{1,2,0:T(8,128)S(1)} %copy.284, f32[1,1,2048]{1,2,0:T(8,128)S(1)} %copy.283, f32[1,1,2048]{1,2,0:T(8,128)S(1)} %copy.276, f32[1,128,1]{1,2,0:T(1,128)S(1)} %get-tuple-element.19, f32[1,128,2047]{1,2,0:T(8,128)S(1)} %get-tuple-element.22, f32[1,128,1]{1,2,0:T(1,128)S(1)} %get-tuple-element.20, ...), kind=kLoop, calls=%fused_computation.51 | loop fusion | flops 5505024 | bytes 6383104 | tf_op jit(solution)/shard_map/jit(_where)/select_n | solution.py:195
  194.1 5.7 %all-to-all-start.7 = ((f32[16,1,16]{2,1,0:T(1,128)}), f32[16,1,16]{2,1,0:T(1,128)S(1)}, u32[]{:S(2)}, u32[]{:S(2)}) async-start(f32[16,1,16]{2,1,0:T(1,128)} %broadcast_in_dim.31), calls=%async_computation.7 | async-start | bytes 16384 | tf_op jit(solution)/shard_map/all_to_all | solution.py:43
  200.9 4.4 %all-to-all-done.7 = f32[16,1,16]{2,1,0:T(1,128)S(1)} async-done(((f32[16,1,16]{2,1,0:T(1,128)}), f32[16,1,16]{2,1,0:T(1,128)S(1)}, u32[]{:S(2)}, u32[]{:S(2)}) %all-to-all-start.7) | async-done | bytes 1056 | tf_op jit(solution)/shard_map/all_to_all | solution.py:43
  (87 shorter events, 68.4 us)
Async XLA Ops:
  4.4 18.2 %all-to-all-start.1 = ((f32[1,512,512]{2,0,1:T(1,128)}), f32[1,512,512]{2,0,1:T(1,128)S(1)}, u32[]{:S(2)}, u32[]{:S(2)}) async-start(f32[1,512,512]{2,0,1:T(1,128)} %bitcast.245), calls=%async_computation.1 | async-start | bytes 2097152 | tf_op jit(solution)/shard_map/all_to_all | solution.py:154
  22.6 15.8 %all-to-all-start = ((f32[1,512,512]{2,0,1:T(1,128)}), f32[1,512,512]{2,0,1:T(1,128)S(1)}, u32[]{:S(2)}, u32[]{:S(2)}) async-start(f32[1,512,512]{2,0,1:T(1,128)} %bitcast.246), calls=%async_computation | async-start | bytes 2097152 | tf_op jit(solution)/shard_map/all_to_all | solution.py:153
  49.2 24.2 %all-to-all-start.3 = ((f32[1,128,2048]{1,0,2:T(1,128)}), f32[1,128,2048]{1,0,2:T(1,128)S(1)}, u32[]{:S(2)}, u32[]{:S(2)}) async-start(f32[1,128,2048]{1,0,2:T(1,128)} %bitcast.32), calls=%async_computation.3 | async-start | bytes 2097152 | tf_op jit(solution)/shard_map/all_to_all | solution.py:159
  73.5 5.2 %copy-start.2 = (f32[1,128,2048]{1,0,2:T(1,128)}, f32[1,128,2048]{1,0,2:T(1,128)S(1)}, u32[]{:S(2)}) copy-start(f32[1,128,2048]{1,0,2:T(1,128)S(1)} %all-to-all-done.3) | copy-start | bytes 3145732
  73.5 19.8 %all-to-all-start.2 = ((f32[1,128,2048]{1,0,2:T(1,128)}), f32[1,128,2048]{1,0,2:T(1,128)S(1)}, u32[]{:S(2)}, u32[]{:S(2)}) async-start(f32[1,128,2048]{1,0,2:T(1,128)} %bitcast.25), calls=%async_computation.2 | async-start | bytes 2097152 | tf_op jit(solution)/shard_map/all_to_all | solution.py:158
  93.2 1.0 copy-start.3
  117.9 5.9 %copy-start.4 = (s32[1,8,128]{2,1,0:T(8,128)S(1)}, s32[1,8,128]{2,1,0:T(8,128)}, u32[]{:S(2)}) copy-start(s32[1,8,128]{2,1,0:T(8,128)} %param.6) | copy-start | bytes 12292
  119.2 22.4 %all-to-all-start.4 = ((f32[1,2048,128]{2,0,1:T(1,128)}), f32[1,2048,128]{2,0,1:T(1,128)S(1)}, u32[]{:S(2)}, u32[]{:S(2)}) async-start(f32[1,2048,128]{2,0,1:T(1,128)} %bitcast.259), calls=%async_computation.4 | async-start | bytes 2097152 | tf_op jit(solution)/shard_map/all_to_all | solution.py:165
  140.3 7.1 %copy-start.5 = (s32[1,16]{1,0:T(1,128)S(1)}, s32[1,16]{1,0:T(1,128)}, u32[]{:S(2)}) copy-start(s32[1,16]{1,0:T(1,128)} %param.7) | copy-start | bytes 196
  141.6 21.3 %all-to-all-start.5 = ((f32[1,2048,128]{2,0,1:T(1,128)}), f32[1,2048,128]{2,0,1:T(1,128)S(1)}, u32[]{:S(2)}, u32[]{:S(2)}) async-start(f32[1,2048,128]{2,0,1:T(1,128)} %bitcast.83), calls=%async_computation.5 | async-start | bytes 2097152 | tf_op jit(solution)/shard_map/all_to_all | solution.py:166
  171.0 1.5 copy-start
  173.8 9.5 %all-to-all-start.6 = ((f32[16,1,1]{2,1,0:T(1,128)}), f32[16,1,1]{2,1,0:T(1,128)S(1)}, u32[]{:S(2)}, u32[]{:S(2)}) async-start(f32[16,1,1]{2,1,0:T(1,128)} %broadcast_in_dim.23), calls=%async_computation.6 | async-start | bytes 16384 | tf_op jit(solution)/shard_map/all_to_all | solution.py:43
  177.8 7.4 %collective-permute-start.1 = (f32[1,1,2048]{2,1,0:T(1,128)S(1)}, f32[1,1,2048]{2,1,0:T(1,128)S(1)}, u32[]{:S(2)}, u32[]{:S(2)}) collective-permute-start(f32[1,1,2048]{2,1,0:T(1,128)S(1)} %get-tuple-element.26), channel_id=1, source_target_pairs={{1,0},{2,1},{3,2},{4,3},{5,4},{6,5},{7,6},{8,7},{9,8},{10,9},{11,1... | collective-permute-start | bytes 24584 | tf_op jit(solution)/shard_map/ppermute | solution.py:30
  180.7 5.0 %collective-permute-start = (f32[1,1,2048]{2,1,0:T(1,128)S(1)}, f32[1,1,2048]{2,1,0:T(1,128)S(1)}, u32[]{:S(2)}, u32[]{:S(2)}) collective-permute-start(f32[1,1,2048]{2,1,0:T(1,128)S(1)} %get-tuple-element.25), channel_id=1, source_target_pairs={{0,1},{1,2},{2,3},{3,4},{4,5},{5,6},{6,7},{7,8},{8,9},{9,10},{10,1... | collective-permute-start | bytes 24584 | tf_op jit(solution)/shard_map/ppermute | solution.py:29
  190.3 9.5 %copy-start.1 = (f32[1,128,2048]{2,1,0:T(8,128)S(1)}, f32[1,128,2048]{2,1,0:T(8,128)}, u32[]{:S(2)}) copy-start(f32[1,128,2048]{2,1,0:T(8,128)} %copy-done) | copy-start | bytes 3145732
  194.1 11.2 %all-to-all-start.7 = ((f32[16,1,16]{2,1,0:T(1,128)}), f32[16,1,16]{2,1,0:T(1,128)S(1)}, u32[]{:S(2)}, u32[]{:S(2)}) async-start(f32[16,1,16]{2,1,0:T(1,128)} %broadcast_in_dim.31), calls=%async_computation.7 | async-start | bytes 16384 | tf_op jit(solution)/shard_map/all_to_all | solution.py:43
where the time goes:
time: 210 us; the launch traced here: 206 us
  waiting for transfers between devices  61.3 us (29%)
  matrix products  52 us (25%)
  starting transfers between devices  44.6 us (21%)
  local copies, waits for them, and re-layouts  36.6 us (17%)
  other arithmetic  8.99 us (4%)
  between operations  2.73 us (1%)
    dot_general x7, matrix products, cform(): apply(left[1], right[1])  13.5 us
    broadcast_in_dim x5, local copies, waits for them, and re-layouts, body(): full = jnp.repeat(jnp.repeat(offsets, CELL, axis=1), CELL, axis=2)  13.2 us
    all_to_all x1, waiting for transfers between devices, spectral_pass(): lax.all_to_all(imag_part, ('row', 'col'), split_axis=1, concat_axis=2, ti...  12.1 us
    all_to_all x1, waiting for transfers between devices, spectral_pass(): lax.all_to_all(real_part, ('row', 'col'), split_axis=2, concat_axis=1, ti...  11.8 us
    dot_general x7, matrix products, cform(): apply(left[1], right[0])  11.3 us
    all_to_all x1, waiting for transfers between devices, spectral_pass(): lax.all_to_all(imag_part, ('row', 'col'), split_axis=2, concat_axis=1, ti...  11.3 us
    all_to_all x1, waiting for transfers between devices, spectral_pass(): lax.all_to_all(imag_part, 'col', split_axis=1, concat_axis=2, tiled=True)  11.3 us
    dot_general x7, matrix products, cform(): apply(left[0], right[0]) - apply(left[1], right[1])  11.1 us
  transfers between devices with their start and end apart: 10, of which 7 were waited for; matrix products, arithmetic and copies ran while one was open for 18% of the time, Pallas kernels for 0%

commit v1 on v0

v1 whole, which is shorter than its diff:
```python
from functools import partial
import math

import jax
import jax.numpy as jnp
from jax import lax
from jax.experimental import pallas as pl
from jax.experimental.pallas import tpu as pltpu
from jax.sharding import PartitionSpec as P

N = 2048
INNER = 512
DEV = 16
ROWS = 128
LANES = 128
HALF = 64
CELL = 16
BLOCK = ROWS + 8
CLASSES = ((0, 0, 4), (2, 4, 4), (1, 8, 8))
MIB = 1 << 20


def call(kernel, out, scratch, limit, flops, ins):
    return pl.pallas_call(
        kernel,
        out_shape=out,
        in_specs=ins,
        scratch_shapes=scratch,
        compiler_params=pltpu.CompilerParams(vmem_limit_bytes=limit * MIB),
        cost_estimate=pl.CostEstimate(flops=flops, bytes_accessed=4 * MIB, transcendentals=0),
    )


def split(x):
    high = x.astype(jnp.bfloat16)
    return high, (x - high.astype(jnp.float32)).astype(jnp.bfloat16)


def dot3(left, right):
    dot = partial(jnp.dot, preferred_element_type=jnp.float32)
    return dot(left[0], right[0]) + (dot(left[0], right[1]) + dot(left[1], right[0]))


def angle(steps):
    wrapped = jnp.bitwise_and(steps, N - 1)
    wrapped = jnp.where(wrapped >= N // 2, wrapped - N, wrapped)
    return wrapped.astype(jnp.float32) * (2.0 * math.pi / N)


def iota(shape, dim):
    return lax.broadcasted_iota(jnp.int32, shape, dim)


def put(high_ref, low_ref, rows, cols, value):
    high, low = split(value)
    high_ref[rows, cols] = high
    low_ref[rows, cols] = low


def sample_form(refs, scratch):
    cos_ref, sin_ref = scratch
    for (start, _, blocks), (high_ref, low_ref) in zip(CLASSES, refs):
        width = LANES * blocks
        col = iota((HALF, width), 1)
        freq = start + 4 * (HALF * (col // LANES) + col % HALF)
        quarter = jnp.where(col % LANES >= HALF, 1, 0)
        if start == 0:
            freq = jnp.where(col == HALF, N // 2, freq)
            quarter = jnp.where(col == HALF, 0, quarter)
        fine = angle(freq * iota((HALF, width), 0))
        cos_ref[:, :width] = jnp.cos(fine)
        sin_ref[:, :width] = jnp.sin(fine)
        coarse = angle(freq[:8] * (HALF * iota((8, width), 0)) + INNER * quarter[:8])
        cos_high, sin_high = jnp.cos(coarse), jnp.sin(coarse)
        for part in range(INNER // HALF):
            cos_part, sin_part = cos_high[part : part + 1], sin_high[part : part + 1]
            rows = pl.ds(HALF * part, HALF)
            cos_fine, sin_fine = cos_ref[:, :width], sin_ref[:, :width]
            put(high_ref, low_ref, rows, slice(None), cos_part * cos_fine - sin_part * sin_fine)
            if start == 1:
                rows = pl.ds(INNER + HALF * part, HALF)
                value = -(sin_part * cos_fine + cos_part * sin_fine)
                put(high_ref, low_ref, rows, slice(None), value)


def frequency_form(refs, scratch):
    cos_ref, sin_ref = scratch
    fine = angle(4 * iota((HALF, INNER), 0) * iota((HALF, INNER), 1))
    cos_ref[:, :INNER] = jnp.cos(fine)
    sin_ref[:, :INNER] = jnp.sin(fine)
    for (start, _, blocks), (high_ref, low_ref) in zip(CLASSES, refs):
        coarse = angle((start + 4 * HALF * iota((8, INNER), 0)) * iota((8, INNER), 1))
        cos_high, sin_high = jnp.cos(coarse), jnp.sin(coarse)
        for part in range(blocks):
            cos_part, sin_part = cos_high[part : part + 1], sin_high[part : part + 1]
            cos_fine, sin_fine = cos_ref[:, :INNER], sin_ref[:, :INNER]
            cosine = cos_part * cos_fine - sin_part * sin_fine
            sine = -(sin_part * cos_fine + cos_part * sin_fine)
            if start == 0 and part == 0:
                flip = (1 - 2 * (iota((HALF, INNER), 1) & 1)).astype(jnp.float32)
                sine = jnp.where(iota((HALF, INNER), 0) == 0, flip, sine)
            upper, lower = pl.ds(LANES * part, HALF), pl.ds(LANES * part + HALF, HALF)
            put(high_ref, low_ref, upper, pl.ds(0, INNER), cosine)
            put(high_ref, low_ref, lower, pl.ds(0, INNER), sine)
            if start == 1:
                put(high_ref, low_ref, upper, pl.ds(INNER, INNER), sine)
                put(high_ref, low_ref, lower, pl.ds(INNER, INNER), -cosine)


def signed(freq):
    return jnp.where(freq < N // 2, freq, freq - N)


def lane_frequency(device, shape):
    lane = iota(shape, 1)
    block = jnp.where(device < 8, device % 4, device - 8)
    start = jnp.where(device < 4, 0, jnp.where(device < 8, 2, 1))
    freq = signed(start + 4 * (HALF * block + lane % HALF))
    nyquist = (device == 0) & (lane == HALF)
    freq = jnp.where(nyquist, -(N // 2), freq)
    single = nyquist | ((device == 0) & (lane == 0))
    return freq.astype(jnp.float32), jnp.where(single, 1.0, 2.0)


def tables_kernel(smooth_ref, device_ref, *refs):
    device = device_ref[0]
    scratch = refs[-2:]
    w_refs = tuple(zip(refs[0:6:2], refs[1:6:2]))
    f_refs = tuple(zip(refs[6:12:2], refs[7:12:2]))
    even_ref, odd_ref, last_ref = refs[12:15]
    sample_form(w_refs, scratch)
    frequency_form(f_refs, scratch)
    width = smooth_ref[0]
    decay = width * width * (-2.0 * math.pi**2 / (N * N))
    shape = (HALF, LANES)
    freq_y, weight = lane_frequency(device, shape)

    def factors(freq_x, weight):
        total = freq_x * freq_x + freq_y * freq_y
        scaled = jnp.exp(decay * total) * weight / jnp.maximum(total, 1.0)
        return (freq_x * freq_x - freq_y * freq_y) * scaled, 2.0 * freq_x * freq_y * scaled

    for start, first, blocks in CLASSES:
        for part in range(blocks):
            freq = signed(start + 4 * (HALF * part + iota(shape, 0)))
            row_weight = jnp.where(freq == 0, 1.0, 2.0) * (1.0 / (N * N))
            even, odd = factors(freq.astype(jnp.float32), weight * row_weight)
            rows = pl.ds(HALF * (first + part), HALF)
            even_ref[rows, :] = even
            odd_ref[rows, :] = odd
    even, odd = factors(jnp.full(shape, -N / 2, jnp.float32), weight * (1.0 / (N * N)))
    last_ref[0:8, :] = even[0:8]
    last_ref[8:16, :] = odd[0:8]


def tables(smoothing, device):
    low = jnp.bfloat16
    pairs = []
    for _ in range(2):
        for size in (INNER, INNER, 2 * INNER):
            pairs += [jax.ShapeDtypeStruct((size, size), low)] * 2
    out = pairs + [
        jax.ShapeDtypeStruct((N // 2, LANES), jnp.float32),
        jax.ShapeDtypeStruct((N // 2, LANES), jnp.float32),
        jax.ShapeDtypeStruct((16, LANES), jnp.float32),
    ]
    scratch = [pltpu.VMEM((HALF, 2 * INNER), jnp.float32)] * 2
    smem = pl.BlockSpec(memory_space=pltpu.SMEM)
    result = call(tables_kernel, out, scratch, 20, 10**7, [smem, smem])(smoothing, device)
    return result[0:6], result[6:12], result[12:15]


def quarters(blocks):
    first, second, third, fourth = blocks
    return (
        (first + third) + (second + fourth),
        (first + third) - (second + fourth),
        first - third,
        second - fourth,
    )


def columns_kernel(x_ref, w0h, w0l, w2h, w2l, w1h, w1l, out_ref):
    for field in range(2):
        zero, two, even, odd = quarters([x_ref[c, field] for c in range(4)])
        rows = pl.ds(ROWS * field, ROWS)

        def emit(value, first):
            for part in range(value.shape[1] // LANES):
                out_ref[first + part, rows, :] = value[:, LANES * part : LANES * (part + 1)]

        emit(dot3(split(zero), (w0h[...], w0l[...])), 0)
        emit(dot3(split(two), (w2h[...], w2l[...])), 4)
        both = jnp.concatenate([even, odd], axis=1)
        emit(dot3(split(both), (w1h[...], w1l[...])), 8)


def columns(x, table):
    out = jax.ShapeDtypeStruct((DEV, 2 * ROWS, LANES), jnp.float32)
    specs = [pl.BlockSpec(memory_space=pltpu.VMEM)] * 7
    return call(columns_kernel, out, (), 24, 2 * 10**9, specs)(x, *table)


def rows_kernel(device_ref, g_ref, *refs):
    w0h, w0l, w2h, w2l, w1h, w1l, f0h, f0l, f2h, f2l, f1h, f1l = refs[:12]
    even_ref, odd_ref, last_ref, out_ref, data_ref, spec_ref = refs[12:]
    device = device_ref[0]
    lane = iota((ROWS, LANES), 1)
    sign = jnp.where(lane < HALF, 1.0, -1.0)
    fix = (lane == HALF) & (device == 0)
    for s in range(DEV):
        first = g_ref[s, 0:ROWS, :]
        second = sign * pltpu.roll(g_ref[s, ROWS : 2 * ROWS, :], HALF, 1)
        rows = pl.ds(ROWS * s, ROWS)
        data_ref[rows, 0:LANES] = first
        data_ref[rows, LANES : 2 * LANES] = jnp.where(fix, -first, second)
    zero, two, even, odd = quarters([data_ref[INNER * r : INNER * (r + 1), :] for r in range(4)])
    spec_ref[0:INNER, :] = dot3((f0h[...], f0l[...]), split(zero))
    spec_ref[INNER : 2 * INNER, :] = dot3((f2h[...], f2l[...]), split(two))
    both = jnp.concatenate([even, odd], axis=0)
    spec_ref[2 * INNER : 4 * INNER, :] = dot3((f1h[...], f1l[...]), split(both))

    _, weight = lane_frequency(device, (8, LANES))
    total = jnp.zeros((HALF, LANES), jnp.float32)
    special = jnp.zeros((8, LANES), jnp.float32)
    row = iota((HALF, LANES), 0)
    for part in range(DEV):
        upper, lower = pl.ds(LANES * part, HALF), pl.ds(LANES * part + HALF, HALF)
        x_one, x_two = spec_ref[upper, 0:LANES], spec_ref[upper, LANES : 2 * LANES]
        y_one, y_two = spec_ref[lower, 0:LANES], spec_ref[lower, LANES : 2 * LANES]
        rows = pl.ds(HALF * part, HALF)
        even, odd = even_ref[rows, :], odd_ref[rows, :]
        cosine = even * x_one - odd * y_two
        sine = even * y_one + odd * x_two
        if part == 0:
            edge, other = y_one[0:8], y_two[0:8]
            side = iota((8, LANES), 1)
            turned = jnp.where(side < HALF, 1.0, -1.0) * pltpu.roll(edge, HALF, 1)
            corner = (side == HALF) & (device == 0)
            turned = jnp.where(corner, pltpu.roll(other, HALF, 1), turned)
            edge = last_ref[0:8, :] * edge + last_ref[8:16, :] * turned
            edge = jnp.concatenate([edge] * 8, axis=0)
            cosine = jnp.where(row == 0, even * x_one, cosine)
            sine = jnp.where(row == 0, edge, sine)
            special = (cosine * cosine + sine * sine)[0:8]
        total = total + (cosine * cosine + sine * sine)
        data_ref[LANES * part : LANES * part + HALF, 0:LANES] = cosine
        data_ref[LANES * part + HALF : LANES * (part + 1), 0:LANES] = sine
    special = jnp.where(iota((8, LANES), 0) == 0, special, 0.0)
    energy = jnp.sum(total, axis=0, keepdims=True) + jnp.sum(special, axis=0, keepdims=True)
    energy = 0.5 * energy / weight[0:1]

    zero = dot3((w0h[...], w0l[...]), split(data_ref[0:INNER, 0:LANES]))
    two = dot3((w2h[...], w2l[...]), split(data_ref[INNER : 2 * INNER, 0:LANES]))
    odd = dot3((w1h[...], w1l[...]), split(data_ref[2 * INNER : 4 * INNER, 0:LANES]))
    plus, minus = zero + two, zero - two
    real, turned = odd[0:INNER], odd[INNER : 2 * INNER]
    for r, value in enumerate((plus + real, minus + turned, plus - real, minus - turned)):
        for part in range(4):
            out_ref[4 * r + part, 0:ROWS, :] = value[ROWS * part : ROWS * (part + 1)]
    for s in range(DEV):
        out_ref[s, ROWS : ROWS + 1, :] = out_ref[(s - 1) % DEV, ROWS - 1 : ROWS, :]
        out_ref[s, ROWS + 1 : ROWS + 2, :] = out_ref[(s + 1) % DEV, 0:1, :]
        out_ref[s, ROWS + 2 : ROWS + 3, :] = energy
        out_ref[s, ROWS + 3 : BLOCK, :] = jnp.zeros((BLOCK - ROWS - 3, LANES), jnp.float32)


def row_pass(device, g, sample, frequency, factors):
    out = jax.ShapeDtypeStruct((DEV, BLOCK, LANES), jnp.float32)
    scratch = [pltpu.VMEM((N, 2 * LANES), jnp.float32)] * 2
    specs = [pl.BlockSpec(memory_space=pltpu.SMEM)] + [pl.BlockSpec(memory_space=pltpu.VMEM)] * 16
    run = call(rows_kernel, out, scratch, 36, 4 * 10**9, specs)
    return run(device, g, *sample, *frequency, *factors)


def peaks_kernel(bins_ref, x_ref, f0h, f0l, f2h, f2l, f1h, f1l, offsets_ref, *refs):
    kappa_ref, heights_ref, counts_ref, inverse_ref, field_ref, wide_ref, pick_ref = refs

    def block(first, count):
        body = jnp.concatenate([x_ref[s] for s in range(first, first + count)], axis=1)
        pad = jnp.zeros((8, body.shape[1]), jnp.float32)
        return split(jnp.concatenate([body, pad], axis=0))

    zero = dot3(block(0, 4), (f0h[...], f0l[...]))
    two = dot3(block(4, 4), (f2h[...], f2l[...]))
    odd = dot3(block(8, 8), (f1h[...], f1l[...]))
    plus, minus = zero + two, zero - two
    real, turned = odd[:, 0:INNER], odd[:, INNER : 2 * INNER]
    energy = x_ref[0, ROWS : BLOCK, :]
    for s in range(1, DEV):
        energy = energy + x_ref[s, ROWS : BLOCK, :]
    mean = jnp.sum(energy[2:3, :], axis=1, keepdims=True)
    inverse = 1.0 / jnp.sqrt(mean + 1e-06)
    for c, value in enumerate((plus + real, minus + turned, plus - real, minus - turned)):
        cols = pl.ds(INNER * c, INNER)
        kappa_ref[:, cols] = value[0:ROWS]
        field_ref[8 : ROWS + 8, cols] = value[0:ROWS]
        field_ref[7:8, cols] = value[ROWS : ROWS + 1]
        field_ref[ROWS + 8 : ROWS + 9, cols] = value[ROWS + 1 : ROWS + 2]
    for start in (0,) + tuple(range(8, ROWS + 8, 16)) + (ROWS + 8,):
        size = 8 if start in (0, ROWS + 8) else 16
        value = field_ref[start : start + size, :]
        side = jnp.maximum(pltpu.roll(value, 1, 1), pltpu.roll(value, N - 1, 1))
        wide_ref[start : start + size, :] = jnp.maximum(side, value)
    blocks = iota((LANES, N), 1) // CELL == iota((LANES, N), 0)
    blocks = jnp.where(blocks, 1.0, 0.0).astype(jnp.bfloat16)
    offsets = offsets_ref[...].astype(jnp.float32).astype(jnp.bfloat16)
    offsets = jnp.concatenate([offsets, offsets], axis=0)
    spread = jnp.dot(offsets, blocks, preferred_element_type=jnp.float32)
    code = (iota((CELL, N), 0) * CELL + (iota((CELL, N), 1) & (CELL - 1))).astype(jnp.float32)
    for p in range(ROWS // CELL):
        base = 8 + CELL * p
        value = field_ref[base : base + CELL, :]
        side = jnp.maximum(pltpu.roll(value, 1, 1), pltpu.roll(value, N - 1, 1))
        above = wide_ref[base - 1 : base - 1 + CELL, :]
        below = wide_ref[base + 1 : base + 1 + CELL, :]
        nearest = jnp.maximum(side, jnp.maximum(above, below))
        chosen = spread[p : p + 1, :] == code
        height = jnp.sum(jnp.where(chosen, value - nearest, 0.0), axis=0, keepdims=True)
        level = jnp.sum(jnp.where(chosen, value, 0.0), axis=0, keepdims=True)
        pick_ref[p : p + 1, :] = height
        pick_ref[8 + p : 9 + p, :] = level
    high, low = split(pick_ref[...])
    gather = partial(
        lax.dot_general,
        dimension_numbers=(((1,), (1,)), ((), ())),
        preferred_element_type=jnp.float32,
    )
    picked = (gather(high, blocks) + gather(low, blocks)) * inverse
    heights, values = picked[0:8], picked[8:16]
    heights_ref[...] = heights
    inverse_ref[...] = jnp.broadcast_to(inverse, (8, LANES))
    weight = jax.nn.sigmoid(heights * 20.0)
    lane = iota((1, LANES), 1)
    counts = jnp.zeros((1, LANES), jnp.float32)
    for k in range(16):
        level = 0.25 * bins_ref[0, k].astype(jnp.float32)
        above = weight * jax.nn.sigmoid((values - level) * 10.0)
        summed = jnp.sum(jnp.sum(above, axis=0, keepdims=True), axis=1, keepdims=True)
        counts = counts + jnp.where(lane == k, summed, 0.0)
    for s in range(DEV):
        counts_ref[s] = jnp.broadcast_to(counts, (8, LANES))


def peak_pass(thresholds, x, table, offsets):
    f32 = jnp.float32
    out = [
        jax.ShapeDtypeStruct((ROWS, N), f32),
        jax.ShapeDtypeStruct((8, LANES), f32),
        jax.ShapeDtypeStruct((DEV, 8, LANES), f32),
        jax.ShapeDtypeStruct((8, LANES), f32),
    ]
    scratch = [
        pltpu.VMEM((ROWS + 16, N), f32),
        pltpu.VMEM((ROWS + 16, N), f32),
        pltpu.VMEM((16, N), f32),
    ]
    specs = [pl.BlockSpec(memory_space=pltpu.SMEM)] + [pl.BlockSpec(memory_space=pltpu.VMEM)] * 8
    run = call(peaks_kernel, out, scratch, 28, 2 * 10**9, specs)
    return run(thresholds, x, *table, offsets)


def body(shear, smoothing, offsets, thresholds):
    group = ("row", "col")
    device = lax.axis_index(group).astype(jnp.int32).reshape(1)
    sample, frequency, factors = tables(smoothing, device)
    x = shear.reshape(2, 4, ROWS, INNER).transpose(1, 0, 2, 3)
    x = lax.all_to_all(x, "col", split_axis=0, concat_axis=0, tiled=True)
    g = columns(x, sample)
    g = lax.all_to_all(g, group, split_axis=0, concat_axis=0, tiled=True)
    k = row_pass(device, g, sample, frequency, factors)
    k = lax.all_to_all(k, group, split_axis=0, concat_axis=0, tiled=True)
    kappa, heights, counts, inverse = peak_pass(thresholds, k, frequency, offsets[0])
    counts = lax.all_to_all(counts, group, split_axis=0, concat_axis=0, tiled=True)
    snr = kappa * inverse[0:1, 0:1]
    return snr[None], heights[None], jnp.sum(counts[:, 0:1, 0:16], axis=0)


def solution(mesh):
    return jax.shard_map(
        body,
        mesh=mesh,
        in_specs=(
            P(None, "maps", "row", "col"),
            P("maps"),
            P("maps", ("row", "col"), None),
            P("maps", None),
        ),
        out_specs=(
            P("maps", ("row", "col"), None),
            P("maps", ("row", "col"), None),
            P("maps", None),
        ),
        check_vma=False,
    )
```

time: 210 us -> 124 us (0.59); the launches traced: 206 us -> 123 us
  blocking collectives: 0 us -> 54.8 us
  matrix products: 52 us -> 0 us
  waiting for transfers between devices: 61.3 us -> 10 us
  starting transfers between devices: 44.6 us -> 8.52 us
  Pallas kernels: 0 us -> 22.2 us
  local copies, waits for them, and re-layouts: 36.6 us -> 22.5 us
  other arithmetic: 8.99 us -> 3.48 us
    all_to_all x0 -> x2, blocking collectives: none -> 54.8 us  [the longest x1 34.2 us: body(): g = lax.all_to_all(g, group, split_axis=0, concat_axis=0, tiled=True)]
    dot_general x32 -> x0, matrix products: 52 us -> none  [the longest x7 13.5 us: cform(): apply(left[1], right[1])]
    all_to_all x8 -> x2, waiting for transfers between devices: 61.3 us -> 10 us  [the longest x1 7.08 us: body(): x = lax.all_to_all(x, 'col', split_axis=0, concat_axis=0, tiled=True)]
    all_to_all x8 -> x2, starting transfers between devices: 41.5 us -> 8.52 us  [the longest x1 4.83 us: body(): x = lax.all_to_all(x, 'col', split_axis=0, concat_axis=0, tiled=True)]
    pallas_call x0 -> x4, Pallas kernels: none -> 22.2 us  [the longest x1 7.12 us: row_pass(): return run(device, g, *sample, *frequency, *factors)]
    broadcast_in_dim x7 -> x0, local copies, waits for them, and re-layouts: 15 us -> none  [the longest x5 13.2 us: body(): full = jnp.repeat(jnp.repeat(offsets, CELL, axis=1), CELL, axis=2)]
    unnamed x14 -> x62, local copies, waits for them, and re-layouts: 5.11 us -> 18.8 us
    all_to_all x4 -> x0, local copies, waits for them, and re-layouts: 5.78 us -> none  [the longest x1 1.73 us: spectral_pass(): lax.all_to_all(imag_part, ('row', 'col'), split_axis=2, concat_axis=1, ti...]
  transfers between devices with their start and end apart: 10 -> 2, of which waited for: 7 -> 2; matrix products, arithmetic and copies ran while one was open for 18% -> 2% of each run, Pallas kernels for 0% -> 5%
where the time goes in v1:
time: 124 us; the launch traced here: 123 us
  blocking collectives  54.8 us (44%)
  local copies, waits for them, and re-layouts  22.5 us (18%)
  Pallas kernels  22.2 us (18%)
  waiting for transfers between devices  10 us (8%)
  starting transfers between devices  8.52 us (7%)
  other arithmetic  3.48 us (3%)
  between operations  1.47 us (1%)
    all_to_all x1, blocking collectives, body(): g = lax.all_to_all(g, group, split_axis=0, concat_axis=0, tiled=True)  34.2 us
    all_to_all x1, blocking collectives, body(): k = lax.all_to_all(k, group, split_axis=0, concat_axis=0, tiled=True)  20.6 us
    unnamed x62, local copies, waits for them, and re-layouts  18.8 us
    pallas_call x1, Pallas kernels, row_pass(): return run(device, g, *sample, *frequency, *factors)  7.12 us
    all_to_all x1, waiting for transfers between devices, body(): x = lax.all_to_all(x, 'col', split_axis=0, concat_axis=0, tiled=True)  7.08 us
    pallas_call x1, Pallas kernels, tables(): call(tables_kernel, out, scratch, 20, 10 ** 7, [smem, smem])  5.89 us
    pallas_call x1, Pallas kernels, peak_pass(): return run(thresholds, x, *table, offsets)  4.84 us
    all_to_all x1, starting transfers between devices, body(): x = lax.all_to_all(x, 'col', split_axis=0, concat_axis=0, tiled=True)  4.83 us
  transfers between devices with their start and end apart: 2, of which 2 were waited for; matrix products, arithmetic and copies ran while one was open for 2% of the time, Pallas kernels for 5%

profile of v1, /device:TPU:1, one launch (start us, length us, event | category | flops | bytes accessed | tf_op | source)
XLA Modules:
  0.0 123.0 jit_solution(16131353882346717924)
XLA Ops:
  0.6 3.2 %copy.9 = f32[2,4,128,512]{3,2,0,1:T(8,128)} copy(f32[2,4,128,512]{3,2,1,0:T(8,128)} %bitcast.12) | data formatting | bytes 4194304 | tf_op jit(solution)/shard_map/reshape | solution.py:367
  3.8 4.8 %all-to-all-start = ((f32[4,2,128,512]{3,2,1,0:T(8,128)}), f32[4,2,128,512]{3,2,1,0:T(8,128)}, u32[]{:S(2)}, u32[]{:S(2)}) async-start(f32[4,2,128,512]{3,2,1,0:T(8,128)} %bitcast.10), calls=%async_computation | async-start | bytes 4194304 | tf_op jit(solution)/shard_map/all_to_all | solution.py:368
  9.3 5.9 %shard_map.67 = (bf16[512,512]{1,0:T(8,128)(2,1)S(1)}, bf16[512,512]{1,0:T(8,128)(2,1)S(1)}, bf16[512,512]{1,0:T(8,128)(2,1)S(1)}, bf16[512,512]{1,0:T(8,128)(2,...) custom-call(f32[1]{0:T(128)S(6)} %copy.10.smooth_ref, ...), custom_call_target="tpu_custom_call" | custom-call | flops 10000000 | bytes 4194304 | tf_op jit(solution)/shard_map/pallas_call | solution.py:169
  15.2 1.3 %copy-done = bf16[1024,1024]{1,0:T(8,128)(2,1)} copy-done((bf16[1024,1024]{1,0:T(8,128)(2,1)}, bf16[1024,1024]{1,0:T(8,128)(2,1)S(1)}, u32[]{:S(2)}) %copy-start) | copy-done | bytes 2097176
  16.5 1.3 %copy-done.2 = bf16[1024,1024]{1,0:T(8,128)(2,1)} copy-done((bf16[1024,1024]{1,0:T(8,128)(2,1)}, bf16[1024,1024]{1,0:T(8,128)(2,1)S(1)}, u32[]{:S(2)}) %copy-start.2) | copy-done | bytes 2097176
  17.9 1.4 %copy-done.5 = bf16[1024,1024]{1,0:T(8,128)(2,1)} copy-done((bf16[1024,1024]{1,0:T(8,128)(2,1)}, bf16[1024,1024]{1,0:T(8,128)(2,1)S(1)}, u32[]{:S(2)}) %copy-start.5) | copy-done | bytes 2097176
  19.2 0.8 copy-done.8
  20.0 0.8 copy-done.10
  25.6 7.1 %all-to-all-done.x_ref = f32[4,2,128,512]{3,2,1,0:T(8,128)} async-done(((f32[4,2,128,512]{3,2,1,0:T(8,128)}), f32[4,2,128,512]{3,2,1,0:T(8,128)}, u32[]{:S(2)}, u32[]{:S(2)}) %all-to-all-start) | async-done | bytes 2097184 | tf_op jit(solution)/shard_map/all_to_all | solution.py:368
  32.7 1.6 %copy-done.3 = bf16[1024,1024]{1,0:T(8,128)(2,1)S(1)} copy-done((bf16[1024,1024]{1,0:T(8,128)(2,1)S(1)}, bf16[1024,1024]{1,0:T(8,128)(2,1)}, u32[]{:S(2)}) %copy-start.3) | copy-done | bytes 2097176
  34.3 1.6 %copy-done.6 = bf16[1024,1024]{1,0:T(8,128)(2,1)S(1)} copy-done((bf16[1024,1024]{1,0:T(8,128)(2,1)S(1)}, bf16[1024,1024]{1,0:T(8,128)(2,1)}, u32[]{:S(2)}) %copy-start.6) | copy-done | bytes 2097176
  35.9 1.0 copy-done.13
  36.9 1.0 copy-done.16
  38.0 1.0 copy-done.19
  39.0 1.0 copy-done.22
  40.1 4.4 %shard_map.68 = f32[16,256,128]{2,1,0:T(8,128)S(1)} custom-call(f32[4,2,128,512]{3,2,1,0:T(8,128)} %all-to-all-done.x_ref, bf16[512,512]{1,0:T(8,128)(2,1)S(1)} %copy-done.13, bf16[512,512]{1,0:T(8,128)(2,1)S(1)} %copy-done.16, bf16[512,512]{1,0:T(8,128)(2,1)S(1)} %copy-done.19, bf16[512,512]{1,0:T(8,128)(2,1)S(1)} %copy-done.22, ...), custom_call_target="tpu_custom_call" | custom-call | flops 2000000000 | bytes 4194304 | tf_op jit(solution)/shard_map/pallas_call | solution.py:201
  44.5 34.2 %all_to_all.20.g_ref = f32[16,256,128]{2,1,0:T(8,128)S(1)} all-to-all(f32[16,256,128]{2,1,0:T(8,128)S(1)} %shard_map.68), channel_id=1, replica_groups=mesh['maps'=16,'row'=4,'col'=4] {'row','col'}, dimensions={0} | all-to-all | bytes 4194304 | tf_op jit(solution)/shard_map/all_to_all | solution.py:370
  78.8 7.1 %shard_map.69 = f32[16,136,128]{2,1,0:T(8,128)S(1)} custom-call(s32[1]{0:T(128)} %bitcast.device_ref, f32[16,256,128]{2,1,0:T(8,128)S(1)} %all_to_all.20.g_ref, bf16[512,512]{1,0:T(8,128)(2,1)S(1)} %copy-done.14, bf16[512,512]{1,0:T(8,128)(2,1)S(1)} %copy-done.17, bf16[512,512]{1,0:T(8,128)(2,1)S(1)} %copy-done.20, bf16[512,512]{1,0:T(8,128)(2,1)S(1)} %copy-done.23, ...), custom_call_target="tpu_custom_call" | custom-call | flops 4000000000 | bytes 4194304 | tf_op jit(solution)/shard_map/pallas_call | solution.py:273
  86.0 20.6 %all_to_all.21.x_ref = f32[16,136,128]{2,1,0:T(8,128)S(1)} all-to-all(f32[16,136,128]{2,1,0:T(8,128)S(1)} %shard_map.69), channel_id=1, replica_groups=mesh['maps'=16,'row'=4,'col'=4] {'row','col'}, dimensions={0} | all-to-all | bytes 2228224 | tf_op jit(solution)/shard_map/all_to_all | solution.py:372
  106.6 4.8 %shard_map.70 = (f32[128,2048]{1,0:T(8,128)S(1)}, f32[8,128]{1,0:T(8,128)}, f32[16,8,128]{2,1,0:T(8,128)}, f32[8,128]{1,0:T(8,128)S(1)}) custom-call(s32[1,16]{1,0:T(1,128)S(1)} %copy-done.30, f32[16,136,128]{2,1,0:T(8,128)S(1)} %all_to_all.21.x_ref, bf16[512,512]{1,0:T(8,128)(2,1)S(1)} %get-tuple-element.28.refs_6_.f0h, ...), custom_call_target="tpu_custom_call" | custom-call | flops 2000000000 | bytes 4194304 | tf_op jit(solution)/shard_map/pallas_call | solution.py:360
  111.4 1.0 copy-done.24
  112.9 3.7 %all-to-all-start.3 = ((f32[16,8,128]{2,1,0:T(8,128)}), f32[16,8,128]{2,1,0:T(8,128)S(1)}, u32[]{:S(2)}, u32[]{:S(2)}) async-start(f32[16,8,128]{2,1,0:T(8,128)} %get-tuple-element.40), calls=%async_computation.3 | async-start | bytes 131072 | tf_op jit(solution)/shard_map/all_to_all | solution.py:374
  116.6 2.9 %multiply_bitcast_fusion = f32[1,128,2048]{2,1,0:T(8,128)} fusion(f32[128,2048]{1,0:T(8,128)} %copy-done.24, f32[]{:T(128)} %bitcast.4), kind=kLoop, calls=%fused_computation.1 | loop fusion | flops 262144 | bytes 2097156 | tf_op jit(solution)/shard_map/broadcast_in_dim | solution.py:376
  119.6 2.9 %all-to-all-done.3 = f32[16,8,128]{2,1,0:T(8,128)S(1)} async-done(((f32[16,8,128]{2,1,0:T(8,128)}), f32[16,8,128]{2,1,0:T(8,128)S(1)}, u32[]{:S(2)}, u32[]{:S(2)}) %all-to-all-start.3) | async-done | bytes 65568 | tf_op jit(solution)/shard_map/all_to_all | solution.py:374
  (52 shorter events, 5.9 us)
Async XLA Ops:
  3.8 28.9 %all-to-all-start = ((f32[4,2,128,512]{3,2,1,0:T(8,128)}), f32[4,2,128,512]{3,2,1,0:T(8,128)}, u32[]{:S(2)}, u32[]{:S(2)}) async-start(f32[4,2,128,512]{3,2,1,0:T(8,128)} %bitcast.10), calls=%async_computation | async-start | bytes 4194304 | tf_op jit(solution)/shard_map/all_to_all | solution.py:368
  15.2 1.3 %copy-start = (bf16[1024,1024]{1,0:T(8,128)(2,1)}, bf16[1024,1024]{1,0:T(8,128)(2,1)S(1)}, u32[]{:S(2)}) copy-start(bf16[1024,1024]{1,0:T(8,128)(2,1)S(1)} %get-tuple-element.33.refs_11_.f1l) | copy-start | bytes 6291460
  16.5 1.4 %copy-start.2 = (bf16[1024,1024]{1,0:T(8,128)(2,1)}, bf16[1024,1024]{1,0:T(8,128)(2,1)S(1)}, u32[]{:S(2)}) copy-start(bf16[1024,1024]{1,0:T(8,128)(2,1)S(1)} %get-tuple-element.26.w1h.refs_4_) | copy-start | bytes 6291460
  17.8 1.4 %copy-start.5 = (bf16[1024,1024]{1,0:T(8,128)(2,1)}, bf16[1024,1024]{1,0:T(8,128)(2,1)S(1)}, u32[]{:S(2)}) copy-start(bf16[1024,1024]{1,0:T(8,128)(2,1)S(1)} %get-tuple-element.27.w1l.refs_5_) | copy-start | bytes 6291460
  32.7 1.6 %copy-start.3 = (bf16[1024,1024]{1,0:T(8,128)(2,1)S(1)}, bf16[1024,1024]{1,0:T(8,128)(2,1)}, u32[]{:S(2)}) copy-start(bf16[1024,1024]{1,0:T(8,128)(2,1)} %copy-done.2) | copy-start | bytes 6291460
  34.3 1.6 %copy-start.6 = (bf16[1024,1024]{1,0:T(8,128)(2,1)S(1)}, bf16[1024,1024]{1,0:T(8,128)(2,1)}, u32[]{:S(2)}) copy-start(bf16[1024,1024]{1,0:T(8,128)(2,1)} %copy-done.5) | copy-start | bytes 6291460
  35.9 1.0 copy-start.13
  36.9 1.0 copy-start.16
  38.0 1.0 copy-start.19
  39.0 1.0 copy-start.22
  40.1 38.7 %copy-start.7 = (bf16[1024,1024]{1,0:T(8,128)(2,1)S(1)}, bf16[1024,1024]{1,0:T(8,128)(2,1)}, u32[]{:S(2)}) copy-start(bf16[1024,1024]{1,0:T(8,128)(2,1)} %copy-done.5) | copy-start | bytes 6291460
  40.1 38.7 %copy-start.9 = (bf16[512,512]{1,0:T(8,128)(2,1)S(1)}, bf16[512,512]{1,0:T(8,128)(2,1)}, u32[]{:S(2)}) copy-start(bf16[512,512]{1,0:T(8,128)(2,1)} %copy-done.8) | copy-start | bytes 1572868
  40.1 38.7 %copy-start.11 = (bf16[512,512]{1,0:T(8,128)(2,1)S(1)}, bf16[512,512]{1,0:T(8,128)(2,1)}, u32[]{:S(2)}) copy-start(bf16[512,512]{1,0:T(8,128)(2,1)} %copy-done.10) | copy-start | bytes 1572868
  40.1 38.7 %copy-start.14 = (bf16[512,512]{1,0:T(8,128)(2,1)S(1)}, bf16[512,512]{1,0:T(8,128)(2,1)}, u32[]{:S(2)}) copy-start(bf16[512,512]{1,0:T(8,128)(2,1)} %copy-done.12) | copy-start | bytes 1572868
  40.1 38.7 %copy-start.17 = (bf16[512,512]{1,0:T(8,128)(2,1)S(1)}, bf16[512,512]{1,0:T(8,128)(2,1)}, u32[]{:S(2)}) copy-start(bf16[512,512]{1,0:T(8,128)(2,1)} %copy-done.15) | copy-start | bytes 1572868
  40.1 38.7 %copy-start.20 = (bf16[512,512]{1,0:T(8,128)(2,1)S(1)}, bf16[512,512]{1,0:T(8,128)(2,1)}, u32[]{:S(2)}) copy-start(bf16[512,512]{1,0:T(8,128)(2,1)} %copy-done.18) | copy-start | bytes 1572868
  40.1 38.7 %copy-start.23 = (bf16[512,512]{1,0:T(8,128)(2,1)S(1)}, bf16[512,512]{1,0:T(8,128)(2,1)}, u32[]{:S(2)}) copy-start(bf16[512,512]{1,0:T(8,128)(2,1)} %copy-done.21) | copy-start | bytes 1572868
  40.1 38.7 %copy-start.26 = (f32[1024,128]{1,0:T(8,128)S(1)}, f32[1024,128]{1,0:T(8,128)}, u32[]{:S(2)}) copy-start(f32[1024,128]{1,0:T(8,128)} %copy-done.25) | copy-start | bytes 1572868
  40.1 38.7 %copy-start.28 = (f32[1024,128]{1,0:T(8,128)S(1)}, f32[1024,128]{1,0:T(8,128)}, u32[]{:S(2)}) copy-start(f32[1024,128]{1,0:T(8,128)} %copy-done.27) | copy-start | bytes 1572868
  44.5 34.3 %copy-start.1 = (bf16[1024,1024]{1,0:T(8,128)(2,1)S(1)}, bf16[1024,1024]{1,0:T(8,128)(2,1)}, u32[]{:S(2)}) copy-start(bf16[1024,1024]{1,0:T(8,128)(2,1)} %copy-done) | copy-start | bytes 6291460
  44.5 34.3 %copy-start.4 = (bf16[1024,1024]{1,0:T(8,128)(2,1)S(1)}, bf16[1024,1024]{1,0:T(8,128)(2,1)}, u32[]{:S(2)}) copy-start(bf16[1024,1024]{1,0:T(8,128)(2,1)} %copy-done.2) | copy-start | bytes 6291460
  86.0 20.6 %copy-start.29 = (s32[1,8,128]{2,1,0:T(8,128)S(1)}, s32[1,8,128]{2,1,0:T(8,128)}, u32[]{:S(2)}) copy-start(s32[1,8,128]{2,1,0:T(8,128)} %param.6) | copy-start | bytes 12292
  86.0 20.6 %copy-start.30 = (s32[1,16]{1,0:T(1,128)S(1)}, s32[1,16]{1,0:T(1,128)}, u32[]{:S(2)}) copy-start(s32[1,16]{1,0:T(1,128)} %bins_ref.1) | copy-start | bytes 196
  112.9 9.5 %all-to-all-start.3 = ((f32[16,8,128]{2,1,0:T(8,128)}), f32[16,8,128]{2,1,0:T(8,128)S(1)}, u32[]{:S(2)}, u32[]{:S(2)}) async-start(f32[16,8,128]{2,1,0:T(8,128)} %get-tuple-element.40), calls=%async_computation.3 | async-start | bytes 131072 | tf_op jit(solution)/shard_map/all_to_all | solution.py:374
  (9 other events, 7.4 us)

commit v2 on v1

--- a/solution.py
+++ b/solution.py
@@ -7,6 +7,7 @@
 from jax.experimental import pallas as pl
 from jax.experimental.pallas import tpu as pltpu
 from jax.sharding import PartitionSpec as P
+
 
 N = 2048
 INNER = 512
@@ -18,6 +19,7 @@
 BLOCK = ROWS + 8
 CLASSES = ((0, 0, 4), (2, 4, 4), (1, 8, 8))
 MIB = 1 << 20
+LIMIT = (20, 24, 24, 36, 28)
 
 
 def call(kernel, out, scratch, limit, flops, ins):
@@ -36,9 +38,22 @@
     return high, (x - high.astype(jnp.float32)).astype(jnp.bfloat16)
 
 
-def dot3(left, right):
-    dot = partial(jnp.dot, preferred_element_type=jnp.float32)
-    return dot(left[0], right[0]) + (dot(left[0], right[1]) + dot(left[1], right[0]))
+def dot(left, right):
+    return jnp.dot(left, right, preferred_element_type=jnp.float32)
+
+
+def from_left(high_ref, low_ref, x):
+    high, low = split(x)
+    width = x.shape[1]
+    both = dot(high_ref[...], jnp.concatenate([high, low], axis=1))
+    return both[:, :width] + (both[:, width:] + dot(low_ref[...], high))
+
+
+def from_right(x, high_ref, low_ref):
+    high, low = split(x)
+    height = x.shape[0]
+    both = dot(jnp.concatenate([high, low], axis=0), high_ref[...])
+    return both[:height] + (both[height:] + dot(high, low_ref[...]))
 
 
 def angle(steps):
@@ -166,7 +181,7 @@
     ]
     scratch = [pltpu.VMEM((HALF, 2 * INNER), jnp.float32)] * 2
     smem = pl.BlockSpec(memory_space=pltpu.SMEM)
-    result = call(tables_kernel, out, scratch, 20, 10**7, [smem, smem])(smoothing, device)
+    result = call(tables_kernel, out, scratch, LIMIT[0], 10**9, [smem, smem])(smoothing, device)
     return result[0:6], result[6:12], result[12:15]
 
 
@@ -180,79 +195,101 @@
     )
 
 
-def columns_kernel(x_ref, w0h, w0l, w2h, w2l, w1h, w1l, out_ref):
-    for field in range(2):
-        zero, two, even, odd = quarters([x_ref[c, field] for c in range(4)])
-        rows = pl.ds(ROWS * field, ROWS)
-
-        def emit(value, first):
-            for part in range(value.shape[1] // LANES):
-                out_ref[first + part, rows, :] = value[:, LANES * part : LANES * (part + 1)]
-
-        emit(dot3(split(zero), (w0h[...], w0l[...])), 0)
-        emit(dot3(split(two), (w2h[...], w2l[...])), 4)
-        both = jnp.concatenate([even, odd], axis=1)
-        emit(dot3(split(both), (w1h[...], w1l[...])), 8)
-
-
-def columns(x, table):
+def pack_kernel(place_ref, x_ref, *outs):
+    for index in range(8):
+        start = pl.multiple_of(((place_ref[0] + index) & 3) * ROWS, ROWS)
+        outs[index][...] = x_ref[index // 4, 0, pl.ds(start, ROWS), :]
+
+
+def pack(place, shear):
+    out = [jax.ShapeDtypeStruct((ROWS, INNER), jnp.float32)] * 8
+    specs = [pl.BlockSpec(memory_space=pltpu.SMEM), pl.BlockSpec(memory_space=pltpu.VMEM)]
+    return call(pack_kernel, out, (), LIMIT[1], 10**6, specs)(place, shear)
+
+
+def columns_kernel(field, place_ref, *refs):
+    blocks, table, out_ref = refs[:4], refs[4:10], refs[-1]
+    zero, two, even, odd = quarters([x[...] for x in blocks])
+    place = place_ref[0]
+    along = jnp.where(place == 0, 1.0, jnp.where(place == 2, -1.0, 0.0))
+    across = jnp.where(place == 1, 1.0, jnp.where(place == 3, -1.0, 0.0))
+    flip = jnp.where((place & 1) == 0, 1.0, -1.0)
+    rows = pl.ds(ROWS * field, ROWS)
+    other = pl.ds(ROWS - ROWS * field, ROWS)
+    for part in range(DEV):
+        out_ref[part, other, :] = refs[10][part, other, :] if field else jnp.zeros((ROWS, LANES), jnp.float32)
+
+    def emit(value, first):
+        for part in range(value.shape[1] // LANES):
+            out_ref[first + part, rows, :] = value[:, LANES * part : LANES * (part + 1)]
+
+    emit(from_right(zero, *table[0:2]), 0)
+    emit(from_right(flip * two, *table[2:4]), 4)
+    both = jnp.concatenate([along * even - across * odd, across * even + along * odd], axis=1)
+    emit(from_right(both, *table[4:6]), 8)
+
+
+def columns(field, place, blocks, table, *before):
     out = jax.ShapeDtypeStruct((DEV, 2 * ROWS, LANES), jnp.float32)
-    specs = [pl.BlockSpec(memory_space=pltpu.VMEM)] * 7
-    return call(columns_kernel, out, (), 24, 2 * 10**9, specs)(x, *table)
+    specs = [pl.BlockSpec(memory_space=pltpu.SMEM)] + [pl.BlockSpec(memory_space=pltpu.VMEM)] * 10
+    specs += [pl.BlockSpec(memory_space=pltpu.VMEM)] * len(before)
+    kernel = partial(columns_kernel, field)
+    run = call(kernel, out, (), LIMIT[1], 2 * 10**9, specs)
+    return run(place, *blocks, *table, *before)
 
 
 def rows_kernel(device_ref, g_ref, *refs):
     w0h, w0l, w2h, w2l, w1h, w1l, f0h, f0l, f2h, f2l, f1h, f1l = refs[:12]
-    even_ref, odd_ref, last_ref, out_ref, data_ref, spec_ref = refs[12:]
+    even_ref, odd_ref, last_ref, out_ref, spec_ref, data_ref = refs[12:]
     device = device_ref[0]
-    lane = iota((ROWS, LANES), 1)
-    sign = jnp.where(lane < HALF, 1.0, -1.0)
-    fix = (lane == HALF) & (device == 0)
-    for s in range(DEV):
-        first = g_ref[s, 0:ROWS, :]
-        second = sign * pltpu.roll(g_ref[s, ROWS : 2 * ROWS, :], HALF, 1)
-        rows = pl.ds(ROWS * s, ROWS)
-        data_ref[rows, 0:LANES] = first
-        data_ref[rows, LANES : 2 * LANES] = jnp.where(fix, -first, second)
-    zero, two, even, odd = quarters([data_ref[INNER * r : INNER * (r + 1), :] for r in range(4)])
-    spec_ref[0:INNER, :] = dot3((f0h[...], f0l[...]), split(zero))
-    spec_ref[INNER : 2 * INNER, :] = dot3((f2h[...], f2l[...]), split(two))
+
+    def rows_of(r):
+        wide = []
+        for s in range(4 * r, 4 * r + 4):
+            block = g_ref[s]
+            wide.append(jnp.concatenate([block[:ROWS], block[ROWS:]], axis=1))
+        return jnp.concatenate(wide, axis=0)
+
+    zero, two, even, odd = quarters([rows_of(r) for r in range(4)])
+    spec_ref[0:INNER, :] = from_left(f0h, f0l, zero)
+    spec_ref[INNER : 2 * INNER, :] = from_left(f2h, f2l, two)
     both = jnp.concatenate([even, odd], axis=0)
-    spec_ref[2 * INNER : 4 * INNER, :] = dot3((f1h[...], f1l[...]), split(both))
-
+    spec_ref[2 * INNER : 4 * INNER, :] = from_left(f1h, f1l, both)
     _, weight = lane_frequency(device, (8, LANES))
     total = jnp.zeros((HALF, LANES), jnp.float32)
     special = jnp.zeros((8, LANES), jnp.float32)
-    row = iota((HALF, LANES), 0)
+    row, lane = iota((HALF, LANES), 0), iota((HALF, LANES), 1)
+    sign = jnp.where(lane < HALF, 1.0, -1.0)
+    fix = (lane == HALF) & (device == 0)
     for part in range(DEV):
         upper, lower = pl.ds(LANES * part, HALF), pl.ds(LANES * part + HALF, HALF)
         x_one, x_two = spec_ref[upper, 0:LANES], spec_ref[upper, LANES : 2 * LANES]
         y_one, y_two = spec_ref[lower, 0:LANES], spec_ref[lower, LANES : 2 * LANES]
+        x_two = jnp.where(fix, -x_one, sign * pltpu.roll(x_two, HALF, 1))
+        y_two = jnp.where(fix, -y_one, sign * pltpu.roll(y_two, HALF, 1))
         rows = pl.ds(HALF * part, HALF)
         even, odd = even_ref[rows, :], odd_ref[rows, :]
         cosine = even * x_one - odd * y_two
         sine = even * y_one + odd * x_two
         if part == 0:
             edge, other = y_one[0:8], y_two[0:8]
-            side = iota((8, LANES), 1)
-            turned = jnp.where(side < HALF, 1.0, -1.0) * pltpu.roll(edge, HALF, 1)
-            corner = (side == HALF) & (device == 0)
-            turned = jnp.where(corner, pltpu.roll(other, HALF, 1), turned)
+            turned = sign[0:8] * pltpu.roll(edge, HALF, 1)
+            turned = jnp.where(fix[0:8], pltpu.roll(other, HALF, 1), turned)
             edge = last_ref[0:8, :] * edge + last_ref[8:16, :] * turned
             edge = jnp.concatenate([edge] * 8, axis=0)
             cosine = jnp.where(row == 0, even * x_one, cosine)
             sine = jnp.where(row == 0, edge, sine)
             special = (cosine * cosine + sine * sine)[0:8]
         total = total + (cosine * cosine + sine * sine)
-        data_ref[LANES * part : LANES * part + HALF, 0:LANES] = cosine
-        data_ref[LANES * part + HALF : LANES * (part + 1), 0:LANES] = sine
+        data_ref[upper, :] = cosine
+        data_ref[lower, :] = sine
     special = jnp.where(iota((8, LANES), 0) == 0, special, 0.0)
     energy = jnp.sum(total, axis=0, keepdims=True) + jnp.sum(special, axis=0, keepdims=True)
     energy = 0.5 * energy / weight[0:1]
 
-    zero = dot3((w0h[...], w0l[...]), split(data_ref[0:INNER, 0:LANES]))
-    two = dot3((w2h[...], w2l[...]), split(data_ref[INNER : 2 * INNER, 0:LANES]))
-    odd = dot3((w1h[...], w1l[...]), split(data_ref[2 * INNER : 4 * INNER, 0:LANES]))
+    zero = from_left(w0h, w0l, data_ref[0:INNER, :])
+    two = from_left(w2h, w2l, data_ref[INNER : 2 * INNER, :])
+    odd = from_left(w1h, w1l, data_ref[2 * INNER : 4 * INNER, :])
     plus, minus = zero + two, zero - two
     real, turned = odd[0:INNER], odd[INNER : 2 * INNER]
     for r, value in enumerate((plus + real, minus + turned, plus - real, minus - turned)):
@@ -267,23 +304,23 @@
 
 def row_pass(device, g, sample, frequency, factors):
     out = jax.ShapeDtypeStruct((DEV, BLOCK, LANES), jnp.float32)
-    scratch = [pltpu.VMEM((N, 2 * LANES), jnp.float32)] * 2
+    scratch = [pltpu.VMEM((N, 2 * LANES), jnp.float32), pltpu.VMEM((N, LANES), jnp.float32)]
     specs = [pl.BlockSpec(memory_space=pltpu.SMEM)] + [pl.BlockSpec(memory_space=pltpu.VMEM)] * 16
-    run = call(rows_kernel, out, scratch, 36, 4 * 10**9, specs)
+    run = call(rows_kernel, out, scratch, LIMIT[3], 4 * 10**9, specs)
     return run(device, g, *sample, *frequency, *factors)
 
 
 def peaks_kernel(bins_ref, x_ref, f0h, f0l, f2h, f2l, f1h, f1l, offsets_ref, *refs):
-    kappa_ref, heights_ref, counts_ref, inverse_ref, field_ref, wide_ref, pick_ref = refs
+    snr_ref, heights_ref, counts_ref, field_ref, wide_ref, pick_ref = refs
 
     def block(first, count):
         body = jnp.concatenate([x_ref[s] for s in range(first, first + count)], axis=1)
         pad = jnp.zeros((8, body.shape[1]), jnp.float32)
-        return split(jnp.concatenate([body, pad], axis=0))
-
-    zero = dot3(block(0, 4), (f0h[...], f0l[...]))
-    two = dot3(block(4, 4), (f2h[...], f2l[...]))
-    odd = dot3(block(8, 8), (f1h[...], f1l[...]))
+        return jnp.concatenate([body, pad], axis=0)
+
+    zero = from_right(block(0, 4), f0h, f0l)
+    two = from_right(block(4, 4), f2h, f2l)
+    odd = from_right(block(8, 8), f1h, f1l)
     plus, minus = zero + two, zero - two
     real, turned = odd[:, 0:INNER], odd[:, INNER : 2 * INNER]
     energy = x_ref[0, ROWS : BLOCK, :]
@@ -293,7 +330,7 @@
     inverse = 1.0 / jnp.sqrt(mean + 1e-06)
     for c, value in enumerate((plus + real, minus + turned, plus - real, minus - turned)):
         cols = pl.ds(INNER * c, INNER)
-        kappa_ref[:, cols] = value[0:ROWS]
+        snr_ref[:, cols] = value[0:ROWS] * inverse
         field_ref[8 : ROWS + 8, cols] = value[0:ROWS]
         field_ref[7:8, cols] = value[ROWS : ROWS + 1]
         field_ref[ROWS + 8 : ROWS + 9, cols] = value[ROWS + 1 : ROWS + 2]
@@ -329,7 +366,6 @@
     picked = (gather(high, blocks) + gather(low, blocks)) * inverse
     heights, values = picked[0:8], picked[8:16]
     heights_ref[...] = heights
-    inverse_ref[...] = jnp.broadcast_to(inverse, (8, LANES))
     weight = jax.nn.sigmoid(heights * 20.0)
     lane = iota((1, LANES), 1)
     counts = jnp.zeros((1, LANES), jnp.float32)
@@ -348,7 +384,6 @@
         jax.ShapeDtypeStruct((ROWS, N), f32),
         jax.ShapeDtypeStruct((8, LANES), f32),
         jax.ShapeDtypeStruct((DEV, 8, LANES), f32),
-        jax.ShapeDtypeStruct((8, LANES), f32),
     ]
     scratch = [
         pltpu.VMEM((ROWS + 16, N), f32),
@@ -356,23 +391,33 @@
         pltpu.VMEM((16, N), f32),
     ]
     specs = [pl.BlockSpec(memory_space=pltpu.SMEM)] + [pl.BlockSpec(memory_space=pltpu.VMEM)] * 8
-    run = call(peaks_kernel, out, scratch, 28, 2 * 10**9, specs)
+    run = call(peaks_kernel, out, scratch, LIMIT[4], 2 * 10**9, specs)
     return run(thresholds, x, *table, offsets)
 
 
 def body(shear, smoothing, offsets, thresholds):
     group = ("row", "col")
     device = lax.axis_index(group).astype(jnp.int32).reshape(1)
+    place = lax.axis_index("col").astype(jnp.int32).reshape(1)
+
+    def exchange(x):
+        return lax.all_to_all(x, group, split_axis=0, concat_axis=0, tiled=True)
+
+    blocks = pack(place, shear)
+    fields = []
+    for field in range(2):
+        got = [blocks[4 * field], None, None, None]
+        for step in (2, 1, 3):
+            pairs = [(c, (c + step) % 4) for c in range(4)]
+            got[4 - step] = lax.ppermute(blocks[4 * field + step], "col", pairs)
+        fields.append(got)
     sample, frequency, factors = tables(smoothing, device)
-    x = shear.reshape(2, 4, ROWS, INNER).transpose(1, 0, 2, 3)
-    x = lax.all_to_all(x, "col", split_axis=0, concat_axis=0, tiled=True)
-    g = columns(x, sample)
-    g = lax.all_to_all(g, group, split_axis=0, concat_axis=0, tiled=True)
-    k = row_pass(device, g, sample, frequency, factors)
-    k = lax.all_to_all(k, group, split_axis=0, concat_axis=0, tiled=True)
-    kappa, heights, counts, inverse = peak_pass(thresholds, k, frequency, offsets[0])
-    counts = lax.all_to_all(counts, group, split_axis=0, concat_axis=0, tiled=True)
-    snr = kappa * inverse[0:1, 0:1]
+    g = columns(0, place, fields[0], sample)
+    g = columns(1, place, fields[1], sample, g)
+    k = row_pass(device, exchange(g), sample, frequency, factors)
+    out = peak_pass(thresholds, exchange(k), frequency, offsets[0])
+    snr, heights, counts = out
+    counts = exchange(counts)
     return snr[None], heights[None], jnp.sum(counts[:, 0:1, 0:16], axis=0)
 
 

time: 124 us -> 106 us (0.85)
  local copies, waits for them, and re-layouts: 22.5 us -> 1.6 us
  blocking collectives: 54.8 us -> 59.8 us
  waiting for transfers between devices: 10 us -> 14 us
  other arithmetic: 3.48 us -> 0.54 us
  Pallas kernels: 22.2 us -> 20.4 us
    unnamed x62 -> x6, local copies, waits for them, and re-layouts: 18.8 us -> 1.6 us
    ppermute x0 -> x6, waiting for transfers between devices: none -> 14 us  [body(): got[4 - step] = lax.ppermute(blocks[4 * field + step], 'col', pairs)]
    all_to_all x2 -> x0, waiting for transfers between devices: 10 us -> none  [the longest x1 7.08 us: body(): x = lax.all_to_all(x, 'col', split_axis=0, concat_axis=0, tiled=True)]
    all_to_all x2 -> x0, starting transfers between devices: 8.52 us -> none  [the longest x1 4.83 us: body(): x = lax.all_to_all(x, 'col', split_axis=0, concat_axis=0, tiled=True)]
    ppermute x0 -> x6, starting transfers between devices: none -> 7.81 us  [body(): got[4 - step] = lax.ppermute(blocks[4 * field + step], 'col', pairs)]
    all_to_all x2 -> x3, blocking collectives: 54.8 us -> 59.8 us  [exchange(): return lax.all_to_all(x, group, split_axis=0, concat_axis=0, tiled=True)]
    reshape x1 -> x0, local copies, waits for them, and re-layouts: 3.16 us -> none  [body(): x = shear.reshape(2, 4, ROWS, INNER).transpose(1, 0, 2, 3)]
    broadcast_in_dim x1 -> x0, other arithmetic: 2.94 us -> none  [body(): return (snr[None], heights[None], jnp.sum(counts[:, 0:1, 0:16], axis=0))]
  transfers between devices with their start and end apart: 2 -> 6, of which waited for: 2 -> 4; matrix products, arithmetic and copies ran while one was open for 2% -> 0% of each run, Pallas kernels for 5% -> 7%
where the time goes in v2:
time: 106 us; the launch traced here: 105 us
  blocking collectives  59.8 us (56%)
  Pallas kernels  20.4 us (19%)
  waiting for transfers between devices  14 us (13%)
  starting transfers between devices  7.81 us (7%)
  local copies, waits for them, and re-layouts  1.6 us (2%)
  between operations  1.35 us (1%)
    all_to_all x3, blocking collectives, exchange(): return lax.all_to_all(x, group, split_axis=0, concat_axis=0, tiled=True)  59.8 us
    ppermute x6, waiting for transfers between devices, body(): got[4 - step] = lax.ppermute(blocks[4 * field + step], 'col', pairs)  14 us
    ppermute x6, starting transfers between devices, body(): got[4 - step] = lax.ppermute(blocks[4 * field + step], 'col', pairs)  7.81 us
    pallas_call x1, Pallas kernels, row_pass(): return run(device, g, *sample, *frequency, *factors)  6.6 us
    pallas_call x1, Pallas kernels, tables(): call(tables_kernel, out, scratch, LIMIT[0], 10 ** 9, [smem, smem])  5.89 us
    pallas_call x1, Pallas kernels, peak_pass(): return run(thresholds, x, *table, offsets)  4.6 us
    pallas_call x2, Pallas kernels, columns(): return run(place, *blocks, *table, *before)  3.14 us
  transfers between devices with their start and end apart: 6, of which 4 were waited for; matrix products, arithmetic and copies ran while one was open for 0% of the time, Pallas kernels for 7%

profile of v2, /device:TPU:1, one launch (start us, length us, event | category | flops | bytes accessed | tf_op | source)
XLA Modules:
  0.0 105.4 jit_solution(17352127407735529461)
XLA Ops:
  0.6 1.6 %copy-done = f32[2,1,512,512]{3,2,1,0:T(8,128)S(1)} copy-done((f32[2,1,512,512]{3,2,1,0:T(8,128)S(1)}, f32[2,1,512,512]{3,2,1,0:T(8,128)}, u32[]{:S(2)}) %copy-start) | copy-done | bytes 2097176
  2.2 0.1 shard_map.67
  2.4 3.4 %collective-permute-start.3 = (f32[128,512]{1,0:T(8,128)S(1)}, f32[128,512]{1,0:T(8,128)S(1)}, u32[]{:S(2)}, u32[]{:S(2)}) collective-permute-start(f32[128,512]{1,0:T(8,128)S(1)} %get-tuple-element.40), channel_id=1, source_target_pairs={{0,3},{1,0},{2,1},{3,2},{4,7},{5,4},{6,5},{7,6},{8,11},{9,8},{10,9... | collective-permute-start | bytes 786440 | tf_op jit(solution)/shard_map/ppermute | solution.py:412
  5.7 0.5 collective-permute-start.4
  6.3 0.6 collective-permute-start.5
  6.9 2.1 %collective-permute-start = (f32[128,512]{1,0:T(8,128)S(1)}, f32[128,512]{1,0:T(8,128)S(1)}, u32[]{:S(2)}, u32[]{:S(2)}) collective-permute-start(f32[128,512]{1,0:T(8,128)S(1)} %get-tuple-element.30), channel_id=1, source_target_pairs={{0,3},{1,0},{2,1},{3,2},{4,7},{5,4},{6,5},{7,6},{8,11},{9,8},{10,9... | collective-permute-start | bytes 786440 | tf_op jit(solution)/shard_map/ppermute | solution.py:412
  8.9 1.2 %collective-permute-start.1 = (f32[128,512]{1,0:T(8,128)S(1)}, f32[128,512]{1,0:T(8,128)S(1)}, u32[]{:S(2)}, u32[]{:S(2)}) collective-permute-start(f32[128,512]{1,0:T(8,128)S(1)} %get-tuple-element.31), channel_id=1, source_target_pairs={{0,2},{1,3},{2,0},{3,1},{4,6},{5,7},{6,4},{7,5},{8,10},{9,11},{10,... | collective-permute-start | bytes 786440 | tf_op jit(solution)/shard_map/ppermute | solution.py:412
  10.8 2.6 %collective-permute-done.3.refs_1_ = f32[128,512]{1,0:T(8,128)S(1)} collective-permute-done((f32[128,512]{1,0:T(8,128)S(1)}, f32[128,512]{1,0:T(8,128)S(1)}, u32[]{:S(2)}, u32[]{:S(2)}) %collective-permute-start.3) | collective-permute-done | bytes 262176 | tf_op jit(solution)/shard_map/ppermute | solution.py:412
  13.4 0.0 collective-permute-start.2
  13.4 5.9 %shard_map.68 = (bf16[512,512]{1,0:T(8,128)(2,1)S(1)}, bf16[512,512]{1,0:T(8,128)(2,1)S(1)}, bf16[512,512]{1,0:T(8,128)(2,1)S(1)}, bf16[512,512]{1,0:T(8,128)(2,...) custom-call(f32[1]{0:T(128)S(6)} %copy.7.smooth_ref, ...), custom_call_target="tpu_custom_call" | custom-call | flops 1000000000 | bytes 4194304 | tf_op jit(solution)/shard_map/pallas_call | solution.py:184
  19.3 0.0 collective-permute-done.4.refs_2_
  19.3 3.1 %collective-permute-done.5.refs_3_ = f32[128,512]{1,0:T(8,128)S(1)} collective-permute-done((f32[128,512]{1,0:T(8,128)S(1)}, f32[128,512]{1,0:T(8,128)S(1)}, u32[]{:S(2)}, u32[]{:S(2)}) %collective-permute-start.5) | collective-permute-done | bytes 262176 | tf_op jit(solution)/shard_map/ppermute | solution.py:412
  22.4 1.6 %shard_map.69.refs_10_ = f32[16,256,128]{2,1,0:T(8,128)S(1)} custom-call(s32[1]{0:T(128)} %bitcast.1.place_ref, f32[128,512]{1,0:T(8,128)S(1)} %get-tuple-element.39.refs_0_, f32[128,512]{1,0:T(8,128)S(1)} %collective-permute-done.3.refs_1_, f32[128,512]{1,0:T(8,128)S(1)} %collective-permute-done.4.refs_2_, f32[128,512]{1,0:T(8,128)S(1)} %collective-permute-done.5.refs_3_, ...), custom_call_target="tpu_custom_call" | custom-call | flops 2000000000 | bytes 4194304 | tf_op jit(solution)/shard_map/pallas_call | solution.py:238
  23.9 3.5 %collective-permute-done.refs_1_ = f32[128,512]{1,0:T(8,128)S(1)} collective-permute-done((f32[128,512]{1,0:T(8,128)S(1)}, f32[128,512]{1,0:T(8,128)S(1)}, u32[]{:S(2)}, u32[]{:S(2)}) %collective-permute-start) | collective-permute-done | bytes 262176 | tf_op jit(solution)/shard_map/ppermute | solution.py:412
  27.4 4.8 %collective-permute-done.2.refs_3_ = f32[128,512]{1,0:T(8,128)S(1)} collective-permute-done((f32[128,512]{1,0:T(8,128)S(1)}, f32[128,512]{1,0:T(8,128)S(1)}, u32[]{:S(2)}, u32[]{:S(2)}) %collective-permute-start.2) | collective-permute-done | bytes 262176 | tf_op jit(solution)/shard_map/ppermute | solution.py:412
  32.3 1.6 %shard_map.70 = f32[16,256,128]{2,1,0:T(8,128)S(1)} custom-call(s32[1]{0:T(128)} %bitcast.1.place_ref, f32[128,512]{1,0:T(8,128)S(1)} %get-tuple-element.29.refs_0_, f32[128,512]{1,0:T(8,128)S(1)} %collective-permute-done.refs_1_, f32[128,512]{1,0:T(8,128)S(1)} %collective-permute-done.1.refs_2_, f32[128,512]{1,0:T(8,128)S(1)} %collective-permute-done.2.refs_3_, ...), custom_call_target="tpu_custom_call" | custom-call | flops 2000000000 | bytes 4194304 | tf_op jit(solution)/shard_map/pallas_call | solution.py:238
  33.9 30.4 %all_to_all.15.g_ref = f32[16,256,128]{2,1,0:T(8,128)S(1)} all-to-all(f32[16,256,128]{2,1,0:T(8,128)S(1)} %shard_map.70), channel_id=1, replica_groups=mesh['maps'=16,'row'=4,'col'=4] {'row','col'}, dimensions={0} | all-to-all | bytes 4194304 | tf_op jit(solution)/shard_map/all_to_all | solution.py:404
  64.3 6.6 %shard_map.71 = f32[16,136,128]{2,1,0:T(8,128)S(1)} custom-call(s32[1]{0:T(128)} %bitcast.device_ref, f32[16,256,128]{2,1,0:T(8,128)S(1)} %all_to_all.15.g_ref, bf16[512,512]{1,0:T(8,128)(2,1)S(1)} %get-tuple-element.33.refs_4_.refs_0_, bf16[512,512]{1,0:T(8,128)(2,1)S(1)} %get-tuple-element.34.refs_5_.refs_1_, ...), custom_call_target="tpu_custom_call" | custom-call | flops 4000000000 | bytes 4194304 | tf_op jit(solution)/shard_map/pallas_call | solution.py:310
  70.9 0.0 copy-start.1
  70.9 0.0 copy-start.2
  70.9 20.6 %all_to_all.16.x_ref = f32[16,136,128]{2,1,0:T(8,128)S(1)} all-to-all(f32[16,136,128]{2,1,0:T(8,128)S(1)} %shard_map.71), channel_id=1, replica_groups=mesh['maps'=16,'row'=4,'col'=4] {'row','col'}, dimensions={0} | all-to-all | bytes 2228224 | tf_op jit(solution)/shard_map/all_to_all | solution.py:404
  91.5 4.6 %shard_map.72 = (f32[128,2048]{1,0:T(8,128)}, f32[8,128]{1,0:T(8,128)}, f32[16,8,128]{2,1,0:T(8,128)S(1)}) custom-call(s32[1,16]{1,0:T(1,128)S(1)} %copy-done.2, f32[16,136,128]{2,1,0:T(8,128)S(1)} %all_to_all.16.x_ref, bf16[512,512]{1,0:T(8,128)(2,1)S(1)} %get-tuple-element.43.refs_6_.f0h, bf16[512,512]{1,0:T(8,128)(2,1)S(1)} %get-tuple-element.44.refs_7_.f0l, ...), custom_call_target="tpu_custom_call" | custom-call | flops 2000000000 | bytes 4194304 | tf_op jit(solution)/shard_map/pallas_call | solution.py:395
  96.1 8.8 %all_to_all.17 = f32[16,8,128]{2,1,0:T(8,128)S(1)} all-to-all(f32[16,8,128]{2,1,0:T(8,128)S(1)} %get-tuple-element.54), channel_id=1, replica_groups=mesh['maps'=16,'row'=4,'col'=4] {'row','col'}, dimensions={0} | all-to-all | bytes 131072 | tf_op jit(solution)/shard_map/all_to_all | solution.py:404
  104.9 0.5 slice_reduce_fusion
  (4 shorter events, 0.0 us)
Async XLA Ops:
  0.6 1.6 %copy-start = (f32[2,1,512,512]{3,2,1,0:T(8,128)S(1)}, f32[2,1,512,512]{3,2,1,0:T(8,128)}, u32[]{:S(2)}) copy-start(f32[2,1,512,512]{3,2,1,0:T(8,128)} %x_ref.1) | copy-start | bytes 6291460
  2.4 11.0 %collective-permute-start.3 = (f32[128,512]{1,0:T(8,128)S(1)}, f32[128,512]{1,0:T(8,128)S(1)}, u32[]{:S(2)}, u32[]{:S(2)}) collective-permute-start(f32[128,512]{1,0:T(8,128)S(1)} %get-tuple-element.40), channel_id=1, source_target_pairs={{0,3},{1,0},{2,1},{3,2},{4,7},{5,4},{6,5},{7,6},{8,11},{9,8},{10,9... | collective-permute-start | bytes 786440 | tf_op jit(solution)/shard_map/ppermute | solution.py:412
  5.7 13.6 %collective-permute-start.4 = (f32[128,512]{1,0:T(8,128)S(1)}, f32[128,512]{1,0:T(8,128)S(1)}, u32[]{:S(2)}, u32[]{:S(2)}) collective-permute-start(f32[128,512]{1,0:T(8,128)S(1)} %get-tuple-element.41), channel_id=1, source_target_pairs={{0,2},{1,3},{2,0},{3,1},{4,6},{5,7},{6,4},{7,5},{8,10},{9,11},{10,... | collective-permute-start | bytes 786440 | tf_op jit(solution)/shard_map/ppermute | solution.py:412
  6.3 16.1 %collective-permute-start.5 = (f32[128,512]{1,0:T(8,128)S(1)}, f32[128,512]{1,0:T(8,128)S(1)}, u32[]{:S(2)}, u32[]{:S(2)}) collective-permute-start(f32[128,512]{1,0:T(8,128)S(1)} %get-tuple-element.42), channel_id=1, source_target_pairs={{0,1},{1,2},{2,3},{3,0},{4,5},{5,6},{6,7},{7,4},{8,9},{9,10},{10,1... | collective-permute-start | bytes 786440 | tf_op jit(solution)/shard_map/ppermute | solution.py:412
  6.9 20.6 %collective-permute-start = (f32[128,512]{1,0:T(8,128)S(1)}, f32[128,512]{1,0:T(8,128)S(1)}, u32[]{:S(2)}, u32[]{:S(2)}) collective-permute-start(f32[128,512]{1,0:T(8,128)S(1)} %get-tuple-element.30), channel_id=1, source_target_pairs={{0,3},{1,0},{2,1},{3,2},{4,7},{5,4},{6,5},{7,6},{8,11},{9,8},{10,9... | collective-permute-start | bytes 786440 | tf_op jit(solution)/shard_map/ppermute | solution.py:412
  8.9 18.5 %collective-permute-start.1 = (f32[128,512]{1,0:T(8,128)S(1)}, f32[128,512]{1,0:T(8,128)S(1)}, u32[]{:S(2)}, u32[]{:S(2)}) collective-permute-start(f32[128,512]{1,0:T(8,128)S(1)} %get-tuple-element.31), channel_id=1, source_target_pairs={{0,2},{1,3},{2,0},{3,1},{4,6},{5,7},{6,4},{7,5},{8,10},{9,11},{10,... | collective-permute-start | bytes 786440 | tf_op jit(solution)/shard_map/ppermute | solution.py:412
  13.4 18.9 %collective-permute-start.2 = (f32[128,512]{1,0:T(8,128)S(1)}, f32[128,512]{1,0:T(8,128)S(1)}, u32[]{:S(2)}, u32[]{:S(2)}) collective-permute-start(f32[128,512]{1,0:T(8,128)S(1)} %get-tuple-element.32), channel_id=1, source_target_pairs={{0,1},{1,2},{2,3},{3,0},{4,5},{5,6},{6,7},{7,4},{8,9},{9,10},{10,1... | collective-permute-start | bytes 786440 | tf_op jit(solution)/shard_map/ppermute | solution.py:412
  70.9 20.6 %copy-start.1 = (s32[1,8,128]{2,1,0:T(8,128)S(1)}, s32[1,8,128]{2,1,0:T(8,128)}, u32[]{:S(2)}) copy-start(s32[1,8,128]{2,1,0:T(8,128)} %param.6) | copy-start | bytes 12292
  70.9 20.6 %copy-start.2 = (s32[1,16]{1,0:T(1,128)S(1)}, s32[1,16]{1,0:T(1,128)}, u32[]{:S(2)}) copy-start(s32[1,16]{1,0:T(1,128)} %bins_ref.1) | copy-start | bytes 196

commit v3 on v2

--- a/solution.py
+++ b/solution.py
@@ -20,6 +20,7 @@
 CLASSES = ((0, 0, 4), (2, 4, 4), (1, 8, 8))
 MIB = 1 << 20
 LIMIT = (20, 24, 24, 36, 28)
+ORDER = (6, 2, 5, 7, 1, 3, 4)
 
 
 def call(kernel, out, scratch, limit, flops, ins):
@@ -195,66 +196,101 @@
     )
 
 
-def pack_kernel(place_ref, x_ref, *outs):
+def pack_kernel(device_ref, x_ref, *outs):
     for index in range(8):
-        start = pl.multiple_of(((place_ref[0] + index) & 3) * ROWS, ROWS)
+        start = pl.multiple_of(((device_ref[0] + index) & 3) * ROWS, ROWS)
         outs[index][...] = x_ref[index // 4, 0, pl.ds(start, ROWS), :]
 
 
-def pack(place, shear):
+def pack(device, shear):
     out = [jax.ShapeDtypeStruct((ROWS, INNER), jnp.float32)] * 8
     specs = [pl.BlockSpec(memory_space=pltpu.SMEM), pl.BlockSpec(memory_space=pltpu.VMEM)]
-    return call(pack_kernel, out, (), LIMIT[1], 10**6, specs)(place, shear)
-
-
-def columns_kernel(field, place_ref, *refs):
-    blocks, table, out_ref = refs[:4], refs[4:10], refs[-1]
+    return call(pack_kernel, out, (), LIMIT[1], 10**6, specs)(device, shear)
+
+
+def columns_kernel(device_ref, *refs):
+    blocks, table = refs[:4], refs[4:10]
+    keep_ref, send_ref, all_ref = refs[10:]
     zero, two, even, odd = quarters([x[...] for x in blocks])
-    place = place_ref[0]
+    device = device_ref[0]
+    place = device & 3
     along = jnp.where(place == 0, 1.0, jnp.where(place == 2, -1.0, 0.0))
     across = jnp.where(place == 1, 1.0, jnp.where(place == 3, -1.0, 0.0))
     flip = jnp.where((place & 1) == 0, 1.0, -1.0)
-    rows = pl.ds(ROWS * field, ROWS)
-    other = pl.ds(ROWS - ROWS * field, ROWS)
-    for part in range(DEV):
-        out_ref[part, other, :] = refs[10][part, other, :] if field else jnp.zeros((ROWS, LANES), jnp.float32)
 
     def emit(value, first):
         for part in range(value.shape[1] // LANES):
-            out_ref[first + part, rows, :] = value[:, LANES * part : LANES * (part + 1)]
+            all_ref[first + part] = value[:, LANES * part : LANES * (part + 1)]
 
     emit(from_right(zero, *table[0:2]), 0)
     emit(from_right(flip * two, *table[2:4]), 4)
     both = jnp.concatenate([along * even - across * odd, across * even + along * odd], axis=1)
     emit(from_right(both, *table[4:6]), 8)
-
-
-def columns(field, place, blocks, table, *before):
-    out = jax.ShapeDtypeStruct((DEV, 2 * ROWS, LANES), jnp.float32)
+    for index in range(8):
+        there = other_chip(device, index)
+        keep_ref[index] = all_ref[there]
+        send_ref[index] = all_ref[there ^ 4]
+
+
+def other_chip(device, index):
+    return ((device & 12) ^ (2 * (index & 4))) + ((device + index) & 3)
+
+
+def columns(device, blocks, table):
+    out = [jax.ShapeDtypeStruct((8, ROWS, LANES), jnp.float32)] * 2
     specs = [pl.BlockSpec(memory_space=pltpu.SMEM)] + [pl.BlockSpec(memory_space=pltpu.VMEM)] * 10
-    specs += [pl.BlockSpec(memory_space=pltpu.VMEM)] * len(before)
-    kernel = partial(columns_kernel, field)
-    run = call(kernel, out, (), LIMIT[1], 2 * 10**9, specs)
-    return run(place, *blocks, *table, *before)
-
-
-def rows_kernel(device_ref, g_ref, *refs):
-    w0h, w0l, w2h, w2l, w1h, w1l, f0h, f0l, f2h, f2l, f1h, f1l = refs[:12]
-    even_ref, odd_ref, last_ref, out_ref, spec_ref, data_ref = refs[12:]
+    scratch = [pltpu.VMEM((DEV, ROWS, LANES), jnp.float32)]
+    return call(columns_kernel, out, scratch, LIMIT[1], 2 * 10**9, specs)(device, *blocks, *table)
+
+
+def merge_kernel(keep_ref, got_ref, *outs):
+    for index in range(8):
+        outs[index][0] = keep_ref[index]
+        outs[index][1] = got_ref[index]
+
+
+def merge(keep, got):
+    out = [jax.ShapeDtypeStruct((2,) + keep.shape[1:], jnp.float32)] * 8
+    specs = [pl.BlockSpec(memory_space=pltpu.VMEM)] * 2
+    return call(merge_kernel, out, (), 8, 10**8, specs)(keep, got)
+
+
+def to_frequency(device, g_refs, f_refs, part_ref, out_ref):
+    f0h, f0l, f2h, f2l, f1h, f1l = f_refs
+    flip_core = jnp.where((device & 4) == 0, 1.0, -1.0)
+    flip_chip = jnp.where((device & 8) == 0, 1.0, -1.0)
+    for step in range(4):
+        near, far = g_refs[step], g_refs[4 + step]
+        same, other = near[0] + far[0], near[1] + far[1]
+        rows = pl.ds(pl.multiple_of(((device - step) & 3) * ROWS, ROWS), ROWS)
+        part_ref[0, rows, :] = same + other
+        part_ref[1, rows, :] = flip_core * (same - other)
+        same, other = flip_chip * (near[0] - far[0]), flip_chip * (near[1] - far[1])
+        part_ref[2, rows, :] = jnp.where(flip_core > 0, same, other)
+        part_ref[3, rows, :] = jnp.where(flip_core > 0, other, same)
+    out_ref[0:INNER, :] = from_left(f0h, f0l, part_ref[0])
+    out_ref[INNER : 2 * INNER, :] = from_left(f2h, f2l, part_ref[1])
+    both = jnp.concatenate([part_ref[2], part_ref[3]], axis=0)
+    out_ref[2 * INNER : 4 * INNER, :] = from_left(f1h, f1l, both)
+
+
+def first_kernel(device_ref, *refs):
+    to_frequency(device_ref[0], refs[:8], refs[8:14], refs[15], refs[14])
+
+
+def first_pass(device, g, frequency):
+    out = jax.ShapeDtypeStruct((N, LANES), jnp.float32)
+    specs = [pl.BlockSpec(memory_space=pltpu.SMEM)] + [pl.BlockSpec(memory_space=pltpu.VMEM)] * 14
+    scratch = [pltpu.VMEM((4, INNER, LANES), jnp.float32)]
+    return call(first_kernel, out, scratch, LIMIT[2], 10**9, specs)(device, *g, *frequency)
+
+
+def rows_kernel(device_ref, one_ref, *refs):
+    g_refs, refs = refs[:8], refs[8:]
+    w0h, w0l, w2h, w2l, w1h, w1l = refs[:6]
+    even_ref, odd_ref, last_ref, out_ref, part_ref, two_ref, data_ref = refs[12:]
     device = device_ref[0]
-
-    def rows_of(r):
-        wide = []
-        for s in range(4 * r, 4 * r + 4):
-            block = g_ref[s]
-            wide.append(jnp.concatenate([block[:ROWS], block[ROWS:]], axis=1))
-        return jnp.concatenate(wide, axis=0)
-
-    zero, two, even, odd = quarters([rows_of(r) for r in range(4)])
-    spec_ref[0:INNER, :] = from_left(f0h, f0l, zero)
-    spec_ref[INNER : 2 * INNER, :] = from_left(f2h, f2l, two)
-    both = jnp.concatenate([even, odd], axis=0)
-    spec_ref[2 * INNER : 4 * INNER, :] = from_left(f1h, f1l, both)
+    to_frequency(device, g_refs, refs[6:12], part_ref, two_ref)
     _, weight = lane_frequency(device, (8, LANES))
     total = jnp.zeros((HALF, LANES), jnp.float32)
     special = jnp.zeros((8, LANES), jnp.float32)
@@ -263,8 +299,8 @@
     fix = (lane == HALF) & (device == 0)
     for part in range(DEV):
         upper, lower = pl.ds(LANES * part, HALF), pl.ds(LANES * part + HALF, HALF)
-        x_one, x_two = spec_ref[upper, 0:LANES], spec_ref[upper, LANES : 2 * LANES]
-        y_one, y_two = spec_ref[lower, 0:LANES], spec_ref[lower, LANES : 2 * LANES]
+        x_one, x_two = one_ref[upper, :], two_ref[upper, :]
+        y_one, y_two = one_ref[lower, :], two_ref[lower, :]
         x_two = jnp.where(fix, -x_one, sign * pltpu.roll(x_two, HALF, 1))
         y_two = jnp.where(fix, -y_one, sign * pltpu.roll(y_two, HALF, 1))
         rows = pl.ds(HALF * part, HALF)
@@ -302,12 +338,16 @@
         out_ref[s, ROWS + 3 : BLOCK, :] = jnp.zeros((BLOCK - ROWS - 3, LANES), jnp.float32)
 
 
-def row_pass(device, g, sample, frequency, factors):
+def row_pass(device, one, g, sample, frequency, factors):
     out = jax.ShapeDtypeStruct((DEV, BLOCK, LANES), jnp.float32)
-    scratch = [pltpu.VMEM((N, 2 * LANES), jnp.float32), pltpu.VMEM((N, LANES), jnp.float32)]
-    specs = [pl.BlockSpec(memory_space=pltpu.SMEM)] + [pl.BlockSpec(memory_space=pltpu.VMEM)] * 16
-    run = call(rows_kernel, out, scratch, LIMIT[3], 4 * 10**9, specs)
-    return run(device, g, *sample, *frequency, *factors)
+    scratch = [
+        pltpu.VMEM((4, INNER, LANES), jnp.float32),
+        pltpu.VMEM((N, LANES), jnp.float32),
+        pltpu.VMEM((N, LANES), jnp.float32),
+    ]
+    specs = [pl.BlockSpec(memory_space=pltpu.SMEM)] + [pl.BlockSpec(memory_space=pltpu.VMEM)] * 24
+    run = call(rows_kernel, out, scratch, LIMIT[3], 3 * 10**9, specs)
+    return run(device, one, *g, *sample, *frequency, *factors)
 
 
 def peaks_kernel(bins_ref, x_ref, f0h, f0l, f2h, f2l, f1h, f1l, offsets_ref, *refs):
@@ -395,15 +435,26 @@
     return run(thresholds, x, *table, offsets)
 
 
+def chip_pairs(index):
+    return [(d, (d & 12 ^ (2 * (index & 4))) + ((d + index) & 3)) for d in range(DEV)]
+
+
 def body(shear, smoothing, offsets, thresholds):
     group = ("row", "col")
     device = lax.axis_index(group).astype(jnp.int32).reshape(1)
-    place = lax.axis_index("col").astype(jnp.int32).reshape(1)
 
     def exchange(x):
         return lax.all_to_all(x, group, split_axis=0, concat_axis=0, tiled=True)
 
-    blocks = pack(place, shear)
+    def scatter(keep, send):
+        got = lax.ppermute(send, group, [(d, d ^ 4) for d in range(DEV)])
+        blocks = merge(keep, got)
+        done = [blocks[0]]
+        for index in ORDER:
+            done.append((index, lax.ppermute(blocks[index], group, chip_pairs(index))))
+        return [blocks[0]] + [value for _, value in sorted(done[1:], key=lambda item: item[0])]
+
+    blocks = pack(device, shear)
     fields = []
     for field in range(2):
         got = [blocks[4 * field], None, None, None]
@@ -412,9 +463,12 @@
             got[4 - step] = lax.ppermute(blocks[4 * field + step], "col", pairs)
         fields.append(got)
     sample, frequency, factors = tables(smoothing, device)
-    g = columns(0, place, fields[0], sample)
-    g = columns(1, place, fields[1], sample, g)
-    k = row_pass(device, exchange(g), sample, frequency, factors)
+    g = columns(device, fields[0], sample)
+    one = scatter(*g)
+    g = columns(device, fields[1], sample)
+    two = scatter(*g)
+    one = first_pass(device, one, frequency)
+    k = row_pass(device, one, two, sample, frequency, factors)
     out = peak_pass(thresholds, exchange(k), frequency, offsets[0])
     snr, heights, counts = out
     counts = exchange(counts)

time: 106 us -> 105 us (level)
  blocking collectives: 59.8 us -> 33 us
  starting transfers between devices: 7.81 us -> 24.1 us
  waiting for transfers between devices: 14 us -> 24.3 us
    all_to_all x3 -> x2, blocking collectives: 59.8 us -> 33 us  [exchange(): return lax.all_to_all(x, group, split_axis=0, concat_axis=0, tiled=True)]
    ppermute x0 -> x16, starting transfers between devices: none -> 16.2 us  [the longest x14 12.6 us: scatter(): done.append((index, lax.ppermute(blocks[index], group, chip_pairs(index))))]
    ppermute x0 -> x16, waiting for transfers between devices: none -> 13.4 us  [the longest x14 13.4 us: scatter(): done.append((index, lax.ppermute(blocks[index], group, chip_pairs(index))))]
    ppermute x6, waiting for transfers between devices: 14 us -> 11 us  [body(): got[4 - step] = lax.ppermute(blocks[4 * field + step], 'col', pairs)]
    pallas_call x4 -> x7, Pallas kernels: 9.87 us -> 8.96 us  [the longest x1 3.76 us: row_pass(): return run(device, one, *g, *sample, *frequency, *factors)]
  transfers between devices with their start and end apart: 6 -> 22, of which waited for: 4 -> 10; matrix products, arithmetic and copies ran while one was open for 0% -> 0% of each run, Pallas kernels for 7% -> 10%
where the time goes in v3:
time: 105 us; the launch traced here: 104 us
  blocking collectives  33 us (31%)
  waiting for transfers between devices  24.3 us (23%)
  starting transfers between devices  24.1 us (23%)
  Pallas kernels  19.4 us (18%)
  local copies, waits for them, and re-layouts  1.6 us (2%)
  between operations  1.4 us (1%)
    all_to_all x2, blocking collectives, exchange(): return lax.all_to_all(x, group, split_axis=0, concat_axis=0, tiled=True)  33 us
    ppermute x14, waiting for transfers between devices, scatter(): done.append((index, lax.ppermute(blocks[index], group, chip_pairs(index))))  13.4 us
    ppermute x14, starting transfers between devices, scatter(): done.append((index, lax.ppermute(blocks[index], group, chip_pairs(index))))  12.6 us
    ppermute x6, waiting for transfers between devices, body(): got[4 - step] = lax.ppermute(blocks[4 * field + step], 'col', pairs)  11 us
    ppermute x6, starting transfers between devices, body(): got[4 - step] = lax.ppermute(blocks[4 * field + step], 'col', pairs)  7.81 us
    pallas_call x1, Pallas kernels, tables(): call(tables_kernel, out, scratch, LIMIT[0], 10 ** 9, [smem, smem])  5.89 us
    pallas_call x1, Pallas kernels, peak_pass(): return run(thresholds, x, *table, offsets)  4.6 us
    pallas_call x1, Pallas kernels, row_pass(): return run(device, one, *g, *sample, *frequency, *factors)  3.76 us
  transfers between devices with their start and end apart: 22, of which 10 were waited for; matrix products, arithmetic and copies ran while one was open for 0% of the time, Pallas kernels for 10%

profile of v3, /device:TPU:1, one launch (start us, length us, event | category | flops | bytes accessed | tf_op | source)
XLA Modules:
  0.0 104.4 jit_solution(8971402438473221920)
XLA Ops:
  0.6 1.6 %copy-done = f32[2,1,512,512]{3,2,1,0:T(8,128)S(1)} copy-done((f32[2,1,512,512]{3,2,1,0:T(8,128)S(1)}, f32[2,1,512,512]{3,2,1,0:T(8,128)}, u32[]{:S(2)}) %copy-start) | copy-done | bytes 2097176
  2.4 3.4 %collective-permute-start = (f32[128,512]{1,0:T(8,128)S(1)}, f32[128,512]{1,0:T(8,128)S(1)}, u32[]{:S(2)}, u32[]{:S(2)}) collective-permute-start(f32[128,512]{1,0:T(8,128)S(1)} %get-tuple-element.50), channel_id=1, source_target_pairs={{0,3},{1,0},{2,1},{3,2},{4,7},{5,4},{6,5},{7,6},{8,11},{9,8},{10,9... | collective-permute-start | bytes 786440 | tf_op jit(solution)/shard_map/ppermute | solution.py:463
  6.9 2.1 %collective-permute-start.11 = (f32[128,512]{1,0:T(8,128)S(1)}, f32[128,512]{1,0:T(8,128)S(1)}, u32[]{:S(2)}, u32[]{:S(2)}) collective-permute-start(f32[128,512]{1,0:T(8,128)S(1)} %get-tuple-element.76), channel_id=1, source_target_pairs={{0,3},{1,0},{2,1},{3,2},{4,7},{5,4},{6,5},{7,6},{8,11},{9,8},{10,9... | collective-permute-start | bytes 786440 | tf_op jit(solution)/shard_map/ppermute | solution.py:463
  10.8 2.6 %collective-permute-done.refs_1_ = f32[128,512]{1,0:T(8,128)S(1)} collective-permute-done((f32[128,512]{1,0:T(8,128)S(1)}, f32[128,512]{1,0:T(8,128)S(1)}, u32[]{:S(2)}, u32[]{:S(2)}) %collective-permute-start) | collective-permute-done | bytes 262176 | tf_op jit(solution)/shard_map/ppermute | solution.py:463
  13.4 5.9 %shard_map.68 = (bf16[512,512]{1,0:T(8,128)(2,1)S(1)}, bf16[512,512]{1,0:T(8,128)(2,1)S(1)}, bf16[512,512]{1,0:T(8,128)(2,1)S(1)}, bf16[512,512]{1,0:T(8,128)(2,...) custom-call(f32[1]{0:T(128)S(6)} %copy.7.smooth_ref, ...), custom_call_target="tpu_custom_call" | custom-call | flops 1000000000 | bytes 4194304 | tf_op jit(solution)/shard_map/pallas_call | solution.py:185
  19.3 3.1 %collective-permute-done.2.refs_3_ = f32[128,512]{1,0:T(8,128)S(1)} collective-permute-done((f32[128,512]{1,0:T(8,128)S(1)}, f32[128,512]{1,0:T(8,128)S(1)}, u32[]{:S(2)}, u32[]{:S(2)}) %collective-permute-start.2) | collective-permute-done | bytes 262176 | tf_op jit(solution)/shard_map/ppermute | solution.py:463
  22.4 1.5 %shard_map.69 = (f32[8,128,128]{2,1,0:T(8,128)S(1)}, f32[8,128,128]{2,1,0:T(8,128)S(1)}) custom-call(s32[1]{0:T(128)} %bitcast.device_ref, f32[128,512]{1,0:T(8,128)S(1)} %get-tuple-element.49.refs_0_, f32[128,512]{1,0:T(8,128)S(1)} %collective-permute-done.refs_1_, f32[128,512]{1,0:T(8,128)S(1)} %collective-permute-done.1.refs_2_, ...), custom_call_target="tpu_custom_call" | custom-call | flops 2000000000 | bytes 4194304 | tf_op jit(solution)/shard_map/pallas_call | solution.py:243
  23.9 3.1 %collective-permute-start.3 = (f32[8,128,128]{2,1,0:T(8,128)S(1)}, f32[8,128,128]{2,1,0:T(8,128)S(1)}, u32[]{:S(2)}, u32[]{:S(2)}) collective-permute-start(f32[8,128,128]{2,1,0:T(8,128)S(1)} %get-tuple-element.60), channel_id=1, source_target_pairs={{0,4},{1,5},{2,6},{3,7},{4,0},{5,1},{6,2},{7,3},{8,12},{9,13},{10,... | collective-permute-start | bytes 1572872 | tf_op jit(solution)/shard_map/ppermute | solution.py:450
  27.4 4.8 %collective-permute-done.13.refs_3_ = f32[128,512]{1,0:T(8,128)S(1)} collective-permute-done((f32[128,512]{1,0:T(8,128)S(1)}, f32[128,512]{1,0:T(8,128)S(1)}, u32[]{:S(2)}, u32[]{:S(2)}) %collective-permute-start.13) | collective-permute-done | bytes 262176 | tf_op jit(solution)/shard_map/ppermute | solution.py:463
  32.3 1.5 %shard_map.72 = (f32[8,128,128]{2,1,0:T(8,128)S(1)}, f32[8,128,128]{2,1,0:T(8,128)S(1)}) custom-call(s32[1]{0:T(128)} %bitcast.device_ref, f32[128,512]{1,0:T(8,128)S(1)} %get-tuple-element.75.refs_0_, f32[128,512]{1,0:T(8,128)S(1)} %collective-permute-done.11.refs_1_, f32[128,512]{1,0:T(8,128)S(1)} %collective-permute-done.12.refs_2_, ...), custom_call_target="tpu_custom_call" | custom-call | flops 2000000000 | bytes 4194304 | tf_op jit(solution)/shard_map/pallas_call | solution.py:243
  34.6 1.5 %collective-permute-start.5 = (f32[2,128,128]{2,1,0:T(8,128)S(1)}, f32[2,128,128]{2,1,0:T(8,128)S(1)}, u32[]{:S(2)}, u32[]{:S(2)}) collective-permute-start(f32[2,128,128]{2,1,0:T(8,128)S(1)} %get-tuple-element.63), channel_id=1, source_target_pairs={{0,2},{1,3},{2,0},{3,1},{4,6},{5,7},{6,4},{7,5},{8,10},{9,11},{10,... | collective-permute-start | bytes 393224 | tf_op jit(solution)/shard_map/ppermute | solution.py:454
  37.3 1.3 %collective-permute-start.7 = (f32[2,128,128]{2,1,0:T(8,128)S(1)}, f32[2,128,128]{2,1,0:T(8,128)S(1)}, u32[]{:S(2)}, u32[]{:S(2)}) collective-permute-start(f32[2,128,128]{2,1,0:T(8,128)S(1)} %get-tuple-element.65), channel_id=1, source_target_pairs={{0,8},{1,9},{2,10},{3,11},{4,12},{5,13},{6,14},{7,15},{8,0},{9,1},... | collective-permute-start | bytes 393224 | tf_op jit(solution)/shard_map/ppermute | solution.py:454
  39.1 4.5 %collective-permute-done.4.refs_1_ = f32[2,128,128]{2,1,0:T(8,128)S(1)} collective-permute-done((f32[2,128,128]{2,1,0:T(8,128)S(1)}, f32[2,128,128]{2,1,0:T(8,128)S(1)}, u32[]{:S(2)}, u32[]{:S(2)}) %collective-permute-start.4) | collective-permute-done | bytes 131104 | tf_op jit(solution)/shard_map/ppermute | solution.py:454
  44.6 1.5 %collective-permute-start.15 = (f32[2,128,128]{2,1,0:T(8,128)S(1)}, f32[2,128,128]{2,1,0:T(8,128)S(1)}, u32[]{:S(2)}, u32[]{:S(2)}) collective-permute-start(f32[2,128,128]{2,1,0:T(8,128)S(1)} %get-tuple-element.82), channel_id=1, source_target_pairs={{0,1},{1,2},{2,3},{3,0},{4,5},{5,6},{6,7},{7,4},{8,9},{9,10},{10,1... | collective-permute-start | bytes 393224 | tf_op jit(solution)/shard_map/ppermute | solution.py:454
  46.1 2.9 %collective-permute-start.16 = (f32[2,128,128]{2,1,0:T(8,128)S(1)}, f32[2,128,128]{2,1,0:T(8,128)S(1)}, u32[]{:S(2)}, u32[]{:S(2)}) collective-permute-start(f32[2,128,128]{2,1,0:T(8,128)S(1)} %get-tuple-element.83), channel_id=1, source_target_pairs={{0,2},{1,3},{2,0},{3,1},{4,6},{5,7},{6,4},{7,5},{8,10},{9,11},{10,... | collective-permute-start | bytes 393224 | tf_op jit(solution)/shard_map/ppermute | solution.py:454
  50.6 1.2 %collective-permute-start.18 = (f32[2,128,128]{2,1,0:T(8,128)S(1)}, f32[2,128,128]{2,1,0:T(8,128)S(1)}, u32[]{:S(2)}, u32[]{:S(2)}) collective-permute-start(f32[2,128,128]{2,1,0:T(8,128)S(1)} %get-tuple-element.85), channel_id=1, source_target_pairs={{0,8},{1,9},{2,10},{3,11},{4,12},{5,13},{6,14},{7,15},{8,0},{9,1},... | collective-permute-start | bytes 393224 | tf_op jit(solution)/shard_map/ppermute | solution.py:454
  51.8 3.1 %collective-permute-done.15.refs_1_ = f32[2,128,128]{2,1,0:T(8,128)S(1)} collective-permute-done((f32[2,128,128]{2,1,0:T(8,128)S(1)}, f32[2,128,128]{2,1,0:T(8,128)S(1)}, u32[]{:S(2)}, u32[]{:S(2)}) %collective-permute-start.15) | collective-permute-done | bytes 131104 | tf_op jit(solution)/shard_map/ppermute | solution.py:454
  55.8 1.9 %shard_map.71.one_ref = f32[2048,128]{1,0:T(8,128)S(1)} custom-call(s32[1]{0:T(128)} %bitcast.device_ref, f32[2,128,128]{2,1,0:T(8,128)S(1)} %get-tuple-element.61.refs_0_, f32[2,128,128]{2,1,0:T(8,128)S(1)} %collective-permute-done.4.refs_1_, f32[2,128,128]{2,1,0:T(8,128)S(1)} %collective-permute-done.5.refs_2_, ...), custom_call_target="tpu_custom_call" | custom-call | flops 1000000000 | bytes 4194304 | tf_op jit(solution)/shard_map/pallas_call | solution.py:285
  57.7 1.4 %collective-permute-done.19.refs_5_ = f32[2,128,128]{2,1,0:T(8,128)S(1)} collective-permute-done((f32[2,128,128]{2,1,0:T(8,128)S(1)}, f32[2,128,128]{2,1,0:T(8,128)S(1)}, u32[]{:S(2)}, u32[]{:S(2)}) %collective-permute-start.19) | collective-permute-done | bytes 131104 | tf_op jit(solution)/shard_map/ppermute | solution.py:454
  59.1 3.3 %collective-permute-done.20.refs_6_ = f32[2,128,128]{2,1,0:T(8,128)S(1)} collective-permute-done((f32[2,128,128]{2,1,0:T(8,128)S(1)}, f32[2,128,128]{2,1,0:T(8,128)S(1)}, u32[]{:S(2)}, u32[]{:S(2)}) %collective-permute-start.20) | collective-permute-done | bytes 131104 | tf_op jit(solution)/shard_map/ppermute | solution.py:454
  62.4 3.8 %shard_map.74 = f32[16,136,128]{2,1,0:T(8,128)S(1)} custom-call(s32[1]{0:T(128)} %bitcast.device_ref, f32[2048,128]{1,0:T(8,128)S(1)} %shard_map.71.one_ref, f32[2,128,128]{2,1,0:T(8,128)S(1)} %get-tuple-element.81.refs_0_, f32[2,128,128]{2,1,0:T(8,128)S(1)} %collective-permute-done.15.refs_1_, f32[2,128,128]{2,1,0:T(8,128)S(1)} %collective-permute-done.16.refs_2_, ...), custom_call_target="tpu_custom_call" | custom-call | flops 3000000000 | bytes 4194304 | tf_op jit(solution)/shard_map/pallas_call | solution.py:350
  66.2 24.2 %all_to_all.10.x_ref = f32[16,136,128]{2,1,0:T(8,128)S(1)} all-to-all(f32[16,136,128]{2,1,0:T(8,128)S(1)} %shard_map.74), channel_id=1, replica_groups=mesh['maps'=16,'row'=4,'col'=4] {'row','col'}, dimensions={0} | all-to-all | bytes 2228224 | tf_op jit(solution)/shard_map/all_to_all | solution.py:447
  90.5 4.6 %shard_map.75 = (f32[128,2048]{1,0:T(8,128)}, f32[8,128]{1,0:T(8,128)}, f32[16,8,128]{2,1,0:T(8,128)S(1)}) custom-call(s32[1,16]{1,0:T(1,128)S(1)} %copy-done.2, f32[16,136,128]{2,1,0:T(8,128)S(1)} %all_to_all.10.x_ref, bf16[512,512]{1,0:T(8,128)(2,1)S(1)} %get-tuple-element.69.refs_8_.refs_14_.f0h, ...), custom_call_target="tpu_custom_call" | custom-call | flops 2000000000 | bytes 4194304 | tf_op jit(solution)/shard_map/pallas_call | solution.py:435
  95.1 8.8 %all_to_all.11 = f32[16,8,128]{2,1,0:T(8,128)S(1)} all-to-all(f32[16,8,128]{2,1,0:T(8,128)S(1)} %get-tuple-element.94), channel_id=1, replica_groups=mesh['maps'=16,'row'=4,'col'=4] {'row','col'}, dimensions={0} | all-to-all | bytes 131072 | tf_op jit(solution)/shard_map/all_to_all | solution.py:447
  (38 shorter events, 9.4 us)
Async XLA Ops:
  2.4 11.0 %collective-permute-start = (f32[128,512]{1,0:T(8,128)S(1)}, f32[128,512]{1,0:T(8,128)S(1)}, u32[]{:S(2)}, u32[]{:S(2)}) collective-permute-start(f32[128,512]{1,0:T(8,128)S(1)} %get-tuple-element.50), channel_id=1, source_target_pairs={{0,3},{1,0},{2,1},{3,2},{4,7},{5,4},{6,5},{7,6},{8,11},{9,8},{10,9... | collective-permute-start | bytes 786440 | tf_op jit(solution)/shard_map/ppermute | solution.py:463
  5.7 13.6 %collective-permute-start.1 = (f32[128,512]{1,0:T(8,128)S(1)}, f32[128,512]{1,0:T(8,128)S(1)}, u32[]{:S(2)}, u32[]{:S(2)}) collective-permute-start(f32[128,512]{1,0:T(8,128)S(1)} %get-tuple-element.51), channel_id=1, source_target_pairs={{0,2},{1,3},{2,0},{3,1},{4,6},{5,7},{6,4},{7,5},{8,10},{9,11},{10,... | collective-permute-start | bytes 786440 | tf_op jit(solution)/shard_map/ppermute | solution.py:463
  6.3 16.1 %collective-permute-start.2 = (f32[128,512]{1,0:T(8,128)S(1)}, f32[128,512]{1,0:T(8,128)S(1)}, u32[]{:S(2)}, u32[]{:S(2)}) collective-permute-start(f32[128,512]{1,0:T(8,128)S(1)} %get-tuple-element.52), channel_id=1, source_target_pairs={{0,1},{1,2},{2,3},{3,0},{4,5},{5,6},{6,7},{7,4},{8,9},{9,10},{10,1... | collective-permute-start | bytes 786440 | tf_op jit(solution)/shard_map/ppermute | solution.py:463
  6.9 20.6 %collective-permute-start.11 = (f32[128,512]{1,0:T(8,128)S(1)}, f32[128,512]{1,0:T(8,128)S(1)}, u32[]{:S(2)}, u32[]{:S(2)}) collective-permute-start(f32[128,512]{1,0:T(8,128)S(1)} %get-tuple-element.76), channel_id=1, source_target_pairs={{0,3},{1,0},{2,1},{3,2},{4,7},{5,4},{6,5},{7,6},{8,11},{9,8},{10,9... | collective-permute-start | bytes 786440 | tf_op jit(solution)/shard_map/ppermute | solution.py:463
  8.9 18.5 %collective-permute-start.12 = (f32[128,512]{1,0:T(8,128)S(1)}, f32[128,512]{1,0:T(8,128)S(1)}, u32[]{:S(2)}, u32[]{:S(2)}) collective-permute-start(f32[128,512]{1,0:T(8,128)S(1)} %get-tuple-element.77), channel_id=1, source_target_pairs={{0,2},{1,3},{2,0},{3,1},{4,6},{5,7},{6,4},{7,5},{8,10},{9,11},{10,... | collective-permute-start | bytes 786440 | tf_op jit(solution)/shard_map/ppermute | solution.py:463
  13.4 18.9 %collective-permute-start.13 = (f32[128,512]{1,0:T(8,128)S(1)}, f32[128,512]{1,0:T(8,128)S(1)}, u32[]{:S(2)}, u32[]{:S(2)}) collective-permute-start(f32[128,512]{1,0:T(8,128)S(1)} %get-tuple-element.78), channel_id=1, source_target_pairs={{0,1},{1,2},{2,3},{3,0},{4,5},{5,6},{6,7},{7,4},{8,9},{9,10},{10,1... | collective-permute-start | bytes 786440 | tf_op jit(solution)/shard_map/ppermute | solution.py:463
  23.9 10.6 %collective-permute-start.3 = (f32[8,128,128]{2,1,0:T(8,128)S(1)}, f32[8,128,128]{2,1,0:T(8,128)S(1)}, u32[]{:S(2)}, u32[]{:S(2)}) collective-permute-start(f32[8,128,128]{2,1,0:T(8,128)S(1)} %get-tuple-element.60), channel_id=1, source_target_pairs={{0,4},{1,5},{2,6},{3,7},{4,0},{5,1},{6,2},{7,3},{8,12},{9,13},{10,... | collective-permute-start | bytes 1572872 | tf_op jit(solution)/shard_map/ppermute | solution.py:450
  33.8 4.8 %collective-permute-start.14 = (f32[8,128,128]{2,1,0:T(8,128)S(1)}, f32[8,128,128]{2,1,0:T(8,128)S(1)}, u32[]{:S(2)}, u32[]{:S(2)}) collective-permute-start(f32[8,128,128]{2,1,0:T(8,128)S(1)} %get-tuple-element.80), channel_id=1, source_target_pairs={{0,4},{1,5},{2,6},{3,7},{4,0},{5,1},{6,2},{7,3},{8,12},{9,13},{10,... | collective-permute-start | bytes 1572872 | tf_op jit(solution)/shard_map/ppermute | solution.py:450
  34.5 9.1 %collective-permute-start.4 = (f32[2,128,128]{2,1,0:T(8,128)S(1)}, f32[2,128,128]{2,1,0:T(8,128)S(1)}, u32[]{:S(2)}, u32[]{:S(2)}) collective-permute-start(f32[2,128,128]{2,1,0:T(8,128)S(1)} %get-tuple-element.62), channel_id=1, source_target_pairs={{0,1},{1,2},{2,3},{3,0},{4,5},{5,6},{6,7},{7,4},{8,9},{9,10},{10,1... | collective-permute-start | bytes 393224 | tf_op jit(solution)/shard_map/ppermute | solution.py:454
  34.6 9.0 %collective-permute-start.5 = (f32[2,128,128]{2,1,0:T(8,128)S(1)}, f32[2,128,128]{2,1,0:T(8,128)S(1)}, u32[]{:S(2)}, u32[]{:S(2)}) collective-permute-start(f32[2,128,128]{2,1,0:T(8,128)S(1)} %get-tuple-element.63), channel_id=1, source_target_pairs={{0,2},{1,3},{2,0},{3,1},{4,6},{5,7},{6,4},{7,5},{8,10},{9,11},{10,... | collective-permute-start | bytes 393224 | tf_op jit(solution)/shard_map/ppermute | solution.py:454
  36.1 8.4 %collective-permute-start.6 = (f32[2,128,128]{2,1,0:T(8,128)S(1)}, f32[2,128,128]{2,1,0:T(8,128)S(1)}, u32[]{:S(2)}, u32[]{:S(2)}) collective-permute-start(f32[2,128,128]{2,1,0:T(8,128)S(1)} %get-tuple-element.64), channel_id=1, source_target_pairs={{0,3},{1,0},{2,1},{3,2},{4,7},{5,4},{6,5},{7,6},{8,11},{9,8},{10,9... | collective-permute-start | bytes 393224 | tf_op jit(solution)/shard_map/ppermute | solution.py:454
  37.3 8.9 %collective-permute-start.7 = (f32[2,128,128]{2,1,0:T(8,128)S(1)}, f32[2,128,128]{2,1,0:T(8,128)S(1)}, u32[]{:S(2)}, u32[]{:S(2)}) collective-permute-start(f32[2,128,128]{2,1,0:T(8,128)S(1)} %get-tuple-element.65), channel_id=1, source_target_pairs={{0,8},{1,9},{2,10},{3,11},{4,12},{5,13},{6,14},{7,15},{8,0},{9,1},... | collective-permute-start | bytes 393224 | tf_op jit(solution)/shard_map/ppermute | solution.py:454
  38.6 10.4 %collective-permute-start.8 = (f32[2,128,128]{2,1,0:T(8,128)S(1)}, f32[2,128,128]{2,1,0:T(8,128)S(1)}, u32[]{:S(2)}, u32[]{:S(2)}) collective-permute-start(f32[2,128,128]{2,1,0:T(8,128)S(1)} %get-tuple-element.66), channel_id=1, source_target_pairs={{0,9},{1,10},{2,11},{3,8},{4,13},{5,14},{6,15},{7,12},{8,1},{9,2},... | collective-permute-start | bytes 393224 | tf_op jit(solution)/shard_map/ppermute | solution.py:454
  43.6 6.9 %collective-permute-start.9 = (f32[2,128,128]{2,1,0:T(8,128)S(1)}, f32[2,128,128]{2,1,0:T(8,128)S(1)}, u32[]{:S(2)}, u32[]{:S(2)}) collective-permute-start(f32[2,128,128]{2,1,0:T(8,128)S(1)} %get-tuple-element.67), channel_id=1, source_target_pairs={{0,10},{1,11},{2,8},{3,9},{4,14},{5,15},{6,12},{7,13},{8,2},{9,3},... | collective-permute-start | bytes 393224 | tf_op jit(solution)/shard_map/ppermute | solution.py:454
  43.6 8.2 %collective-permute-start.10 = (f32[2,128,128]{2,1,0:T(8,128)S(1)}, f32[2,128,128]{2,1,0:T(8,128)S(1)}, u32[]{:S(2)}, u32[]{:S(2)}) collective-permute-start(f32[2,128,128]{2,1,0:T(8,128)S(1)} %get-tuple-element.68), channel_id=1, source_target_pairs={{0,11},{1,8},{2,9},{3,10},{4,15},{5,12},{6,13},{7,14},{8,3},{9,0},... | collective-permute-start | bytes 393224 | tf_op jit(solution)/shard_map/ppermute | solution.py:454
  44.6 10.4 %collective-permute-start.15 = (f32[2,128,128]{2,1,0:T(8,128)S(1)}, f32[2,128,128]{2,1,0:T(8,128)S(1)}, u32[]{:S(2)}, u32[]{:S(2)}) collective-permute-start(f32[2,128,128]{2,1,0:T(8,128)S(1)} %get-tuple-element.82), channel_id=1, source_target_pairs={{0,1},{1,2},{2,3},{3,0},{4,5},{5,6},{6,7},{7,4},{8,9},{9,10},{10,1... | collective-permute-start | bytes 393224 | tf_op jit(solution)/shard_map/ppermute | solution.py:454
  46.1 9.0 %collective-permute-start.16 = (f32[2,128,128]{2,1,0:T(8,128)S(1)}, f32[2,128,128]{2,1,0:T(8,128)S(1)}, u32[]{:S(2)}, u32[]{:S(2)}) collective-permute-start(f32[2,128,128]{2,1,0:T(8,128)S(1)} %get-tuple-element.83), channel_id=1, source_target_pairs={{0,2},{1,3},{2,0},{3,1},{4,6},{5,7},{6,4},{7,5},{8,10},{9,11},{10,... | collective-permute-start | bytes 393224 | tf_op jit(solution)/shard_map/ppermute | solution.py:454
  49.0 8.7 %collective-permute-start.17 = (f32[2,128,128]{2,1,0:T(8,128)S(1)}, f32[2,128,128]{2,1,0:T(8,128)S(1)}, u32[]{:S(2)}, u32[]{:S(2)}) collective-permute-start(f32[2,128,128]{2,1,0:T(8,128)S(1)} %get-tuple-element.84), channel_id=1, source_target_pairs={{0,3},{1,0},{2,1},{3,2},{4,7},{5,4},{6,5},{7,6},{8,11},{9,8},{10,9... | collective-permute-start | bytes 393224 | tf_op jit(solution)/shard_map/ppermute | solution.py:454
  50.6 7.1 %collective-permute-start.18 = (f32[2,128,128]{2,1,0:T(8,128)S(1)}, f32[2,128,128]{2,1,0:T(8,128)S(1)}, u32[]{:S(2)}, u32[]{:S(2)}) collective-permute-start(f32[2,128,128]{2,1,0:T(8,128)S(1)} %get-tuple-element.85), channel_id=1, source_target_pairs={{0,8},{1,9},{2,10},{3,11},{4,12},{5,13},{6,14},{7,15},{8,0},{9,1},... | collective-permute-start | bytes 393224 | tf_op jit(solution)/shard_map/ppermute | solution.py:454
  51.8 7.3 %collective-permute-start.19 = (f32[2,128,128]{2,1,0:T(8,128)S(1)}, f32[2,128,128]{2,1,0:T(8,128)S(1)}, u32[]{:S(2)}, u32[]{:S(2)}) collective-permute-start(f32[2,128,128]{2,1,0:T(8,128)S(1)} %get-tuple-element.86), channel_id=1, source_target_pairs={{0,9},{1,10},{2,11},{3,8},{4,13},{5,14},{6,15},{7,12},{8,1},{9,2},... | collective-permute-start | bytes 393224 | tf_op jit(solution)/shard_map/ppermute | solution.py:454
  55.0 7.5 %collective-permute-start.20 = (f32[2,128,128]{2,1,0:T(8,128)S(1)}, f32[2,128,128]{2,1,0:T(8,128)S(1)}, u32[]{:S(2)}, u32[]{:S(2)}) collective-permute-start(f32[2,128,128]{2,1,0:T(8,128)S(1)} %get-tuple-element.87), channel_id=1, source_target_pairs={{0,10},{1,11},{2,8},{3,9},{4,14},{5,15},{6,12},{7,13},{8,2},{9,3},... | collective-permute-start | bytes 393224 | tf_op jit(solution)/shard_map/ppermute | solution.py:454
  55.2 7.3 %collective-permute-start.21 = (f32[2,128,128]{2,1,0:T(8,128)S(1)}, f32[2,128,128]{2,1,0:T(8,128)S(1)}, u32[]{:S(2)}, u32[]{:S(2)}) collective-permute-start(f32[2,128,128]{2,1,0:T(8,128)S(1)} %get-tuple-element.88), channel_id=1, source_target_pairs={{0,11},{1,8},{2,9},{3,10},{4,15},{5,12},{6,13},{7,14},{8,3},{9,0},... | collective-permute-start | bytes 393224 | tf_op jit(solution)/shard_map/ppermute | solution.py:454
  66.2 24.2 %copy-start.1 = (s32[1,8,128]{2,1,0:T(8,128)S(1)}, s32[1,8,128]{2,1,0:T(8,128)}, u32[]{:S(2)}) copy-start(s32[1,8,128]{2,1,0:T(8,128)} %param.6) | copy-start | bytes 12292
  66.2 24.2 %copy-start.2 = (s32[1,16]{1,0:T(1,128)S(1)}, s32[1,16]{1,0:T(1,128)}, u32[]{:S(2)}) copy-start(s32[1,16]{1,0:T(1,128)} %bins_ref.1) | copy-start | bytes 196
  (1 other events, 1.6 us)

commit v4 on v3

--- a/solution.py
+++ b/solution.py
@@ -11,13 +11,15 @@
 
 N = 2048
 INNER = 512
+DENSE = 256
 DEV = 16
 ROWS = 128
 LANES = 128
 HALF = 64
 CELL = 16
 BLOCK = ROWS + 8
-CLASSES = ((0, 0, 4), (2, 4, 4), (1, 8, 8))
+CLASSES = ((0, 0, 2), (4, 2, 2), (2, 4, 4), (1, 8, 4), (3, 12, 4))
+ROOT = math.sqrt(0.5)
 MIB = 1 << 20
 LIMIT = (20, 24, 24, 36, 28)
 ORDER = (6, 2, 5, 7, 1, 3, 4)
@@ -57,6 +59,44 @@
     return both[:height] + (both[height:] + dot(high, low_ref[...]))
 
 
+def pairs(refs):
+    return tuple(zip(refs[0::2], refs[1::2]))
+
+
+def take(x, start, size, axis):
+    return lax.slice_in_dim(x, start, start + size, axis=axis)
+
+
+def front(zero, two, even, odd, axis):
+    near = [take(x, 0, DENSE, axis) for x in (zero, two, even, odd)]
+    far = [take(x, DENSE, DENSE, axis) for x in (zero, two, even, odd)]
+    change, total = ROOT * (far[2] - far[3]), ROOT * (far[2] + far[3])
+    join = partial(jnp.concatenate, axis=axis)
+    return (
+        near[0] + far[0],
+        near[0] - far[0],
+        join([near[1], -far[1]]),
+        join([near[2] + change, -near[3] - total]),
+        join([near[2] - change, near[3] - total]),
+    )
+
+
+def back(values, axis):
+    first, second, turn, one, three = values
+    real = [take(x, 0, DENSE, axis) for x in (turn, one, three)]
+    imag = [take(x, DENSE, DENSE, axis) for x in (turn, one, three)]
+    change, total = real[1] - real[2], -imag[1] - imag[2]
+    halves = (
+        (first + second, real[0], real[1] + real[2], imag[2] - imag[1]),
+        (first - second, -imag[0], ROOT * (total + change), ROOT * (total - change)),
+    )
+    blocks = []
+    for zero, two, even, odd in halves:
+        plus, minus = zero + two, zero - two
+        blocks.append((plus + even, minus + odd, plus - even, minus - odd))
+    return [jnp.concatenate([near, far], axis=axis) for near, far in zip(*blocks)]
+
+
 def angle(steps):
     wrapped = jnp.bitwise_and(steps, N - 1)
     wrapped = jnp.where(wrapped >= N // 2, wrapped - N, wrapped)
@@ -78,7 +118,7 @@
     for (start, _, blocks), (high_ref, low_ref) in zip(CLASSES, refs):
         width = LANES * blocks
         col = iota((HALF, width), 1)
-        freq = start + 4 * (HALF * (col // LANES) + col % HALF)
+        freq = start + 8 * (HALF * (col // LANES) + col % HALF)
         quarter = jnp.where(col % LANES >= HALF, 1, 0)
         if start == 0:
             freq = jnp.where(col == HALF, N // 2, freq)
@@ -88,39 +128,40 @@
         sin_ref[:, :width] = jnp.sin(fine)
         coarse = angle(freq[:8] * (HALF * iota((8, width), 0)) + INNER * quarter[:8])
         cos_high, sin_high = jnp.cos(coarse), jnp.sin(coarse)
-        for part in range(INNER // HALF):
+        for part in range(DENSE // HALF):
             cos_part, sin_part = cos_high[part : part + 1], sin_high[part : part + 1]
             rows = pl.ds(HALF * part, HALF)
             cos_fine, sin_fine = cos_ref[:, :width], sin_ref[:, :width]
             put(high_ref, low_ref, rows, slice(None), cos_part * cos_fine - sin_part * sin_fine)
-            if start == 1:
-                rows = pl.ds(INNER + HALF * part, HALF)
-                value = -(sin_part * cos_fine + cos_part * sin_fine)
+            if blocks == 4:
+                rows = pl.ds(DENSE + HALF * part, HALF)
+                value = sin_part * cos_fine + cos_part * sin_fine
                 put(high_ref, low_ref, rows, slice(None), value)
 
 
 def frequency_form(refs, scratch):
     cos_ref, sin_ref = scratch
-    fine = angle(4 * iota((HALF, INNER), 0) * iota((HALF, INNER), 1))
-    cos_ref[:, :INNER] = jnp.cos(fine)
-    sin_ref[:, :INNER] = jnp.sin(fine)
+    fine = angle(8 * iota((HALF, DENSE), 0) * iota((HALF, DENSE), 1))
+    cos_ref[:, :DENSE] = jnp.cos(fine)
+    sin_ref[:, :DENSE] = jnp.sin(fine)
     for (start, _, blocks), (high_ref, low_ref) in zip(CLASSES, refs):
-        coarse = angle((start + 4 * HALF * iota((8, INNER), 0)) * iota((8, INNER), 1))
+        coarse = angle((start + 8 * HALF * iota((8, DENSE), 0)) * iota((8, DENSE), 1))
         cos_high, sin_high = jnp.cos(coarse), jnp.sin(coarse)
         for part in range(blocks):
             cos_part, sin_part = cos_high[part : part + 1], sin_high[part : part + 1]
-            cos_fine, sin_fine = cos_ref[:, :INNER], sin_ref[:, :INNER]
+            cos_fine, sin_fine = cos_ref[:, :DENSE], sin_ref[:, :DENSE]
             cosine = cos_part * cos_fine - sin_part * sin_fine
-            sine = -(sin_part * cos_fine + cos_part * sin_fine)
+            sine = sin_part * cos_fine + cos_part * sin_fine
+            turned = -sine
             if start == 0 and part == 0:
-                flip = (1 - 2 * (iota((HALF, INNER), 1) & 1)).astype(jnp.float32)
-                sine = jnp.where(iota((HALF, INNER), 0) == 0, flip, sine)
+                flip = (1 - 2 * (iota((HALF, DENSE), 1) & 1)).astype(jnp.float32)
+                turned = jnp.where(iota((HALF, DENSE), 0) == 0, flip, turned)
             upper, lower = pl.ds(LANES * part, HALF), pl.ds(LANES * part + HALF, HALF)
-            put(high_ref, low_ref, upper, pl.ds(0, INNER), cosine)
-            put(high_ref, low_ref, lower, pl.ds(0, INNER), sine)
-            if start == 1:
-                put(high_ref, low_ref, upper, pl.ds(INNER, INNER), sine)
-                put(high_ref, low_ref, lower, pl.ds(INNER, INNER), -cosine)
+            put(high_ref, low_ref, upper, pl.ds(0, DENSE), cosine)
+            put(high_ref, low_ref, lower, pl.ds(0, DENSE), turned)
+            if blocks == 4:
+                put(high_ref, low_ref, upper, pl.ds(DENSE, DENSE), sine)
+                put(high_ref, low_ref, lower, pl.ds(DENSE, DENSE), cosine)
 
 
 def signed(freq):
@@ -129,9 +170,10 @@
 
 def lane_frequency(device, shape):
     lane = iota(shape, 1)
-    block = jnp.where(device < 8, device % 4, device - 8)
-    start = jnp.where(device < 4, 0, jnp.where(device < 8, 2, 1))
-    freq = signed(start + 4 * (HALF * block + lane % HALF))
+    block = jnp.where(device < 4, device & 1, device & 3)
+    start = jnp.where(device < 2, 0, jnp.where(device < 4, 4, 2))
+    start = jnp.where(device < 8, start, jnp.where(device < 12, 1, 3))
+    freq = signed(start + 8 * (HALF * block + lane % HALF))
     nyquist = (device == 0) & (lane == HALF)
     freq = jnp.where(nyquist, -(N // 2), freq)
     single = nyquist | ((device == 0) & (lane == 0))
@@ -141,9 +183,8 @@
 def tables_kernel(smooth_ref, device_ref, *refs):
     device = device_ref[0]
     scratch = refs[-2:]
-    w_refs = tuple(zip(refs[0:6:2], refs[1:6:2]))
-    f_refs = tuple(zip(refs[6:12:2], refs[7:12:2]))
-    even_ref, odd_ref, last_ref = refs[12:15]
+    w_refs, f_refs = pairs(refs[0:10]), pairs(refs[10:20])
+    even_ref, odd_ref, last_ref = refs[20:23]
     sample_form(w_refs, scratch)
     frequency_form(f_refs, scratch)
     width = smooth_ref[0]
@@ -158,7 +199,7 @@
 
     for start, first, blocks in CLASSES:
         for part in range(blocks):
-            freq = signed(start + 4 * (HALF * part + iota(shape, 0)))
+            freq = signed(start + 8 * (HALF * part + iota(shape, 0)))
             row_weight = jnp.where(freq == 0, 1.0, 2.0) * (1.0 / (N * N))
             even, odd = factors(freq.astype(jnp.float32), weight * row_weight)
             rows = pl.ds(HALF * (first + part), HALF)
@@ -171,19 +212,18 @@
 
 def tables(smoothing, device):
     low = jnp.bfloat16
-    pairs = []
-    for _ in range(2):
-        for size in (INNER, INNER, 2 * INNER):
-            pairs += [jax.ShapeDtypeStruct((size, size), low)] * 2
-    out = pairs + [
+    table = []
+    for _, _, blocks in CLASSES:
+        table += [jax.ShapeDtypeStruct((LANES * blocks, LANES * blocks), low)] * 2
+    out = table + table + [
         jax.ShapeDtypeStruct((N // 2, LANES), jnp.float32),
         jax.ShapeDtypeStruct((N // 2, LANES), jnp.float32),
         jax.ShapeDtypeStruct((16, LANES), jnp.float32),
     ]
-    scratch = [pltpu.VMEM((HALF, 2 * INNER), jnp.float32)] * 2
+    scratch = [pltpu.VMEM((HALF, INNER), jnp.float32)] * 2
     smem = pl.BlockSpec(memory_space=pltpu.SMEM)
     result = call(tables_kernel, out, scratch, LIMIT[0], 10**9, [smem, smem])(smoothing, device)
-    return result[0:6], result[6:12], result[12:15]
+    return result[0:10], result[10:20], result[20:23]
 
 
 def quarters(blocks):
@@ -209,8 +249,8 @@
 
 
 def columns_kernel(device_ref, *refs):
-    blocks, table = refs[:4], refs[4:10]
-    keep_ref, send_ref, all_ref = refs[10:]
+    blocks, table = refs[:4], pairs(refs[4:14])
+    keep_ref, send_ref, all_ref = refs[14:]
     zero, two, even, odd = quarters([x[...] for x in blocks])
     device = device_ref[0]
     place = device & 3
@@ -218,14 +258,12 @@
     across = jnp.where(place == 1, 1.0, jnp.where(place == 3, -1.0, 0.0))
     flip = jnp.where((place & 1) == 0, 1.0, -1.0)
 
-    def emit(value, first):
-        for part in range(value.shape[1] // LANES):
+    even, odd = along * even - across * odd, across * even + along * odd
+    operands = front(zero, flip * two, even, odd, 1)
+    for (_, first, count), operand, refs in zip(CLASSES, operands, table):
+        value = from_right(operand, *refs)
+        for part in range(count):
             all_ref[first + part] = value[:, LANES * part : LANES * (part + 1)]
-
-    emit(from_right(zero, *table[0:2]), 0)
-    emit(from_right(flip * two, *table[2:4]), 4)
-    both = jnp.concatenate([along * even - across * odd, across * even + along * odd], axis=1)
-    emit(from_right(both, *table[4:6]), 8)
     for index in range(8):
         there = other_chip(device, index)
         keep_ref[index] = all_ref[there]
@@ -238,7 +276,7 @@
 
 def columns(device, blocks, table):
     out = [jax.ShapeDtypeStruct((8, ROWS, LANES), jnp.float32)] * 2
-    specs = [pl.BlockSpec(memory_space=pltpu.SMEM)] + [pl.BlockSpec(memory_space=pltpu.VMEM)] * 10
+    specs = [pl.BlockSpec(memory_space=pltpu.SMEM)] + [pl.BlockSpec(memory_space=pltpu.VMEM)] * 14
     scratch = [pltpu.VMEM((DEV, ROWS, LANES), jnp.float32)]
     return call(columns_kernel, out, scratch, LIMIT[1], 2 * 10**9, specs)(device, *blocks, *table)
 
@@ -256,7 +294,6 @@
 
 
 def to_frequency(device, g_refs, f_refs, part_ref, out_ref):
-    f0h, f0l, f2h, f2l, f1h, f1l = f_refs
     flip_core = jnp.where((device & 4) == 0, 1.0, -1.0)
     flip_chip = jnp.where((device & 8) == 0, 1.0, -1.0)
     for step in range(4):
@@ -268,29 +305,28 @@
         same, other = flip_chip * (near[0] - far[0]), flip_chip * (near[1] - far[1])
         part_ref[2, rows, :] = jnp.where(flip_core > 0, same, other)
         part_ref[3, rows, :] = jnp.where(flip_core > 0, other, same)
-    out_ref[0:INNER, :] = from_left(f0h, f0l, part_ref[0])
-    out_ref[INNER : 2 * INNER, :] = from_left(f2h, f2l, part_ref[1])
-    both = jnp.concatenate([part_ref[2], part_ref[3]], axis=0)
-    out_ref[2 * INNER : 4 * INNER, :] = from_left(f1h, f1l, both)
+    operands = front(*[part_ref[i] for i in range(4)], 0)
+    for (_, first, count), operand, refs in zip(CLASSES, operands, f_refs):
+        out_ref[LANES * first : LANES * (first + count), :] = from_left(*refs, operand)
 
 
 def first_kernel(device_ref, *refs):
-    to_frequency(device_ref[0], refs[:8], refs[8:14], refs[15], refs[14])
+    to_frequency(device_ref[0], refs[:8], pairs(refs[8:18]), refs[19], refs[18])
 
 
 def first_pass(device, g, frequency):
     out = jax.ShapeDtypeStruct((N, LANES), jnp.float32)
-    specs = [pl.BlockSpec(memory_space=pltpu.SMEM)] + [pl.BlockSpec(memory_space=pltpu.VMEM)] * 14
+    specs = [pl.BlockSpec(memory_space=pltpu.SMEM)] + [pl.BlockSpec(memory_space=pltpu.VMEM)] * 18
     scratch = [pltpu.VMEM((4, INNER, LANES), jnp.float32)]
     return call(first_kernel, out, scratch, LIMIT[2], 10**9, specs)(device, *g, *frequency)
 
 
 def rows_kernel(device_ref, one_ref, *refs):
     g_refs, refs = refs[:8], refs[8:]
-    w0h, w0l, w2h, w2l, w1h, w1l = refs[:6]
-    even_ref, odd_ref, last_ref, out_ref, part_ref, two_ref, data_ref = refs[12:]
+    table = pairs(refs[:10])
+    even_ref, odd_ref, last_ref, out_ref, part_ref, two_ref, data_ref = refs[20:]
     device = device_ref[0]
-    to_frequency(device, g_refs, refs[6:12], part_ref, two_ref)
+    to_frequency(device, g_refs, pairs(refs[10:20]), part_ref, two_ref)
     _, weight = lane_frequency(device, (8, LANES))
     total = jnp.zeros((HALF, LANES), jnp.float32)
     special = jnp.zeros((8, LANES), jnp.float32)
@@ -323,12 +359,10 @@
     energy = jnp.sum(total, axis=0, keepdims=True) + jnp.sum(special, axis=0, keepdims=True)
     energy = 0.5 * energy / weight[0:1]
 
-    zero = from_left(w0h, w0l, data_ref[0:INNER, :])
-    two = from_left(w2h, w2l, data_ref[INNER : 2 * INNER, :])
-    odd = from_left(w1h, w1l, data_ref[2 * INNER : 4 * INNER, :])
-    plus, minus = zero + two, zero - two
-    real, turned = odd[0:INNER], odd[INNER : 2 * INNER]
-    for r, value in enumerate((plus + real, minus + turned, plus - real, minus - turned)):
+    values = []
+    for (_, first, count), refs in zip(CLASSES, table):
+        values.append(from_left(*refs, data_ref[LANES * first : LANES * (first + count), :]))
+    for r, value in enumerate(back(values, 0)):
         for part in range(4):
             out_ref[4 * r + part, 0:ROWS, :] = value[ROWS * part : ROWS * (part + 1)]
     for s in range(DEV):
@@ -345,12 +379,13 @@
         pltpu.VMEM((N, LANES), jnp.float32),
         pltpu.VMEM((N, LANES), jnp.float32),
     ]
-    specs = [pl.BlockSpec(memory_space=pltpu.SMEM)] + [pl.BlockSpec(memory_space=pltpu.VMEM)] * 24
+    specs = [pl.BlockSpec(memory_space=pltpu.SMEM)] + [pl.BlockSpec(memory_space=pltpu.VMEM)] * 32
     run = call(rows_kernel, out, scratch, LIMIT[3], 3 * 10**9, specs)
     return run(device, one, *g, *sample, *frequency, *factors)
 
 
-def peaks_kernel(bins_ref, x_ref, f0h, f0l, f2h, f2l, f1h, f1l, offsets_ref, *refs):
+def peaks_kernel(bins_ref, x_ref, *refs):
+    table, offsets_ref, refs = pairs(refs[:10]), refs[10], refs[11:]
     snr_ref, heights_ref, counts_ref, field_ref, wide_ref, pick_ref = refs
 
     def block(first, count):
@@ -358,17 +393,15 @@
         pad = jnp.zeros((8, body.shape[1]), jnp.float32)
         return jnp.concatenate([body, pad], axis=0)
 
-    zero = from_right(block(0, 4), f0h, f0l)
-    two = from_right(block(4, 4), f2h, f2l)
-    odd = from_right(block(8, 8), f1h, f1l)
-    plus, minus = zero + two, zero - two
-    real, turned = odd[:, 0:INNER], odd[:, INNER : 2 * INNER]
+    values = []
+    for (_, first, count), pair in zip(CLASSES, table):
+        values.append(from_right(block(first, count), *pair))
     energy = x_ref[0, ROWS : BLOCK, :]
     for s in range(1, DEV):
         energy = energy + x_ref[s, ROWS : BLOCK, :]
     mean = jnp.sum(energy[2:3, :], axis=1, keepdims=True)
     inverse = 1.0 / jnp.sqrt(mean + 1e-06)
-    for c, value in enumerate((plus + real, minus + turned, plus - real, minus - turned)):
+    for c, value in enumerate(back(values, 1)):
         cols = pl.ds(INNER * c, INNER)
         snr_ref[:, cols] = value[0:ROWS] * inverse
         field_ref[8 : ROWS + 8, cols] = value[0:ROWS]
@@ -430,7 +463,7 @@
         pltpu.VMEM((ROWS + 16, N), f32),
         pltpu.VMEM((16, N), f32),
     ]
-    specs = [pl.BlockSpec(memory_space=pltpu.SMEM)] + [pl.BlockSpec(memory_space=pltpu.VMEM)] * 8
+    specs = [pl.BlockSpec(memory_space=pltpu.SMEM)] + [pl.BlockSpec(memory_space=pltpu.VMEM)] * 12
     run = call(peaks_kernel, out, scratch, LIMIT[4], 2 * 10**9, specs)
     return run(thresholds, x, *table, offsets)
 

time: 105 us -> 103 us (0.981)
  Pallas kernels: 19.4 us -> 14.9 us
  waiting for transfers between devices: 24.3 us -> 28.4 us
  starting transfers between devices: 24.1 us -> 22.6 us
    ppermute x6, waiting for transfers between devices: 11 us -> 14.4 us  [body(): got[4 - step] = lax.ppermute(blocks[4 * field + step], 'col', pairs)]
    pallas_call x1, Pallas kernels: 5.89 us -> 4.45 us  [tables(): call(tables_kernel, out, scratch, LIMIT[0], 10 ** 9, [smem, smem])]
    ppermute x2, starting transfers between devices: 3.69 us -> 2.25 us  [scatter(): got = lax.ppermute(send, group, [(d, d ^ 4) for d in range(DEV)])]
    pallas_call x1, Pallas kernels: 3.76 us -> 2.48 us  [row_pass(): return run(device, one, *g, *sample, *frequency, *factors)]
  transfers between devices with their start and end apart: 22 -> 22, of which waited for: 10 -> 10; matrix products, arithmetic and copies ran while one was open for 0% -> 0% of each run, Pallas kernels for 10% -> 8%
where the time goes in v4:
time: 103 us; the launch traced here: 102 us
  blocking collectives  33 us (32%)
  waiting for transfers between devices  28.4 us (28%)
  starting transfers between devices  22.6 us (22%)
  Pallas kernels  14.9 us (14%)
  local copies, waits for them, and re-layouts  1.6 us (2%)
  between operations  1.41 us (1%)
    all_to_all x2, blocking collectives, exchange(): return lax.all_to_all(x, group, split_axis=0, concat_axis=0, tiled=True)  33 us
    ppermute x6, waiting for transfers between devices, body(): got[4 - step] = lax.ppermute(blocks[4 * field + step], 'col', pairs)  14.4 us
    ppermute x14, waiting for transfers between devices, scatter(): done.append((index, lax.ppermute(blocks[index], group, chip_pairs(index))))  14 us
    ppermute x14, starting transfers between devices, scatter(): done.append((index, lax.ppermute(blocks[index], group, chip_pairs(index))))  12.6 us
    ppermute x6, starting transfers between devices, body(): got[4 - step] = lax.ppermute(blocks[4 * field + step], 'col', pairs)  7.81 us
    pallas_call x1, Pallas kernels, tables(): call(tables_kernel, out, scratch, LIMIT[0], 10 ** 9, [smem, smem])  4.45 us
    pallas_call x1, Pallas kernels, peak_pass(): return run(thresholds, x, *table, offsets)  4.26 us
    pallas_call x1, Pallas kernels, row_pass(): return run(device, one, *g, *sample, *frequency, *factors)  2.48 us
  transfers between devices with their start and end apart: 22, of which 10 were waited for; matrix products, arithmetic and copies ran while one was open for 0% of the time, Pallas kernels for 8%

profile of v4, /device:TPU:1, one launch (start us, length us, event | category | flops | bytes accessed | tf_op | source)
XLA Modules:
  0.0 102.5 jit_solution(7635248852677197416)
XLA Ops:
  0.6 1.6 %copy-done = f32[2,1,512,512]{3,2,1,0:T(8,128)S(1)} copy-done((f32[2,1,512,512]{3,2,1,0:T(8,128)S(1)}, f32[2,1,512,512]{3,2,1,0:T(8,128)}, u32[]{:S(2)}) %copy-start) | copy-done | bytes 2097176
  2.4 3.4 %collective-permute-start = (f32[128,512]{1,0:T(8,128)S(1)}, f32[128,512]{1,0:T(8,128)S(1)}, u32[]{:S(2)}, u32[]{:S(2)}) collective-permute-start(f32[128,512]{1,0:T(8,128)S(1)} %get-tuple-element.58), channel_id=1, source_target_pairs={{0,3},{1,0},{2,1},{3,2},{4,7},{5,4},{6,5},{7,6},{8,11},{9,8},{10,9... | collective-permute-start | bytes 786440 | tf_op jit(solution)/shard_map/ppermute | solution.py:496
  6.9 2.1 %collective-permute-start.11 = (f32[128,512]{1,0:T(8,128)S(1)}, f32[128,512]{1,0:T(8,128)S(1)}, u32[]{:S(2)}, u32[]{:S(2)}) collective-permute-start(f32[128,512]{1,0:T(8,128)S(1)} %get-tuple-element.92), channel_id=1, source_target_pairs={{0,3},{1,0},{2,1},{3,2},{4,7},{5,4},{6,5},{7,6},{8,11},{9,8},{10,9... | collective-permute-start | bytes 786440 | tf_op jit(solution)/shard_map/ppermute | solution.py:496
  8.9 1.2 %collective-permute-start.12 = (f32[128,512]{1,0:T(8,128)S(1)}, f32[128,512]{1,0:T(8,128)S(1)}, u32[]{:S(2)}, u32[]{:S(2)}) collective-permute-start(f32[128,512]{1,0:T(8,128)S(1)} %get-tuple-element.93), channel_id=1, source_target_pairs={{0,2},{1,3},{2,0},{3,1},{4,6},{5,7},{6,4},{7,5},{8,10},{9,11},{10,... | collective-permute-start | bytes 786440 | tf_op jit(solution)/shard_map/ppermute | solution.py:496
  10.8 2.6 %collective-permute-done.refs_1_ = f32[128,512]{1,0:T(8,128)S(1)} collective-permute-done((f32[128,512]{1,0:T(8,128)S(1)}, f32[128,512]{1,0:T(8,128)S(1)}, u32[]{:S(2)}, u32[]{:S(2)}) %collective-permute-start) | collective-permute-done | bytes 262176 | tf_op jit(solution)/shard_map/ppermute | solution.py:496
  13.4 4.4 %shard_map.68 = (bf16[256,256]{1,0:T(8,128)(2,1)S(1)}, bf16[256,256]{1,0:T(8,128)(2,1)S(1)}, bf16[256,256]{1,0:T(8,128)(2,1)S(1)}, bf16[256,256]{1,0:T(8,128)(2,...) custom-call(f32[1]{0:T(128)S(6)} %copy.7.smooth_ref, ...), custom_call_target="tpu_custom_call" | custom-call | flops 1000000000 | bytes 4194304 | tf_op jit(solution)/shard_map/pallas_call | solution.py:225
  17.9 4.5 %collective-permute-done.2.refs_3_ = f32[128,512]{1,0:T(8,128)S(1)} collective-permute-done((f32[128,512]{1,0:T(8,128)S(1)}, f32[128,512]{1,0:T(8,128)S(1)}, u32[]{:S(2)}, u32[]{:S(2)}) %collective-permute-start.2) | collective-permute-done | bytes 262176 | tf_op jit(solution)/shard_map/ppermute | solution.py:496
  23.5 1.4 %collective-permute-start.3 = (f32[8,128,128]{2,1,0:T(8,128)S(1)}, f32[8,128,128]{2,1,0:T(8,128)S(1)}, u32[]{:S(2)}, u32[]{:S(2)}) collective-permute-start(f32[8,128,128]{2,1,0:T(8,128)S(1)} %get-tuple-element.72), channel_id=1, source_target_pairs={{0,4},{1,5},{2,6},{3,7},{4,0},{5,1},{6,2},{7,3},{8,12},{9,13},{10,... | collective-permute-start | bytes 1572872 | tf_op jit(solution)/shard_map/ppermute | solution.py:483
  24.9 2.5 %collective-permute-done.11.refs_1_ = f32[128,512]{1,0:T(8,128)S(1)} collective-permute-done((f32[128,512]{1,0:T(8,128)S(1)}, f32[128,512]{1,0:T(8,128)S(1)}, u32[]{:S(2)}, u32[]{:S(2)}) %collective-permute-start.11) | collective-permute-done | bytes 262176 | tf_op jit(solution)/shard_map/ppermute | solution.py:496
  27.4 4.8 %collective-permute-done.13.refs_3_ = f32[128,512]{1,0:T(8,128)S(1)} collective-permute-done((f32[128,512]{1,0:T(8,128)S(1)}, f32[128,512]{1,0:T(8,128)S(1)}, u32[]{:S(2)}, u32[]{:S(2)}) %collective-permute-start.13) | collective-permute-done | bytes 262176 | tf_op jit(solution)/shard_map/ppermute | solution.py:496
  34.3 1.5 %collective-permute-start.5 = (f32[2,128,128]{2,1,0:T(8,128)S(1)}, f32[2,128,128]{2,1,0:T(8,128)S(1)}, u32[]{:S(2)}, u32[]{:S(2)}) collective-permute-start(f32[2,128,128]{2,1,0:T(8,128)S(1)} %get-tuple-element.75), channel_id=1, source_target_pairs={{0,2},{1,3},{2,0},{3,1},{4,6},{5,7},{6,4},{7,5},{8,10},{9,11},{10,... | collective-permute-start | bytes 393224 | tf_op jit(solution)/shard_map/ppermute | solution.py:487
  37.0 1.3 %collective-permute-start.7 = (f32[2,128,128]{2,1,0:T(8,128)S(1)}, f32[2,128,128]{2,1,0:T(8,128)S(1)}, u32[]{:S(2)}, u32[]{:S(2)}) collective-permute-start(f32[2,128,128]{2,1,0:T(8,128)S(1)} %get-tuple-element.77), channel_id=1, source_target_pairs={{0,8},{1,9},{2,10},{3,11},{4,12},{5,13},{6,14},{7,15},{8,0},{9,1},... | collective-permute-start | bytes 393224 | tf_op jit(solution)/shard_map/ppermute | solution.py:487
  38.8 4.5 %collective-permute-done.4.refs_1_ = f32[2,128,128]{2,1,0:T(8,128)S(1)} collective-permute-done((f32[2,128,128]{2,1,0:T(8,128)S(1)}, f32[2,128,128]{2,1,0:T(8,128)S(1)}, u32[]{:S(2)}, u32[]{:S(2)}) %collective-permute-start.4) | collective-permute-done | bytes 131104 | tf_op jit(solution)/shard_map/ppermute | solution.py:487
  44.3 1.5 %collective-permute-start.15 = (f32[2,128,128]{2,1,0:T(8,128)S(1)}, f32[2,128,128]{2,1,0:T(8,128)S(1)}, u32[]{:S(2)}, u32[]{:S(2)}) collective-permute-start(f32[2,128,128]{2,1,0:T(8,128)S(1)} %get-tuple-element.98), channel_id=1, source_target_pairs={{0,1},{1,2},{2,3},{3,0},{4,5},{5,6},{6,7},{7,4},{8,9},{9,10},{10,1... | collective-permute-start | bytes 393224 | tf_op jit(solution)/shard_map/ppermute | solution.py:487
  45.9 2.9 %collective-permute-start.16 = (f32[2,128,128]{2,1,0:T(8,128)S(1)}, f32[2,128,128]{2,1,0:T(8,128)S(1)}, u32[]{:S(2)}, u32[]{:S(2)}) collective-permute-start(f32[2,128,128]{2,1,0:T(8,128)S(1)} %get-tuple-element.99), channel_id=1, source_target_pairs={{0,2},{1,3},{2,0},{3,1},{4,6},{5,7},{6,4},{7,5},{8,10},{9,11},{10,... | collective-permute-start | bytes 393224 | tf_op jit(solution)/shard_map/ppermute | solution.py:487
  50.3 1.2 %collective-permute-start.18 = (f32[2,128,128]{2,1,0:T(8,128)S(1)}, f32[2,128,128]{2,1,0:T(8,128)S(1)}, u32[]{:S(2)}, u32[]{:S(2)}) collective-permute-start(f32[2,128,128]{2,1,0:T(8,128)S(1)} %get-tuple-element.101), channel_id=1, source_target_pairs={{0,8},{1,9},{2,10},{3,11},{4,12},{5,13},{6,14},{7,15},{8,0},{9,1},... | collective-permute-start | bytes 393224 | tf_op jit(solution)/shard_map/ppermute | solution.py:487
  51.6 3.1 %collective-permute-done.15.refs_1_ = f32[2,128,128]{2,1,0:T(8,128)S(1)} collective-permute-done((f32[2,128,128]{2,1,0:T(8,128)S(1)}, f32[2,128,128]{2,1,0:T(8,128)S(1)}, u32[]{:S(2)}, u32[]{:S(2)}) %collective-permute-start.15) | collective-permute-done | bytes 131104 | tf_op jit(solution)/shard_map/ppermute | solution.py:487
  55.5 1.3 %shard_map.71.one_ref = f32[2048,128]{1,0:T(8,128)S(1)} custom-call(s32[1]{0:T(128)} %bitcast.device_ref, f32[2,128,128]{2,1,0:T(8,128)S(1)} %get-tuple-element.73.refs_0_, f32[2,128,128]{2,1,0:T(8,128)S(1)} %collective-permute-done.4.refs_1_, f32[2,128,128]{2,1,0:T(8,128)S(1)} %collective-permute-done.5.refs_2_, ...), custom_call_target="tpu_custom_call" | custom-call | flops 1000000000 | bytes 4194304 | tf_op jit(solution)/shard_map/pallas_call | solution.py:321
  56.9 2.0 %collective-permute-done.19.refs_5_ = f32[2,128,128]{2,1,0:T(8,128)S(1)} collective-permute-done((f32[2,128,128]{2,1,0:T(8,128)S(1)}, f32[2,128,128]{2,1,0:T(8,128)S(1)}, u32[]{:S(2)}, u32[]{:S(2)}) %collective-permute-start.19) | collective-permute-done | bytes 131104 | tf_op jit(solution)/shard_map/ppermute | solution.py:487
  58.9 3.3 %collective-permute-done.20.refs_6_ = f32[2,128,128]{2,1,0:T(8,128)S(1)} collective-permute-done((f32[2,128,128]{2,1,0:T(8,128)S(1)}, f32[2,128,128]{2,1,0:T(8,128)S(1)}, u32[]{:S(2)}, u32[]{:S(2)}) %collective-permute-start.20) | collective-permute-done | bytes 131104 | tf_op jit(solution)/shard_map/ppermute | solution.py:487
  62.2 2.5 %shard_map.74 = f32[16,136,128]{2,1,0:T(8,128)S(1)} custom-call(s32[1]{0:T(128)} %bitcast.device_ref, f32[2048,128]{1,0:T(8,128)S(1)} %shard_map.71.one_ref, f32[2,128,128]{2,1,0:T(8,128)S(1)} %get-tuple-element.97.refs_0_, f32[2,128,128]{2,1,0:T(8,128)S(1)} %collective-permute-done.15.refs_1_, f32[2,128,128]{2,1,0:T(8,128)S(1)} %collective-permute-done.16.refs_2_, ...), custom_call_target="tpu_custom_call" | custom-call | flops 3000000000 | bytes 4194304 | tf_op jit(solution)/shard_map/pallas_call | solution.py:384
  64.7 24.2 %all_to_all.10.x_ref = f32[16,136,128]{2,1,0:T(8,128)S(1)} all-to-all(f32[16,136,128]{2,1,0:T(8,128)S(1)} %shard_map.74), channel_id=1, replica_groups=mesh['maps'=16,'row'=4,'col'=4] {'row','col'}, dimensions={0} | all-to-all | bytes 2228224 | tf_op jit(solution)/shard_map/all_to_all | solution.py:480
  88.9 4.3 %shard_map.75 = (f32[128,2048]{1,0:T(8,128)}, f32[8,128]{1,0:T(8,128)}, f32[16,8,128]{2,1,0:T(8,128)S(1)}) custom-call(s32[1,16]{1,0:T(1,128)S(1)} %copy-done.2, f32[16,136,128]{2,1,0:T(8,128)S(1)} %all_to_all.10.x_ref, bf16[256,256]{1,0:T(8,128)(2,1)S(1)} %get-tuple-element.81.refs_8_.refs_18_.refs_0_, ...), custom_call_target="tpu_custom_call" | custom-call | flops 2000000000 | bytes 4194304 | tf_op jit(solution)/shard_map/pallas_call | solution.py:468
  93.2 8.8 %all_to_all.11 = f32[16,8,128]{2,1,0:T(8,128)S(1)} all-to-all(f32[16,8,128]{2,1,0:T(8,128)S(1)} %get-tuple-element.110), channel_id=1, replica_groups=mesh['maps'=16,'row'=4,'col'=4] {'row','col'}, dimensions={0} | all-to-all | bytes 131072 | tf_op jit(solution)/shard_map/all_to_all | solution.py:480
  (38 shorter events, 10.0 us)
Async XLA Ops:
  2.4 11.0 %collective-permute-start = (f32[128,512]{1,0:T(8,128)S(1)}, f32[128,512]{1,0:T(8,128)S(1)}, u32[]{:S(2)}, u32[]{:S(2)}) collective-permute-start(f32[128,512]{1,0:T(8,128)S(1)} %get-tuple-element.58), channel_id=1, source_target_pairs={{0,3},{1,0},{2,1},{3,2},{4,7},{5,4},{6,5},{7,6},{8,11},{9,8},{10,9... | collective-permute-start | bytes 786440 | tf_op jit(solution)/shard_map/ppermute | solution.py:496
  5.7 12.1 %collective-permute-start.1 = (f32[128,512]{1,0:T(8,128)S(1)}, f32[128,512]{1,0:T(8,128)S(1)}, u32[]{:S(2)}, u32[]{:S(2)}) collective-permute-start(f32[128,512]{1,0:T(8,128)S(1)} %get-tuple-element.59), channel_id=1, source_target_pairs={{0,2},{1,3},{2,0},{3,1},{4,6},{5,7},{6,4},{7,5},{8,10},{9,11},{10,... | collective-permute-start | bytes 786440 | tf_op jit(solution)/shard_map/ppermute | solution.py:496
  6.3 16.1 %collective-permute-start.2 = (f32[128,512]{1,0:T(8,128)S(1)}, f32[128,512]{1,0:T(8,128)S(1)}, u32[]{:S(2)}, u32[]{:S(2)}) collective-permute-start(f32[128,512]{1,0:T(8,128)S(1)} %get-tuple-element.60), channel_id=1, source_target_pairs={{0,1},{1,2},{2,3},{3,0},{4,5},{5,6},{6,7},{7,4},{8,9},{9,10},{10,1... | collective-permute-start | bytes 786440 | tf_op jit(solution)/shard_map/ppermute | solution.py:496
  6.9 20.6 %collective-permute-start.11 = (f32[128,512]{1,0:T(8,128)S(1)}, f32[128,512]{1,0:T(8,128)S(1)}, u32[]{:S(2)}, u32[]{:S(2)}) collective-permute-start(f32[128,512]{1,0:T(8,128)S(1)} %get-tuple-element.92), channel_id=1, source_target_pairs={{0,3},{1,0},{2,1},{3,2},{4,7},{5,4},{6,5},{7,6},{8,11},{9,8},{10,9... | collective-permute-start | bytes 786440 | tf_op jit(solution)/shard_map/ppermute | solution.py:496
  8.9 18.5 %collective-permute-start.12 = (f32[128,512]{1,0:T(8,128)S(1)}, f32[128,512]{1,0:T(8,128)S(1)}, u32[]{:S(2)}, u32[]{:S(2)}) collective-permute-start(f32[128,512]{1,0:T(8,128)S(1)} %get-tuple-element.93), channel_id=1, source_target_pairs={{0,2},{1,3},{2,0},{3,1},{4,6},{5,7},{6,4},{7,5},{8,10},{9,11},{10,... | collective-permute-start | bytes 786440 | tf_op jit(solution)/shard_map/ppermute | solution.py:496
  13.4 18.9 %collective-permute-start.13 = (f32[128,512]{1,0:T(8,128)S(1)}, f32[128,512]{1,0:T(8,128)S(1)}, u32[]{:S(2)}, u32[]{:S(2)}) collective-permute-start(f32[128,512]{1,0:T(8,128)S(1)} %get-tuple-element.94), channel_id=1, source_target_pairs={{0,1},{1,2},{2,3},{3,0},{4,5},{5,6},{6,7},{7,4},{8,9},{9,10},{10,1... | collective-permute-start | bytes 786440 | tf_op jit(solution)/shard_map/ppermute | solution.py:496
  23.5 10.7 %collective-permute-start.3 = (f32[8,128,128]{2,1,0:T(8,128)S(1)}, f32[8,128,128]{2,1,0:T(8,128)S(1)}, u32[]{:S(2)}, u32[]{:S(2)}) collective-permute-start(f32[8,128,128]{2,1,0:T(8,128)S(1)} %get-tuple-element.72), channel_id=1, source_target_pairs={{0,4},{1,5},{2,6},{3,7},{4,0},{5,1},{6,2},{7,3},{8,12},{9,13},{10,... | collective-permute-start | bytes 1572872 | tf_op jit(solution)/shard_map/ppermute | solution.py:483
  33.4 4.9 %collective-permute-start.14 = (f32[8,128,128]{2,1,0:T(8,128)S(1)}, f32[8,128,128]{2,1,0:T(8,128)S(1)}, u32[]{:S(2)}, u32[]{:S(2)}) collective-permute-start(f32[8,128,128]{2,1,0:T(8,128)S(1)} %get-tuple-element.96), channel_id=1, source_target_pairs={{0,4},{1,5},{2,6},{3,7},{4,0},{5,1},{6,2},{7,3},{8,12},{9,13},{10,... | collective-permute-start | bytes 1572872 | tf_op jit(solution)/shard_map/ppermute | solution.py:483
  34.3 9.1 %collective-permute-start.4 = (f32[2,128,128]{2,1,0:T(8,128)S(1)}, f32[2,128,128]{2,1,0:T(8,128)S(1)}, u32[]{:S(2)}, u32[]{:S(2)}) collective-permute-start(f32[2,128,128]{2,1,0:T(8,128)S(1)} %get-tuple-element.74), channel_id=1, source_target_pairs={{0,1},{1,2},{2,3},{3,0},{4,5},{5,6},{6,7},{7,4},{8,9},{9,10},{10,1... | collective-permute-start | bytes 393224 | tf_op jit(solution)/shard_map/ppermute | solution.py:487
  34.3 9.0 %collective-permute-start.5 = (f32[2,128,128]{2,1,0:T(8,128)S(1)}, f32[2,128,128]{2,1,0:T(8,128)S(1)}, u32[]{:S(2)}, u32[]{:S(2)}) collective-permute-start(f32[2,128,128]{2,1,0:T(8,128)S(1)} %get-tuple-element.75), channel_id=1, source_target_pairs={{0,2},{1,3},{2,0},{3,1},{4,6},{5,7},{6,4},{7,5},{8,10},{9,11},{10,... | collective-permute-start | bytes 393224 | tf_op jit(solution)/shard_map/ppermute | solution.py:487
  35.9 8.4 %collective-permute-start.6 = (f32[2,128,128]{2,1,0:T(8,128)S(1)}, f32[2,128,128]{2,1,0:T(8,128)S(1)}, u32[]{:S(2)}, u32[]{:S(2)}) collective-permute-start(f32[2,128,128]{2,1,0:T(8,128)S(1)} %get-tuple-element.76), channel_id=1, source_target_pairs={{0,3},{1,0},{2,1},{3,2},{4,7},{5,4},{6,5},{7,6},{8,11},{9,8},{10,9... | collective-permute-start | bytes 393224 | tf_op jit(solution)/shard_map/ppermute | solution.py:487
  37.0 8.9 %collective-permute-start.7 = (f32[2,128,128]{2,1,0:T(8,128)S(1)}, f32[2,128,128]{2,1,0:T(8,128)S(1)}, u32[]{:S(2)}, u32[]{:S(2)}) collective-permute-start(f32[2,128,128]{2,1,0:T(8,128)S(1)} %get-tuple-element.77), channel_id=1, source_target_pairs={{0,8},{1,9},{2,10},{3,11},{4,12},{5,13},{6,14},{7,15},{8,0},{9,1},... | collective-permute-start | bytes 393224 | tf_op jit(solution)/shard_map/ppermute | solution.py:487
  38.3 10.4 %collective-permute-start.8 = (f32[2,128,128]{2,1,0:T(8,128)S(1)}, f32[2,128,128]{2,1,0:T(8,128)S(1)}, u32[]{:S(2)}, u32[]{:S(2)}) collective-permute-start(f32[2,128,128]{2,1,0:T(8,128)S(1)} %get-tuple-element.78), channel_id=1, source_target_pairs={{0,9},{1,10},{2,11},{3,8},{4,13},{5,14},{6,15},{7,12},{8,1},{9,2},... | collective-permute-start | bytes 393224 | tf_op jit(solution)/shard_map/ppermute | solution.py:487
  43.4 6.9 %collective-permute-start.9 = (f32[2,128,128]{2,1,0:T(8,128)S(1)}, f32[2,128,128]{2,1,0:T(8,128)S(1)}, u32[]{:S(2)}, u32[]{:S(2)}) collective-permute-start(f32[2,128,128]{2,1,0:T(8,128)S(1)} %get-tuple-element.79), channel_id=1, source_target_pairs={{0,10},{1,11},{2,8},{3,9},{4,14},{5,15},{6,12},{7,13},{8,2},{9,3},... | collective-permute-start | bytes 393224 | tf_op jit(solution)/shard_map/ppermute | solution.py:487
  43.4 8.2 %collective-permute-start.10 = (f32[2,128,128]{2,1,0:T(8,128)S(1)}, f32[2,128,128]{2,1,0:T(8,128)S(1)}, u32[]{:S(2)}, u32[]{:S(2)}) collective-permute-start(f32[2,128,128]{2,1,0:T(8,128)S(1)} %get-tuple-element.80), channel_id=1, source_target_pairs={{0,11},{1,8},{2,9},{3,10},{4,15},{5,12},{6,13},{7,14},{8,3},{9,0},... | collective-permute-start | bytes 393224 | tf_op jit(solution)/shard_map/ppermute | solution.py:487
  44.3 10.4 %collective-permute-start.15 = (f32[2,128,128]{2,1,0:T(8,128)S(1)}, f32[2,128,128]{2,1,0:T(8,128)S(1)}, u32[]{:S(2)}, u32[]{:S(2)}) collective-permute-start(f32[2,128,128]{2,1,0:T(8,128)S(1)} %get-tuple-element.98), channel_id=1, source_target_pairs={{0,1},{1,2},{2,3},{3,0},{4,5},{5,6},{6,7},{7,4},{8,9},{9,10},{10,1... | collective-permute-start | bytes 393224 | tf_op jit(solution)/shard_map/ppermute | solution.py:487
  45.9 9.0 %collective-permute-start.16 = (f32[2,128,128]{2,1,0:T(8,128)S(1)}, f32[2,128,128]{2,1,0:T(8,128)S(1)}, u32[]{:S(2)}, u32[]{:S(2)}) collective-permute-start(f32[2,128,128]{2,1,0:T(8,128)S(1)} %get-tuple-element.99), channel_id=1, source_target_pairs={{0,2},{1,3},{2,0},{3,1},{4,6},{5,7},{6,4},{7,5},{8,10},{9,11},{10,... | collective-permute-start | bytes 393224 | tf_op jit(solution)/shard_map/ppermute | solution.py:487
  48.7 8.1 %collective-permute-start.17 = (f32[2,128,128]{2,1,0:T(8,128)S(1)}, f32[2,128,128]{2,1,0:T(8,128)S(1)}, u32[]{:S(2)}, u32[]{:S(2)}) collective-permute-start(f32[2,128,128]{2,1,0:T(8,128)S(1)} %get-tuple-element.100), channel_id=1, source_target_pairs={{0,3},{1,0},{2,1},{3,2},{4,7},{5,4},{6,5},{7,6},{8,11},{9,8},{10,9... | collective-permute-start | bytes 393224 | tf_op jit(solution)/shard_map/ppermute | solution.py:487
  50.3 6.5 %collective-permute-start.18 = (f32[2,128,128]{2,1,0:T(8,128)S(1)}, f32[2,128,128]{2,1,0:T(8,128)S(1)}, u32[]{:S(2)}, u32[]{:S(2)}) collective-permute-start(f32[2,128,128]{2,1,0:T(8,128)S(1)} %get-tuple-element.101), channel_id=1, source_target_pairs={{0,8},{1,9},{2,10},{3,11},{4,12},{5,13},{6,14},{7,15},{8,0},{9,1},... | collective-permute-start | bytes 393224 | tf_op jit(solution)/shard_map/ppermute | solution.py:487
  51.6 7.3 %collective-permute-start.19 = (f32[2,128,128]{2,1,0:T(8,128)S(1)}, f32[2,128,128]{2,1,0:T(8,128)S(1)}, u32[]{:S(2)}, u32[]{:S(2)}) collective-permute-start(f32[2,128,128]{2,1,0:T(8,128)S(1)} %get-tuple-element.102), channel_id=1, source_target_pairs={{0,9},{1,10},{2,11},{3,8},{4,13},{5,14},{6,15},{7,12},{8,1},{9,2},... | collective-permute-start | bytes 393224 | tf_op jit(solution)/shard_map/ppermute | solution.py:487
  54.7 7.5 %collective-permute-start.20 = (f32[2,128,128]{2,1,0:T(8,128)S(1)}, f32[2,128,128]{2,1,0:T(8,128)S(1)}, u32[]{:S(2)}, u32[]{:S(2)}) collective-permute-start(f32[2,128,128]{2,1,0:T(8,128)S(1)} %get-tuple-element.103), channel_id=1, source_target_pairs={{0,10},{1,11},{2,8},{3,9},{4,14},{5,15},{6,12},{7,13},{8,2},{9,3},... | collective-permute-start | bytes 393224 | tf_op jit(solution)/shard_map/ppermute | solution.py:487
  54.9 7.3 %collective-permute-start.21 = (f32[2,128,128]{2,1,0:T(8,128)S(1)}, f32[2,128,128]{2,1,0:T(8,128)S(1)}, u32[]{:S(2)}, u32[]{:S(2)}) collective-permute-start(f32[2,128,128]{2,1,0:T(8,128)S(1)} %get-tuple-element.104), channel_id=1, source_target_pairs={{0,11},{1,8},{2,9},{3,10},{4,15},{5,12},{6,13},{7,14},{8,3},{9,0},... | collective-permute-start | bytes 393224 | tf_op jit(solution)/shard_map/ppermute | solution.py:487
  64.7 24.2 %copy-start.1 = (s32[1,8,128]{2,1,0:T(8,128)S(1)}, s32[1,8,128]{2,1,0:T(8,128)}, u32[]{:S(2)}) copy-start(s32[1,8,128]{2,1,0:T(8,128)} %param.6) | copy-start | bytes 12292
  64.7 24.2 %copy-start.2 = (s32[1,16]{1,0:T(1,128)S(1)}, s32[1,16]{1,0:T(1,128)}, u32[]{:S(2)}) copy-start(s32[1,16]{1,0:T(1,128)} %bins_ref.1) | copy-start | bytes 196
  (1 other events, 1.6 us)

commit v5 on v4

--- a/solution.py
+++ b/solution.py
@@ -21,8 +21,8 @@
 CLASSES = ((0, 0, 2), (4, 2, 2), (2, 4, 4), (1, 8, 4), (3, 12, 4))
 ROOT = math.sqrt(0.5)
 MIB = 1 << 20
-LIMIT = (20, 24, 24, 36, 28)
-ORDER = (6, 2, 5, 7, 1, 3, 4)
+LIMIT = (20, 24, 24, 36, 32)
+ORDER = (6, 5, 7, 4, 2, 1, 3)
 
 
 def call(kernel, out, scratch, limit, flops, ins):
@@ -324,7 +324,7 @@
 def rows_kernel(device_ref, one_ref, *refs):
     g_refs, refs = refs[:8], refs[8:]
     table = pairs(refs[:10])
-    even_ref, odd_ref, last_ref, out_ref, part_ref, two_ref, data_ref = refs[20:]
+    even_ref, odd_ref, last_ref, keep_ref, send_ref, part_ref, two_ref, data_ref, out_ref = refs[20:]
     device = device_ref[0]
     to_frequency(device, g_refs, pairs(refs[10:20]), part_ref, two_ref)
     _, weight = lane_frequency(device, (8, LANES))
@@ -370,23 +370,32 @@
         out_ref[s, ROWS + 1 : ROWS + 2, :] = out_ref[(s + 1) % DEV, 0:1, :]
         out_ref[s, ROWS + 2 : ROWS + 3, :] = energy
         out_ref[s, ROWS + 3 : BLOCK, :] = jnp.zeros((BLOCK - ROWS - 3, LANES), jnp.float32)
+    for index in range(8):
+        there = other_chip(device, index)
+        keep_ref[index] = out_ref[there]
+        send_ref[index] = out_ref[there ^ 4]
 
 
 def row_pass(device, one, g, sample, frequency, factors):
-    out = jax.ShapeDtypeStruct((DEV, BLOCK, LANES), jnp.float32)
+    out = [jax.ShapeDtypeStruct((8, BLOCK, LANES), jnp.float32)] * 2
     scratch = [
         pltpu.VMEM((4, INNER, LANES), jnp.float32),
         pltpu.VMEM((N, LANES), jnp.float32),
         pltpu.VMEM((N, LANES), jnp.float32),
+        pltpu.VMEM((DEV, BLOCK, LANES), jnp.float32),
     ]
     specs = [pl.BlockSpec(memory_space=pltpu.SMEM)] + [pl.BlockSpec(memory_space=pltpu.VMEM)] * 32
     run = call(rows_kernel, out, scratch, LIMIT[3], 3 * 10**9, specs)
     return run(device, one, *g, *sample, *frequency, *factors)
 
 
-def peaks_kernel(bins_ref, x_ref, *refs):
-    table, offsets_ref, refs = pairs(refs[:10]), refs[10], refs[11:]
-    snr_ref, heights_ref, counts_ref, field_ref, wide_ref, pick_ref = refs
+def peaks_kernel(bins_ref, device_ref, *refs):
+    got, table, offsets_ref, refs = refs[:8], pairs(refs[8:18]), refs[18], refs[19:]
+    snr_ref, heights_ref, counts_ref, field_ref, wide_ref, side_ref, pick_ref, x_ref = refs
+    for index in range(8):
+        there = other_chip(device_ref[0], (index & 4) | (-index & 3))
+        x_ref[there] = got[index][0]
+        x_ref[there ^ 4] = got[index][1]
 
     def block(first, count):
         body = jnp.concatenate([x_ref[s] for s in range(first, first + count)], axis=1)
@@ -412,6 +421,7 @@
         value = field_ref[start : start + size, :]
         side = jnp.maximum(pltpu.roll(value, 1, 1), pltpu.roll(value, N - 1, 1))
         wide_ref[start : start + size, :] = jnp.maximum(side, value)
+        side_ref[start : start + size, :] = side
     blocks = iota((LANES, N), 1) // CELL == iota((LANES, N), 0)
     blocks = jnp.where(blocks, 1.0, 0.0).astype(jnp.bfloat16)
     offsets = offsets_ref[...].astype(jnp.float32).astype(jnp.bfloat16)
@@ -420,8 +430,7 @@
     code = (iota((CELL, N), 0) * CELL + (iota((CELL, N), 1) & (CELL - 1))).astype(jnp.float32)
     for p in range(ROWS // CELL):
         base = 8 + CELL * p
-        value = field_ref[base : base + CELL, :]
-        side = jnp.maximum(pltpu.roll(value, 1, 1), pltpu.roll(value, N - 1, 1))
+        value, side = field_ref[base : base + CELL, :], side_ref[base : base + CELL, :]
         above = wide_ref[base - 1 : base - 1 + CELL, :]
         below = wide_ref[base + 1 : base + 1 + CELL, :]
         nearest = jnp.maximum(side, jnp.maximum(above, below))
@@ -451,7 +460,7 @@
         counts_ref[s] = jnp.broadcast_to(counts, (8, LANES))
 
 
-def peak_pass(thresholds, x, table, offsets):
+def peak_pass(thresholds, device, x, table, offsets):
     f32 = jnp.float32
     out = [
         jax.ShapeDtypeStruct((ROWS, N), f32),
@@ -461,11 +470,13 @@
     scratch = [
         pltpu.VMEM((ROWS + 16, N), f32),
         pltpu.VMEM((ROWS + 16, N), f32),
+        pltpu.VMEM((ROWS + 16, N), f32),
         pltpu.VMEM((16, N), f32),
+        pltpu.VMEM((DEV, BLOCK, LANES), f32),
     ]
-    specs = [pl.BlockSpec(memory_space=pltpu.SMEM)] + [pl.BlockSpec(memory_space=pltpu.VMEM)] * 12
+    specs = [pl.BlockSpec(memory_space=pltpu.SMEM)] * 2 + [pl.BlockSpec(memory_space=pltpu.VMEM)] * 19
     run = call(peaks_kernel, out, scratch, LIMIT[4], 2 * 10**9, specs)
-    return run(thresholds, x, *table, offsets)
+    return run(thresholds, device, *x, *table, offsets)
 
 
 def chip_pairs(index):
@@ -502,7 +513,7 @@
     two = scatter(*g)
     one = first_pass(device, one, frequency)
     k = row_pass(device, one, two, sample, frequency, factors)
-    out = peak_pass(thresholds, exchange(k), frequency, offsets[0])
+    out = peak_pass(thresholds, device, scatter(*k), frequency, offsets[0])
     snr, heights, counts = out
     counts = exchange(counts)
     return snr[None], heights[None], jnp.sum(counts[:, 0:1, 0:16], axis=0)

time: 103 us -> 105 us (1.019)
  blocking collectives: 33 us -> 12.5 us
  waiting for transfers between devices: 28.4 us -> 41.3 us
  starting transfers between devices: 22.6 us -> 32.1 us
    all_to_all x2 -> x1, blocking collectives: 33 us -> 12.5 us  [exchange(): return lax.all_to_all(x, group, split_axis=0, concat_axis=0, tiled=True)]
    ppermute x14 -> x21, waiting for transfers between devices: 14 us -> 25.3 us  [scatter(): done.append((index, lax.ppermute(blocks[index], group, chip_pairs(index))))]
    ppermute x2 -> x3, starting transfers between devices: 2.25 us -> 7.12 us  [scatter(): got = lax.ppermute(send, group, [(d, d ^ 4) for d in range(DEV)])]
    ppermute x14 -> x21, starting transfers between devices: 12.6 us -> 17.2 us  [scatter(): done.append((index, lax.ppermute(blocks[index], group, chip_pairs(index))))]
    ppermute x2 -> x3, waiting for transfers between devices: 0.01 us -> 1.59 us  [scatter(): got = lax.ppermute(send, group, [(d, d ^ 4) for d in range(DEV)])]
  transfers between devices with their start and end apart: 22 -> 30, of which waited for: 10 -> 15; matrix products, arithmetic and copies ran while one was open for 0% -> 0% of each run, Pallas kernels for 8% -> 8%
where the time goes in v5:
time: 105 us
  waiting for transfers between devices  41.3 us (39%)
  starting transfers between devices  32.1 us (31%)
  Pallas kernels  15.1 us (14%)
  blocking collectives  12.5 us (12%)
  local copies, waits for them, and re-layouts  1.59 us (2%)
  between operations  1.42 us (1%)
    ppermute x21, waiting for transfers between devices, scatter(): done.append((index, lax.ppermute(blocks[index], group, chip_pairs(index))))  25.3 us
    ppermute x21, starting transfers between devices, scatter(): done.append((index, lax.ppermute(blocks[index], group, chip_pairs(index))))  17.2 us
    ppermute x6, waiting for transfers between devices, body(): got[4 - step] = lax.ppermute(blocks[4 * field + step], 'col', pairs)  14.4 us
    all_to_all x1, blocking collectives, exchange(): return lax.all_to_all(x, group, split_axis=0, concat_axis=0, tiled=True)  12.5 us
    ppermute x6, starting transfers between devices, body(): got[4 - step] = lax.ppermute(blocks[4 * field + step], 'col', pairs)  7.81 us
    ppermute x3, starting transfers between devices, scatter(): got = lax.ppermute(send, group, [(d, d ^ 4) for d in range(DEV)])  7.12 us
    pallas_call x1, Pallas kernels, tables(): call(tables_kernel, out, scratch, LIMIT[0], 10 ** 9, [smem, smem])  4.45 us
    pallas_call x1, Pallas kernels, peak_pass(): return run(thresholds, device, *x, *table, offsets)  4.26 us
  transfers between devices with their start and end apart: 30, of which 15 were waited for; matrix products, arithmetic and copies ran while one was open for 0% of the time, Pallas kernels for 8%

profile of v5, /device:TPU:1, one launch (start us, length us, event | category | flops | bytes accessed | tf_op | source)
XLA Modules:
  0.0 104.5 jit_solution(6869835282409110770)
XLA Ops:
  0.6 1.6 %copy-done = f32[2,1,512,512]{3,2,1,0:T(8,128)S(1)} copy-done((f32[2,1,512,512]{3,2,1,0:T(8,128)S(1)}, f32[2,1,512,512]{3,2,1,0:T(8,128)}, u32[]{:S(2)}) %copy-start) | copy-done | bytes 2097176
  2.4 3.4 %collective-permute-start = (f32[128,512]{1,0:T(8,128)S(1)}, f32[128,512]{1,0:T(8,128)S(1)}, u32[]{:S(2)}, u32[]{:S(2)}) collective-permute-start(f32[128,512]{1,0:T(8,128)S(1)} %get-tuple-element.68), channel_id=1, source_target_pairs={{0,3},{1,0},{2,1},{3,2},{4,7},{5,4},{6,5},{7,6},{8,11},{9,8},{10,9... | collective-permute-start | bytes 786440 | tf_op jit(solution)/shard_map/ppermute | solution.py:507
  6.9 2.1 %collective-permute-start.11 = (f32[128,512]{1,0:T(8,128)S(1)}, f32[128,512]{1,0:T(8,128)S(1)}, u32[]{:S(2)}, u32[]{:S(2)}) collective-permute-start(f32[128,512]{1,0:T(8,128)S(1)} %get-tuple-element.102), channel_id=1, source_target_pairs={{0,3},{1,0},{2,1},{3,2},{4,7},{5,4},{6,5},{7,6},{8,11},{9,8},{10,9... | collective-permute-start | bytes 786440 | tf_op jit(solution)/shard_map/ppermute | solution.py:507
  10.8 2.6 %collective-permute-done.refs_1_ = f32[128,512]{1,0:T(8,128)S(1)} collective-permute-done((f32[128,512]{1,0:T(8,128)S(1)}, f32[128,512]{1,0:T(8,128)S(1)}, u32[]{:S(2)}, u32[]{:S(2)}) %collective-permute-start) | collective-permute-done | bytes 262176 | tf_op jit(solution)/shard_map/ppermute | solution.py:507
  13.4 4.4 %shard_map.68 = (bf16[256,256]{1,0:T(8,128)(2,1)S(1)}, bf16[256,256]{1,0:T(8,128)(2,1)S(1)}, bf16[256,256]{1,0:T(8,128)(2,1)S(1)}, bf16[256,256]{1,0:T(8,128)(2,...) custom-call(f32[1]{0:T(128)S(6)} %copy.7.smooth_ref, ...), custom_call_target="tpu_custom_call" | custom-call | flops 1000000000 | bytes 4194304 | tf_op jit(solution)/shard_map/pallas_call | solution.py:225
  17.9 4.5 %collective-permute-done.2.refs_3_ = f32[128,512]{1,0:T(8,128)S(1)} collective-permute-done((f32[128,512]{1,0:T(8,128)S(1)}, f32[128,512]{1,0:T(8,128)S(1)}, u32[]{:S(2)}, u32[]{:S(2)}) %collective-permute-start.2) | collective-permute-done | bytes 262176 | tf_op jit(solution)/shard_map/ppermute | solution.py:507
  24.9 2.5 %collective-permute-done.11.refs_1_ = f32[128,512]{1,0:T(8,128)S(1)} collective-permute-done((f32[128,512]{1,0:T(8,128)S(1)}, f32[128,512]{1,0:T(8,128)S(1)}, u32[]{:S(2)}, u32[]{:S(2)}) %collective-permute-start.11) | collective-permute-done | bytes 262176 | tf_op jit(solution)/shard_map/ppermute | solution.py:507
  27.4 4.8 %collective-permute-done.13.refs_3_ = f32[128,512]{1,0:T(8,128)S(1)} collective-permute-done((f32[128,512]{1,0:T(8,128)S(1)}, f32[128,512]{1,0:T(8,128)S(1)}, u32[]{:S(2)}, u32[]{:S(2)}) %collective-permute-start.13) | collective-permute-done | bytes 262176 | tf_op jit(solution)/shard_map/ppermute | solution.py:507
  34.3 1.5 %collective-permute-start.5 = (f32[2,128,128]{2,1,0:T(8,128)S(1)}, f32[2,128,128]{2,1,0:T(8,128)S(1)}, u32[]{:S(2)}, u32[]{:S(2)}) collective-permute-start(f32[2,128,128]{2,1,0:T(8,128)S(1)} %get-tuple-element.85), channel_id=1, source_target_pairs={{0,2},{1,3},{2,0},{3,1},{4,6},{5,7},{6,4},{7,5},{8,10},{9,11},{10,... | collective-permute-start | bytes 393224 | tf_op jit(solution)/shard_map/ppermute | solution.py:498
  38.9 4.5 %collective-permute-done.4.refs_1_ = f32[2,128,128]{2,1,0:T(8,128)S(1)} collective-permute-done((f32[2,128,128]{2,1,0:T(8,128)S(1)}, f32[2,128,128]{2,1,0:T(8,128)S(1)}, u32[]{:S(2)}, u32[]{:S(2)}) %collective-permute-start.4) | collective-permute-done | bytes 131104 | tf_op jit(solution)/shard_map/ppermute | solution.py:498
  44.3 1.5 %collective-permute-start.15 = (f32[2,128,128]{2,1,0:T(8,128)S(1)}, f32[2,128,128]{2,1,0:T(8,128)S(1)}, u32[]{:S(2)}, u32[]{:S(2)}) collective-permute-start(f32[2,128,128]{2,1,0:T(8,128)S(1)} %get-tuple-element.108), channel_id=1, source_target_pairs={{0,1},{1,2},{2,3},{3,0},{4,5},{5,6},{6,7},{7,4},{8,9},{9,10},{10,1... | collective-permute-start | bytes 393224 | tf_op jit(solution)/shard_map/ppermute | solution.py:498
  45.9 2.9 %collective-permute-start.16 = (f32[2,128,128]{2,1,0:T(8,128)S(1)}, f32[2,128,128]{2,1,0:T(8,128)S(1)}, u32[]{:S(2)}, u32[]{:S(2)}) collective-permute-start(f32[2,128,128]{2,1,0:T(8,128)S(1)} %get-tuple-element.109), channel_id=1, source_target_pairs={{0,2},{1,3},{2,0},{3,1},{4,6},{5,7},{6,4},{7,5},{8,10},{9,11},{10,... | collective-permute-start | bytes 393224 | tf_op jit(solution)/shard_map/ppermute | solution.py:498
  51.6 3.1 %collective-permute-done.15.refs_1_ = f32[2,128,128]{2,1,0:T(8,128)S(1)} collective-permute-done((f32[2,128,128]{2,1,0:T(8,128)S(1)}, f32[2,128,128]{2,1,0:T(8,128)S(1)}, u32[]{:S(2)}, u32[]{:S(2)}) %collective-permute-start.15) | collective-permute-done | bytes 131104 | tf_op jit(solution)/shard_map/ppermute | solution.py:498
  56.9 2.0 %collective-permute-done.19.refs_5_ = f32[2,128,128]{2,1,0:T(8,128)S(1)} collective-permute-done((f32[2,128,128]{2,1,0:T(8,128)S(1)}, f32[2,128,128]{2,1,0:T(8,128)S(1)}, u32[]{:S(2)}, u32[]{:S(2)}) %collective-permute-start.19) | collective-permute-done | bytes 131104 | tf_op jit(solution)/shard_map/ppermute | solution.py:498
  58.9 3.3 %collective-permute-done.20.refs_6_ = f32[2,128,128]{2,1,0:T(8,128)S(1)} collective-permute-done((f32[2,128,128]{2,1,0:T(8,128)S(1)}, f32[2,128,128]{2,1,0:T(8,128)S(1)}, u32[]{:S(2)}, u32[]{:S(2)}) %collective-permute-start.20) | collective-permute-done | bytes 131104 | tf_op jit(solution)/shard_map/ppermute | solution.py:498
  62.2 2.6 %shard_map.74 = (f32[8,136,128]{2,1,0:T(8,128)S(1)}, f32[8,136,128]{2,1,0:T(8,128)S(1)}) custom-call(s32[1]{0:T(128)} %bitcast.device_ref, f32[2048,128]{1,0:T(8,128)S(1)} %shard_map.71.one_ref, f32[2,128,128]{2,1,0:T(8,128)S(1)} %get-tuple-element.107.refs_0_, f32[2,128,128]{2,1,0:T(8,128)S(1)} %collective-permute-done.15.refs_1_, ...), custom_call_target="tpu_custom_call" | custom-call | flops 3000000000 | bytes 4194304 | tf_op jit(solution)/shard_map/pallas_call | solution.py:389
  64.8 4.9 %collective-permute-start.22 = (f32[8,136,128]{2,1,0:T(8,128)S(1)}, f32[8,136,128]{2,1,0:T(8,128)S(1)}, u32[]{:S(2)}, u32[]{:S(2)}) collective-permute-start(f32[8,136,128]{2,1,0:T(8,128)S(1)} %get-tuple-element.119), channel_id=1, source_target_pairs={{0,4},{1,5},{2,6},{3,7},{4,0},{5,1},{6,2},{7,3},{8,12},{9,13},{10,... | collective-permute-start | bytes 1671176 | tf_op jit(solution)/shard_map/ppermute | solution.py:494
  69.7 1.6 %collective-permute-done.22.got_ref = f32[8,136,128]{2,1,0:T(8,128)S(1)} collective-permute-done((f32[8,136,128]{2,1,0:T(8,128)S(1)}, f32[8,136,128]{2,1,0:T(8,128)S(1)}, u32[]{:S(2)}, u32[]{:S(2)}) %collective-permute-start.22) | collective-permute-done | bytes 557088 | tf_op jit(solution)/shard_map/ppermute | solution.py:494
  72.5 1.5 %collective-permute-start.25 = (f32[2,136,128]{2,1,0:T(8,128)S(1)}, f32[2,136,128]{2,1,0:T(8,128)S(1)}, u32[]{:S(2)}, u32[]{:S(2)}) collective-permute-start(f32[2,136,128]{2,1,0:T(8,128)S(1)} %get-tuple-element.123), channel_id=1, source_target_pairs={{0,3},{1,0},{2,1},{3,2},{4,7},{5,4},{6,5},{7,6},{8,11},{9,8},{10,9... | collective-permute-start | bytes 417800 | tf_op jit(solution)/shard_map/ppermute | solution.py:498
  75.8 4.6 %collective-permute-done.23.refs_1_ = f32[2,136,128]{2,1,0:T(8,128)S(1)} collective-permute-done((f32[2,136,128]{2,1,0:T(8,128)S(1)}, f32[2,136,128]{2,1,0:T(8,128)S(1)}, u32[]{:S(2)}, u32[]{:S(2)}) %collective-permute-start.23) | collective-permute-done | bytes 139296 | tf_op jit(solution)/shard_map/ppermute | solution.py:498
  80.8 3.0 %collective-permute-done.27.refs_5_ = f32[2,136,128]{2,1,0:T(8,128)S(1)} collective-permute-done((f32[2,136,128]{2,1,0:T(8,128)S(1)}, f32[2,136,128]{2,1,0:T(8,128)S(1)}, u32[]{:S(2)}, u32[]{:S(2)}) %collective-permute-start.27) | collective-permute-done | bytes 139296 | tf_op jit(solution)/shard_map/ppermute | solution.py:498
  83.9 3.4 %collective-permute-done.28.refs_6_ = f32[2,136,128]{2,1,0:T(8,128)S(1)} collective-permute-done((f32[2,136,128]{2,1,0:T(8,128)S(1)}, f32[2,136,128]{2,1,0:T(8,128)S(1)}, u32[]{:S(2)}, u32[]{:S(2)}) %collective-permute-start.28) | collective-permute-done | bytes 139296 | tf_op jit(solution)/shard_map/ppermute | solution.py:498
  87.3 4.3 %shard_map.76 = (f32[128,2048]{1,0:T(8,128)}, f32[8,128]{1,0:T(8,128)}, f32[16,8,128]{2,1,0:T(8,128)S(1)}) custom-call(s32[1,16]{1,0:T(1,128)S(1)} %copy-done.2, s32[1]{0:T(128)} %bitcast.device_ref, f32[2,136,128]{2,1,0:T(8,128)S(1)} %get-tuple-element.120.refs_0_, f32[2,136,128]{2,1,0:T(8,128)S(1)} %collective-permute-done.23.refs_1_, ...), custom_call_target="tpu_custom_call" | custom-call | flops 2000000000 | bytes 4194304 | tf_op jit(solution)/shard_map/pallas_call | solution.py:479
  91.5 12.5 %all_to_all.5 = f32[16,8,128]{2,1,0:T(8,128)S(1)} all-to-all(f32[16,8,128]{2,1,0:T(8,128)S(1)} %get-tuple-element.130), channel_id=1, replica_groups=mesh['maps'=16,'row'=4,'col'=4] {'row','col'}, dimensions={0} | all-to-all | bytes 131072 | tf_op jit(solution)/shard_map/all_to_all | solution.py:491
  (54 shorter events, 19.9 us)
Async XLA Ops:
  2.4 11.0 %collective-permute-start = (f32[128,512]{1,0:T(8,128)S(1)}, f32[128,512]{1,0:T(8,128)S(1)}, u32[]{:S(2)}, u32[]{:S(2)}) collective-permute-start(f32[128,512]{1,0:T(8,128)S(1)} %get-tuple-element.68), channel_id=1, source_target_pairs={{0,3},{1,0},{2,1},{3,2},{4,7},{5,4},{6,5},{7,6},{8,11},{9,8},{10,9... | collective-permute-start | bytes 786440 | tf_op jit(solution)/shard_map/ppermute | solution.py:507
  5.7 12.1 %collective-permute-start.1 = (f32[128,512]{1,0:T(8,128)S(1)}, f32[128,512]{1,0:T(8,128)S(1)}, u32[]{:S(2)}, u32[]{:S(2)}) collective-permute-start(f32[128,512]{1,0:T(8,128)S(1)} %get-tuple-element.69), channel_id=1, source_target_pairs={{0,2},{1,3},{2,0},{3,1},{4,6},{5,7},{6,4},{7,5},{8,10},{9,11},{10,... | collective-permute-start | bytes 786440 | tf_op jit(solution)/shard_map/ppermute | solution.py:507
  6.3 16.1 %collective-permute-start.2 = (f32[128,512]{1,0:T(8,128)S(1)}, f32[128,512]{1,0:T(8,128)S(1)}, u32[]{:S(2)}, u32[]{:S(2)}) collective-permute-start(f32[128,512]{1,0:T(8,128)S(1)} %get-tuple-element.70), channel_id=1, source_target_pairs={{0,1},{1,2},{2,3},{3,0},{4,5},{5,6},{6,7},{7,4},{8,9},{9,10},{10,1... | collective-permute-start | bytes 786440 | tf_op jit(solution)/shard_map/ppermute | solution.py:507
  6.9 20.6 %collective-permute-start.11 = (f32[128,512]{1,0:T(8,128)S(1)}, f32[128,512]{1,0:T(8,128)S(1)}, u32[]{:S(2)}, u32[]{:S(2)}) collective-permute-start(f32[128,512]{1,0:T(8,128)S(1)} %get-tuple-element.102), channel_id=1, source_target_pairs={{0,3},{1,0},{2,1},{3,2},{4,7},{5,4},{6,5},{7,6},{8,11},{9,8},{10,9... | collective-permute-start | bytes 786440 | tf_op jit(solution)/shard_map/ppermute | solution.py:507
  8.9 18.5 %collective-permute-start.12 = (f32[128,512]{1,0:T(8,128)S(1)}, f32[128,512]{1,0:T(8,128)S(1)}, u32[]{:S(2)}, u32[]{:S(2)}) collective-permute-start(f32[128,512]{1,0:T(8,128)S(1)} %get-tuple-element.103), channel_id=1, source_target_pairs={{0,2},{1,3},{2,0},{3,1},{4,6},{5,7},{6,4},{7,5},{8,10},{9,11},{10,... | collective-permute-start | bytes 786440 | tf_op jit(solution)/shard_map/ppermute | solution.py:507
  13.4 18.9 %collective-permute-start.13 = (f32[128,512]{1,0:T(8,128)S(1)}, f32[128,512]{1,0:T(8,128)S(1)}, u32[]{:S(2)}, u32[]{:S(2)}) collective-permute-start(f32[128,512]{1,0:T(8,128)S(1)} %get-tuple-element.104), channel_id=1, source_target_pairs={{0,1},{1,2},{2,3},{3,0},{4,5},{5,6},{6,7},{7,4},{8,9},{9,10},{10,1... | collective-permute-start | bytes 786440 | tf_op jit(solution)/shard_map/ppermute | solution.py:507
  23.5 10.7 %collective-permute-start.3 = (f32[8,128,128]{2,1,0:T(8,128)S(1)}, f32[8,128,128]{2,1,0:T(8,128)S(1)}, u32[]{:S(2)}, u32[]{:S(2)}) collective-permute-start(f32[8,128,128]{2,1,0:T(8,128)S(1)} %get-tuple-element.82), channel_id=1, source_target_pairs={{0,4},{1,5},{2,6},{3,7},{4,0},{5,1},{6,2},{7,3},{8,12},{9,13},{10,... | collective-permute-start | bytes 1572872 | tf_op jit(solution)/shard_map/ppermute | solution.py:494
  34.3 9.1 %collective-permute-start.4 = (f32[2,128,128]{2,1,0:T(8,128)S(1)}, f32[2,128,128]{2,1,0:T(8,128)S(1)}, u32[]{:S(2)}, u32[]{:S(2)}) collective-permute-start(f32[2,128,128]{2,1,0:T(8,128)S(1)} %get-tuple-element.84), channel_id=1, source_target_pairs={{0,1},{1,2},{2,3},{3,0},{4,5},{5,6},{6,7},{7,4},{8,9},{9,10},{10,1... | collective-permute-start | bytes 393224 | tf_op jit(solution)/shard_map/ppermute | solution.py:498
  34.3 9.0 %collective-permute-start.5 = (f32[2,128,128]{2,1,0:T(8,128)S(1)}, f32[2,128,128]{2,1,0:T(8,128)S(1)}, u32[]{:S(2)}, u32[]{:S(2)}) collective-permute-start(f32[2,128,128]{2,1,0:T(8,128)S(1)} %get-tuple-element.85), channel_id=1, source_target_pairs={{0,2},{1,3},{2,0},{3,1},{4,6},{5,7},{6,4},{7,5},{8,10},{9,11},{10,... | collective-permute-start | bytes 393224 | tf_op jit(solution)/shard_map/ppermute | solution.py:498
  35.9 8.4 %collective-permute-start.6 = (f32[2,128,128]{2,1,0:T(8,128)S(1)}, f32[2,128,128]{2,1,0:T(8,128)S(1)}, u32[]{:S(2)}, u32[]{:S(2)}) collective-permute-start(f32[2,128,128]{2,1,0:T(8,128)S(1)} %get-tuple-element.86), channel_id=1, source_target_pairs={{0,3},{1,0},{2,1},{3,2},{4,7},{5,4},{6,5},{7,6},{8,11},{9,8},{10,9... | collective-permute-start | bytes 393224 | tf_op jit(solution)/shard_map/ppermute | solution.py:498
  37.0 8.9 %collective-permute-start.7 = (f32[2,128,128]{2,1,0:T(8,128)S(1)}, f32[2,128,128]{2,1,0:T(8,128)S(1)}, u32[]{:S(2)}, u32[]{:S(2)}) collective-permute-start(f32[2,128,128]{2,1,0:T(8,128)S(1)} %get-tuple-element.87), channel_id=1, source_target_pairs={{0,8},{1,9},{2,10},{3,11},{4,12},{5,13},{6,14},{7,15},{8,0},{9,1},... | collective-permute-start | bytes 393224 | tf_op jit(solution)/shard_map/ppermute | solution.py:498
  38.3 10.4 %collective-permute-start.8 = (f32[2,128,128]{2,1,0:T(8,128)S(1)}, f32[2,128,128]{2,1,0:T(8,128)S(1)}, u32[]{:S(2)}, u32[]{:S(2)}) collective-permute-start(f32[2,128,128]{2,1,0:T(8,128)S(1)} %get-tuple-element.88), channel_id=1, source_target_pairs={{0,9},{1,10},{2,11},{3,8},{4,13},{5,14},{6,15},{7,12},{8,1},{9,2},... | collective-permute-start | bytes 393224 | tf_op jit(solution)/shard_map/ppermute | solution.py:498
  43.4 6.9 %collective-permute-start.9 = (f32[2,128,128]{2,1,0:T(8,128)S(1)}, f32[2,128,128]{2,1,0:T(8,128)S(1)}, u32[]{:S(2)}, u32[]{:S(2)}) collective-permute-start(f32[2,128,128]{2,1,0:T(8,128)S(1)} %get-tuple-element.89), channel_id=1, source_target_pairs={{0,10},{1,11},{2,8},{3,9},{4,14},{5,15},{6,12},{7,13},{8,2},{9,3},... | collective-permute-start | bytes 393224 | tf_op jit(solution)/shard_map/ppermute | solution.py:498
  43.4 8.2 %collective-permute-start.10 = (f32[2,128,128]{2,1,0:T(8,128)S(1)}, f32[2,128,128]{2,1,0:T(8,128)S(1)}, u32[]{:S(2)}, u32[]{:S(2)}) collective-permute-start(f32[2,128,128]{2,1,0:T(8,128)S(1)} %get-tuple-element.90), channel_id=1, source_target_pairs={{0,11},{1,8},{2,9},{3,10},{4,15},{5,12},{6,13},{7,14},{8,3},{9,0},... | collective-permute-start | bytes 393224 | tf_op jit(solution)/shard_map/ppermute | solution.py:498
  44.3 10.4 %collective-permute-start.15 = (f32[2,128,128]{2,1,0:T(8,128)S(1)}, f32[2,128,128]{2,1,0:T(8,128)S(1)}, u32[]{:S(2)}, u32[]{:S(2)}) collective-permute-start(f32[2,128,128]{2,1,0:T(8,128)S(1)} %get-tuple-element.108), channel_id=1, source_target_pairs={{0,1},{1,2},{2,3},{3,0},{4,5},{5,6},{6,7},{7,4},{8,9},{9,10},{10,1... | collective-permute-start | bytes 393224 | tf_op jit(solution)/shard_map/ppermute | solution.py:498
  45.9 9.0 %collective-permute-start.16 = (f32[2,128,128]{2,1,0:T(8,128)S(1)}, f32[2,128,128]{2,1,0:T(8,128)S(1)}, u32[]{:S(2)}, u32[]{:S(2)}) collective-permute-start(f32[2,128,128]{2,1,0:T(8,128)S(1)} %get-tuple-element.109), channel_id=1, source_target_pairs={{0,2},{1,3},{2,0},{3,1},{4,6},{5,7},{6,4},{7,5},{8,10},{9,11},{10,... | collective-permute-start | bytes 393224 | tf_op jit(solution)/shard_map/ppermute | solution.py:498
  48.7 8.1 %collective-permute-start.17 = (f32[2,128,128]{2,1,0:T(8,128)S(1)}, f32[2,128,128]{2,1,0:T(8,128)S(1)}, u32[]{:S(2)}, u32[]{:S(2)}) collective-permute-start(f32[2,128,128]{2,1,0:T(8,128)S(1)} %get-tuple-element.110), channel_id=1, source_target_pairs={{0,3},{1,0},{2,1},{3,2},{4,7},{5,4},{6,5},{7,6},{8,11},{9,8},{10,9... | collective-permute-start | bytes 393224 | tf_op jit(solution)/shard_map/ppermute | solution.py:498
  51.6 7.3 %collective-permute-start.19 = (f32[2,128,128]{2,1,0:T(8,128)S(1)}, f32[2,128,128]{2,1,0:T(8,128)S(1)}, u32[]{:S(2)}, u32[]{:S(2)}) collective-permute-start(f32[2,128,128]{2,1,0:T(8,128)S(1)} %get-tuple-element.112), channel_id=1, source_target_pairs={{0,9},{1,10},{2,11},{3,8},{4,13},{5,14},{6,15},{7,12},{8,1},{9,2},... | collective-permute-start | bytes 393224 | tf_op jit(solution)/shard_map/ppermute | solution.py:498
  54.7 7.5 %collective-permute-start.20 = (f32[2,128,128]{2,1,0:T(8,128)S(1)}, f32[2,128,128]{2,1,0:T(8,128)S(1)}, u32[]{:S(2)}, u32[]{:S(2)}) collective-permute-start(f32[2,128,128]{2,1,0:T(8,128)S(1)} %get-tuple-element.113), channel_id=1, source_target_pairs={{0,10},{1,11},{2,8},{3,9},{4,14},{5,15},{6,12},{7,13},{8,2},{9,3},... | collective-permute-start | bytes 393224 | tf_op jit(solution)/shard_map/ppermute | solution.py:498
  54.9 7.3 %collective-permute-start.21 = (f32[2,128,128]{2,1,0:T(8,128)S(1)}, f32[2,128,128]{2,1,0:T(8,128)S(1)}, u32[]{:S(2)}, u32[]{:S(2)}) collective-permute-start(f32[2,128,128]{2,1,0:T(8,128)S(1)} %get-tuple-element.114), channel_id=1, source_target_pairs={{0,11},{1,8},{2,9},{3,10},{4,15},{5,12},{6,13},{7,14},{8,3},{9,0},... | collective-permute-start | bytes 393224 | tf_op jit(solution)/shard_map/ppermute | solution.py:498
  71.3 9.2 %collective-permute-start.23 = (f32[2,136,128]{2,1,0:T(8,128)S(1)}, f32[2,136,128]{2,1,0:T(8,128)S(1)}, u32[]{:S(2)}, u32[]{:S(2)}) collective-permute-start(f32[2,136,128]{2,1,0:T(8,128)S(1)} %get-tuple-element.121), channel_id=1, source_target_pairs={{0,1},{1,2},{2,3},{3,0},{4,5},{5,6},{6,7},{7,4},{8,9},{9,10},{10,1... | collective-permute-start | bytes 417800 | tf_op jit(solution)/shard_map/ppermute | solution.py:498
  71.4 9.1 %collective-permute-start.24 = (f32[2,136,128]{2,1,0:T(8,128)S(1)}, f32[2,136,128]{2,1,0:T(8,128)S(1)}, u32[]{:S(2)}, u32[]{:S(2)}) collective-permute-start(f32[2,136,128]{2,1,0:T(8,128)S(1)} %get-tuple-element.122), channel_id=1, source_target_pairs={{0,2},{1,3},{2,0},{3,1},{4,6},{5,7},{6,4},{7,5},{8,10},{9,11},{10,... | collective-permute-start | bytes 417800 | tf_op jit(solution)/shard_map/ppermute | solution.py:498
  72.5 8.3 %collective-permute-start.25 = (f32[2,136,128]{2,1,0:T(8,128)S(1)}, f32[2,136,128]{2,1,0:T(8,128)S(1)}, u32[]{:S(2)}, u32[]{:S(2)}) collective-permute-start(f32[2,136,128]{2,1,0:T(8,128)S(1)} %get-tuple-element.123), channel_id=1, source_target_pairs={{0,3},{1,0},{2,1},{3,2},{4,7},{5,4},{6,5},{7,6},{8,11},{9,8},{10,9... | collective-permute-start | bytes 417800 | tf_op jit(solution)/shard_map/ppermute | solution.py:498
  74.7 9.2 %collective-permute-start.27 = (f32[2,136,128]{2,1,0:T(8,128)S(1)}, f32[2,136,128]{2,1,0:T(8,128)S(1)}, u32[]{:S(2)}, u32[]{:S(2)}) collective-permute-start(f32[2,136,128]{2,1,0:T(8,128)S(1)} %get-tuple-element.125), channel_id=1, source_target_pairs={{0,9},{1,10},{2,11},{3,8},{4,13},{5,14},{6,15},{7,12},{8,1},{9,2},... | collective-permute-start | bytes 417800 | tf_op jit(solution)/shard_map/ppermute | solution.py:498
  (9 other events, 90.0 us)

commit v6 on v5

--- a/solution.py
+++ b/solution.py
@@ -25,11 +25,12 @@
 ORDER = (6, 5, 7, 4, 2, 1, 3)
 
 
-def call(kernel, out, scratch, limit, flops, ins):
+def call(kernel, out, scratch, limit, flops, ins, outs=None):
     return pl.pallas_call(
         kernel,
         out_shape=out,
         in_specs=ins,
+        **({} if outs is None else {"out_specs": outs}),
         scratch_shapes=scratch,
         compiler_params=pltpu.CompilerParams(vmem_limit_bytes=limit * MIB),
         cost_estimate=pl.CostEstimate(flops=flops, bytes_accessed=4 * MIB, transcendentals=0),
@@ -236,9 +237,14 @@
     )
 
 
+def way(device):
+    return 1 - ((device & 4) >> 1)
+
+
 def pack_kernel(device_ref, x_ref, *outs):
+    device = device_ref[0]
     for index in range(8):
-        start = pl.multiple_of(((device_ref[0] + index) & 3) * ROWS, ROWS)
+        start = pl.multiple_of(((device + way(device) * (index & 3)) & 3) * ROWS, ROWS)
         outs[index][...] = x_ref[index // 4, 0, pl.ds(start, ROWS), :]
 
 
@@ -254,6 +260,7 @@
     zero, two, even, odd = quarters([x[...] for x in blocks])
     device = device_ref[0]
     place = device & 3
+    odd = way(device).astype(jnp.float32) * odd
     along = jnp.where(place == 0, 1.0, jnp.where(place == 2, -1.0, 0.0))
     across = jnp.where(place == 1, 1.0, jnp.where(place == 3, -1.0, 0.0))
     flip = jnp.where((place & 1) == 0, 1.0, -1.0)
@@ -265,13 +272,12 @@
         for part in range(count):
             all_ref[first + part] = value[:, LANES * part : LANES * (part + 1)]
     for index in range(8):
-        there = other_chip(device, index)
-        keep_ref[index] = all_ref[there]
-        send_ref[index] = all_ref[there ^ 4]
+        keep_ref[index] = all_ref[other_chip(device, index)]
+        send_ref[index] = all_ref[other_chip(device ^ 4, index)]
 
 
 def other_chip(device, index):
-    return ((device & 12) ^ (2 * (index & 4))) + ((device + index) & 3)
+    return ((device & 12) ^ (2 * (index & 4))) + ((device + way(device) * (index & 3)) & 3)
 
 
 def columns(device, blocks, table):
@@ -299,7 +305,7 @@
     for step in range(4):
         near, far = g_refs[step], g_refs[4 + step]
         same, other = near[0] + far[0], near[1] + far[1]
-        rows = pl.ds(pl.multiple_of(((device - step) & 3) * ROWS, ROWS), ROWS)
+        rows = pl.ds(pl.multiple_of(((device - way(device) * step) & 3) * ROWS, ROWS), ROWS)
         part_ref[0, rows, :] = same + other
         part_ref[1, rows, :] = flip_core * (same - other)
         same, other = flip_chip * (near[0] - far[0]), flip_chip * (near[1] - far[1])
@@ -371,9 +377,8 @@
         out_ref[s, ROWS + 2 : ROWS + 3, :] = energy
         out_ref[s, ROWS + 3 : BLOCK, :] = jnp.zeros((BLOCK - ROWS - 3, LANES), jnp.float32)
     for index in range(8):
-        there = other_chip(device, index)
-        keep_ref[index] = out_ref[there]
-        send_ref[index] = out_ref[there ^ 4]
+        keep_ref[index] = out_ref[other_chip(device, index)]
+        send_ref[index] = out_ref[other_chip(device ^ 4, index)]
 
 
 def row_pass(device, one, g, sample, frequency, factors):
@@ -391,7 +396,7 @@
 
 def peaks_kernel(bins_ref, device_ref, *refs):
     got, table, offsets_ref, refs = refs[:8], pairs(refs[8:18]), refs[18], refs[19:]
-    snr_ref, heights_ref, counts_ref, field_ref, wide_ref, side_ref, pick_ref, x_ref = refs
+    snr_ref, heights_ref, counts_ref, field_ref, wide_ref, side_ref, pick_ref, x_ref, own_ref, sem = refs
     for index in range(8):
         there = other_chip(device_ref[0], (index & 4) | (-index & 3))
         x_ref[there] = got[index][0]
@@ -412,7 +417,7 @@
     inverse = 1.0 / jnp.sqrt(mean + 1e-06)
     for c, value in enumerate(back(values, 1)):
         cols = pl.ds(INNER * c, INNER)
-        snr_ref[:, cols] = value[0:ROWS] * inverse
+        own_ref[:, cols] = value[0:ROWS] * inverse
         field_ref[8 : ROWS + 8, cols] = value[0:ROWS]
         field_ref[7:8, cols] = value[ROWS : ROWS + 1]
         field_ref[ROWS + 8 : ROWS + 9, cols] = value[ROWS + 1 : ROWS + 2]
@@ -422,7 +427,9 @@
         side = jnp.maximum(pltpu.roll(value, 1, 1), pltpu.roll(value, N - 1, 1))
         wide_ref[start : start + size, :] = jnp.maximum(side, value)
         side_ref[start : start + size, :] = side
-    blocks = iota((LANES, N), 1) // CELL == iota((LANES, N), 0)
+    copy = pltpu.make_async_copy(own_ref, snr_ref, sem.at[0])
+    copy.start()
+    blocks = lax.shift_right_logical(iota((LANES, N), 1), 4) == iota((LANES, N), 0)
     blocks = jnp.where(blocks, 1.0, 0.0).astype(jnp.bfloat16)
     offsets = offsets_ref[...].astype(jnp.float32).astype(jnp.bfloat16)
     offsets = jnp.concatenate([offsets, offsets], axis=0)
@@ -435,17 +442,20 @@
         below = wide_ref[base + 1 : base + 1 + CELL, :]
         nearest = jnp.maximum(side, jnp.maximum(above, below))
         chosen = spread[p : p + 1, :] == code
-        height = jnp.sum(jnp.where(chosen, value - nearest, 0.0), axis=0, keepdims=True)
-        level = jnp.sum(jnp.where(chosen, value, 0.0), axis=0, keepdims=True)
-        pick_ref[p : p + 1, :] = height
-        pick_ref[8 + p : 9 + p, :] = level
+        height = jnp.where(chosen, value - nearest, 0.0)
+        level = jnp.where(chosen, value, 0.0)
+        pick_ref[8 * p : 8 * p + 8, :] = height[0:8] + height[8:16]
+        pick_ref[HALF + 8 * p : HALF + 8 * p + 8, :] = level[0:8] + level[8:16]
     high, low = split(pick_ref[...])
     gather = partial(
         lax.dot_general,
         dimension_numbers=(((1,), (1,)), ((), ())),
         preferred_element_type=jnp.float32,
     )
-    picked = (gather(high, blocks) + gather(low, blocks)) * inverse
+    both = gather(jnp.concatenate([high, low], axis=0), blocks)
+    both = both[0:LANES] + both[LANES : 2 * LANES]
+    rows = [jnp.sum(both[8 * p : 8 * p + 8], axis=0, keepdims=True) for p in range(16)]
+    picked = jnp.concatenate(rows, axis=0) * inverse
     heights, values = picked[0:8], picked[8:16]
     heights_ref[...] = heights
     weight = jax.nn.sigmoid(heights * 20.0)
@@ -458,6 +468,7 @@
         counts = counts + jnp.where(lane == k, summed, 0.0)
     for s in range(DEV):
         counts_ref[s] = jnp.broadcast_to(counts, (8, LANES))
+    copy.wait()
 
 
 def peak_pass(thresholds, device, x, table, offsets):
@@ -471,16 +482,19 @@
         pltpu.VMEM((ROWS + 16, N), f32),
         pltpu.VMEM((ROWS + 16, N), f32),
         pltpu.VMEM((ROWS + 16, N), f32),
-        pltpu.VMEM((16, N), f32),
+        pltpu.VMEM((LANES, N), f32),
         pltpu.VMEM((DEV, BLOCK, LANES), f32),
+        pltpu.VMEM((ROWS, N), f32),
+        pltpu.SemaphoreType.DMA((1,)),
     ]
     specs = [pl.BlockSpec(memory_space=pltpu.SMEM)] * 2 + [pl.BlockSpec(memory_space=pltpu.VMEM)] * 19
-    run = call(peaks_kernel, out, scratch, LIMIT[4], 2 * 10**9, specs)
+    places = [pl.BlockSpec(memory_space=pl.ANY)] + [pl.BlockSpec(memory_space=pltpu.VMEM)] * 2
+    run = call(peaks_kernel, out, scratch, LIMIT[4], 2 * 10**9, specs, places)
     return run(thresholds, device, *x, *table, offsets)
 
 
 def chip_pairs(index):
-    return [(d, (d & 12 ^ (2 * (index & 4))) + ((d + index) & 3)) for d in range(DEV)]
+    return [(d, other_chip(d, index)) for d in range(DEV)]
 
 
 def body(shear, smoothing, offsets, thresholds):
@@ -503,8 +517,7 @@
     for field in range(2):
         got = [blocks[4 * field], None, None, None]
         for step in (2, 1, 3):
-            pairs = [(c, (c + step) % 4) for c in range(4)]
-            got[4 - step] = lax.ppermute(blocks[4 * field + step], "col", pairs)
+            got[4 - step] = lax.ppermute(blocks[4 * field + step], group, chip_pairs(step))
         fields.append(got)
     sample, frequency, factors = tables(smoothing, device)
     g = columns(device, fields[0], sample)

time: 105 us -> 104 us (level)
  starting transfers between devices: 32.1 us -> 48.2 us
  waiting for transfers between devices: 41.3 us -> 25.8 us
  blocking collectives: 12.5 us -> 11.3 us
    ppermute x21, starting transfers between devices: 17.2 us -> 26.2 us  [scatter(): done.append((index, lax.ppermute(blocks[index], group, chip_pairs(index))))]
    ppermute x6, waiting for transfers between devices: 14.4 us -> 6.65 us  [body(): lax.ppermute(blocks[4 * field + step], group, chip_pairs(step))]
    ppermute x21, waiting for transfers between devices: 25.3 us -> 17.5 us  [scatter(): done.append((index, lax.ppermute(blocks[index], group, chip_pairs(index))))]
    ppermute x3, starting transfers between devices: 7.12 us -> 13.5 us  [scatter(): got = lax.ppermute(send, group, [(d, d ^ 4) for d in range(DEV)])]
    all_to_all x1, blocking collectives: 12.5 us -> 11.3 us  [exchange(): return lax.all_to_all(x, group, split_axis=0, concat_axis=0, tiled=True)]
  transfers between devices with their start and end apart: 30 -> 30, of which waited for: 15 -> 16; matrix products, arithmetic and copies ran while one was open for 0% -> 0% of each run, Pallas kernels for 8% -> 8%
where the time goes in v6:
time: 104 us
  starting transfers between devices  48.2 us (46%)
  waiting for transfers between devices  25.8 us (25%)
  Pallas kernels  15.4 us (15%)
  blocking collectives  11.3 us (11%)
  local copies, waits for them, and re-layouts  1.59 us (2%)
  between operations  1.4 us (1%)
    ppermute x21, starting transfers between devices, scatter(): done.append((index, lax.ppermute(blocks[index], group, chip_pairs(index))))  26.2 us
    ppermute x21, waiting for transfers between devices, scatter(): done.append((index, lax.ppermute(blocks[index], group, chip_pairs(index))))  17.5 us
    ppermute x3, starting transfers between devices, scatter(): got = lax.ppermute(send, group, [(d, d ^ 4) for d in range(DEV)])  13.5 us
    all_to_all x1, blocking collectives, exchange(): return lax.all_to_all(x, group, split_axis=0, concat_axis=0, tiled=True)  11.3 us
    ppermute x6, starting transfers between devices, body(): lax.ppermute(blocks[4 * field + step], group, chip_pairs(step))  8.49 us
    ppermute x6, waiting for transfers between devices, body(): lax.ppermute(blocks[4 * field + step], group, chip_pairs(step))  6.65 us
    pallas_call x1, Pallas kernels, peak_pass(): return run(thresholds, device, *x, *table, offsets)  4.58 us
    pallas_call x1, Pallas kernels, tables(): call(tables_kernel, out, scratch, LIMIT[0], 10 ** 9, [smem, smem])  4.45 us
  transfers between devices with their start and end apart: 30, of which 16 were waited for; matrix products, arithmetic and copies ran while one was open for 0% of the time, Pallas kernels for 8%

profile of v6, /device:TPU:1, one launch (start us, length us, event | category | flops | bytes accessed | tf_op | source)
XLA Modules:
  0.0 104.2 jit_solution(1053578680577265003)
XLA Ops:
  2.4 2.1 %collective-permute-start = (f32[128,512]{1,0:T(8,128)S(1)}, f32[128,512]{1,0:T(8,128)S(1)}, u32[]{:S(2)}, u32[]{:S(2)}) collective-permute-start(f32[128,512]{1,0:T(8,128)S(1)} %get-tuple-element.68), channel_id=1, source_target_pairs={{0,3},{1,0},{2,1},{3,2},{4,5},{5,6},{6,7},{7,4},{8,11},{9,8},{10,9... | collective-permute-start | bytes 786440 | tf_op jit(solution)/shard_map/ppermute | solution.py:520
  4.5 2.5 %collective-permute-start.1 = (f32[128,512]{1,0:T(8,128)S(1)}, f32[128,512]{1,0:T(8,128)S(1)}, u32[]{:S(2)}, u32[]{:S(2)}) collective-permute-start(f32[128,512]{1,0:T(8,128)S(1)} %get-tuple-element.69), channel_id=1, source_target_pairs={{0,2},{1,3},{2,0},{3,1},{4,6},{5,7},{6,4},{7,5},{8,10},{9,11},{10,... | collective-permute-start | bytes 786440 | tf_op jit(solution)/shard_map/ppermute | solution.py:520
  9.9 1.6 %collective-permute-start.13 = (f32[128,512]{1,0:T(8,128)S(1)}, f32[128,512]{1,0:T(8,128)S(1)}, u32[]{:S(2)}, u32[]{:S(2)}) collective-permute-start(f32[128,512]{1,0:T(8,128)S(1)} %get-tuple-element.104), channel_id=1, source_target_pairs={{0,1},{1,2},{2,3},{3,0},{4,7},{5,4},{6,5},{7,6},{8,9},{9,10},{10,1... | collective-permute-start | bytes 786440 | tf_op jit(solution)/shard_map/ppermute | solution.py:520
  11.5 4.4 %shard_map.68 = (bf16[256,256]{1,0:T(8,128)(2,1)S(1)}, bf16[256,256]{1,0:T(8,128)(2,1)S(1)}, bf16[256,256]{1,0:T(8,128)(2,1)S(1)}, bf16[256,256]{1,0:T(8,128)(2,...) custom-call(f32[1]{0:T(128)S(6)} %copy.7.smooth_ref, ...), custom_call_target="tpu_custom_call" | custom-call | flops 1000000000 | bytes 4194304 | tf_op jit(solution)/shard_map/pallas_call | solution.py:226
  18.9 5.3 %collective-permute-start.3 = (f32[8,128,128]{2,1,0:T(8,128)S(1)}, f32[8,128,128]{2,1,0:T(8,128)S(1)}, u32[]{:S(2)}, u32[]{:S(2)}) collective-permute-start(f32[8,128,128]{2,1,0:T(8,128)S(1)} %get-tuple-element.82), channel_id=1, source_target_pairs={{0,4},{1,5},{2,6},{3,7},{4,0},{5,1},{6,2},{7,3},{8,12},{9,13},{10,... | collective-permute-start | bytes 1572872 | tf_op jit(solution)/shard_map/ppermute | solution.py:508
  24.1 3.4 %collective-permute-done.12.refs_2_ = f32[128,512]{1,0:T(8,128)S(1)} collective-permute-done((f32[128,512]{1,0:T(8,128)S(1)}, f32[128,512]{1,0:T(8,128)S(1)}, u32[]{:S(2)}, u32[]{:S(2)}) %collective-permute-start.12) | collective-permute-done | bytes 262176 | tf_op jit(solution)/shard_map/ppermute | solution.py:520
  30.1 2.3 %collective-permute-start.14 = (f32[8,128,128]{2,1,0:T(8,128)S(1)}, f32[8,128,128]{2,1,0:T(8,128)S(1)}, u32[]{:S(2)}, u32[]{:S(2)}) collective-permute-start(f32[8,128,128]{2,1,0:T(8,128)S(1)} %get-tuple-element.106), channel_id=1, source_target_pairs={{0,4},{1,5},{2,6},{3,7},{4,0},{5,1},{6,2},{7,3},{8,12},{9,13},{10,... | collective-permute-start | bytes 1572872 | tf_op jit(solution)/shard_map/ppermute | solution.py:508
  32.5 2.0 %collective-permute-start.4 = (f32[2,128,128]{2,1,0:T(8,128)S(1)}, f32[2,128,128]{2,1,0:T(8,128)S(1)}, u32[]{:S(2)}, u32[]{:S(2)}) collective-permute-start(f32[2,128,128]{2,1,0:T(8,128)S(1)} %get-tuple-element.84), channel_id=1, source_target_pairs={{0,1},{1,2},{2,3},{3,0},{4,7},{5,4},{6,5},{7,6},{8,9},{9,10},{10,1... | collective-permute-start | bytes 393224 | tf_op jit(solution)/shard_map/ppermute | solution.py:512
  36.3 2.5 %collective-permute-start.8 = (f32[2,128,128]{2,1,0:T(8,128)S(1)}, f32[2,128,128]{2,1,0:T(8,128)S(1)}, u32[]{:S(2)}, u32[]{:S(2)}) collective-permute-start(f32[2,128,128]{2,1,0:T(8,128)S(1)} %get-tuple-element.88), channel_id=1, source_target_pairs={{0,9},{1,10},{2,11},{3,8},{4,15},{5,12},{6,13},{7,14},{8,1},{9,2},... | collective-permute-start | bytes 393224 | tf_op jit(solution)/shard_map/ppermute | solution.py:512
  41.6 3.2 %collective-permute-start.10 = (f32[2,128,128]{2,1,0:T(8,128)S(1)}, f32[2,128,128]{2,1,0:T(8,128)S(1)}, u32[]{:S(2)}, u32[]{:S(2)}) collective-permute-start(f32[2,128,128]{2,1,0:T(8,128)S(1)} %get-tuple-element.90), channel_id=1, source_target_pairs={{0,11},{1,8},{2,9},{3,10},{4,13},{5,14},{6,15},{7,12},{8,3},{9,0},... | collective-permute-start | bytes 393224 | tf_op jit(solution)/shard_map/ppermute | solution.py:512
  46.3 2.2 %collective-permute-done.9.refs_6_ = f32[2,128,128]{2,1,0:T(8,128)S(1)} collective-permute-done((f32[2,128,128]{2,1,0:T(8,128)S(1)}, f32[2,128,128]{2,1,0:T(8,128)S(1)}, u32[]{:S(2)}, u32[]{:S(2)}) %collective-permute-start.9) | collective-permute-done | bytes 131104 | tf_op jit(solution)/shard_map/ppermute | solution.py:512
  48.6 2.4 %collective-permute-done.10.refs_7_ = f32[2,128,128]{2,1,0:T(8,128)S(1)} collective-permute-done((f32[2,128,128]{2,1,0:T(8,128)S(1)}, f32[2,128,128]{2,1,0:T(8,128)S(1)}, u32[]{:S(2)}, u32[]{:S(2)}) %collective-permute-start.10) | collective-permute-done | bytes 131104 | tf_op jit(solution)/shard_map/ppermute | solution.py:512
  51.0 2.0 %collective-permute-start.19 = (f32[2,128,128]{2,1,0:T(8,128)S(1)}, f32[2,128,128]{2,1,0:T(8,128)S(1)}, u32[]{:S(2)}, u32[]{:S(2)}) collective-permute-start(f32[2,128,128]{2,1,0:T(8,128)S(1)} %get-tuple-element.112), channel_id=1, source_target_pairs={{0,9},{1,10},{2,11},{3,8},{4,15},{5,12},{6,13},{7,14},{8,1},{9,2},... | collective-permute-start | bytes 393224 | tf_op jit(solution)/shard_map/ppermute | solution.py:512
  53.6 2.1 %collective-permute-start.21 = (f32[2,128,128]{2,1,0:T(8,128)S(1)}, f32[2,128,128]{2,1,0:T(8,128)S(1)}, u32[]{:S(2)}, u32[]{:S(2)}) collective-permute-start(f32[2,128,128]{2,1,0:T(8,128)S(1)} %get-tuple-element.114), channel_id=1, source_target_pairs={{0,11},{1,8},{2,9},{3,10},{4,13},{5,14},{6,15},{7,12},{8,3},{9,0},... | collective-permute-start | bytes 393224 | tf_op jit(solution)/shard_map/ppermute | solution.py:512
  57.1 2.3 %collective-permute-done.20.refs_6_ = f32[2,128,128]{2,1,0:T(8,128)S(1)} collective-permute-done((f32[2,128,128]{2,1,0:T(8,128)S(1)}, f32[2,128,128]{2,1,0:T(8,128)S(1)}, u32[]{:S(2)}, u32[]{:S(2)}) %collective-permute-start.20) | collective-permute-done | bytes 131104 | tf_op jit(solution)/shard_map/ppermute | solution.py:512
  60.7 2.5 %shard_map.74 = (f32[8,136,128]{2,1,0:T(8,128)S(1)}, f32[8,136,128]{2,1,0:T(8,128)S(1)}) custom-call(s32[1]{0:T(128)} %bitcast.device_ref, f32[2048,128]{1,0:T(8,128)S(1)} %shard_map.71.one_ref, f32[2,128,128]{2,1,0:T(8,128)S(1)} %get-tuple-element.107.refs_0_, f32[2,128,128]{2,1,0:T(8,128)S(1)} %collective-permute-done.15.refs_1_, ...), custom_call_target="tpu_custom_call" | custom-call | flops 3000000000 | bytes 4194304 | tf_op jit(solution)/shard_map/pallas_call | solution.py:394
  63.2 5.9 %collective-permute-start.22 = (f32[8,136,128]{2,1,0:T(8,128)S(1)}, f32[8,136,128]{2,1,0:T(8,128)S(1)}, u32[]{:S(2)}, u32[]{:S(2)}) collective-permute-start(f32[8,136,128]{2,1,0:T(8,128)S(1)} %get-tuple-element.119), channel_id=1, source_target_pairs={{0,4},{1,5},{2,6},{3,7},{4,0},{5,1},{6,2},{7,3},{8,12},{9,13},{10,... | collective-permute-start | bytes 1671176 | tf_op jit(solution)/shard_map/ppermute | solution.py:508
  74.3 2.6 %collective-permute-start.27 = (f32[2,136,128]{2,1,0:T(8,128)S(1)}, f32[2,136,128]{2,1,0:T(8,128)S(1)}, u32[]{:S(2)}, u32[]{:S(2)}) collective-permute-start(f32[2,136,128]{2,1,0:T(8,128)S(1)} %get-tuple-element.125), channel_id=1, source_target_pairs={{0,9},{1,10},{2,11},{3,8},{4,15},{5,12},{6,13},{7,14},{8,1},{9,2},... | collective-permute-start | bytes 417800 | tf_op jit(solution)/shard_map/ppermute | solution.py:512
  77.0 2.0 %collective-permute-start.28 = (f32[2,136,128]{2,1,0:T(8,128)S(1)}, f32[2,136,128]{2,1,0:T(8,128)S(1)}, u32[]{:S(2)}, u32[]{:S(2)}) collective-permute-start(f32[2,136,128]{2,1,0:T(8,128)S(1)} %get-tuple-element.126), channel_id=1, source_target_pairs={{0,10},{1,11},{2,8},{3,9},{4,14},{5,15},{6,12},{7,13},{8,2},{9,3},... | collective-permute-start | bytes 417800 | tf_op jit(solution)/shard_map/ppermute | solution.py:512
  80.2 2.3 %collective-permute-done.25.refs_3_ = f32[2,136,128]{2,1,0:T(8,128)S(1)} collective-permute-done((f32[2,136,128]{2,1,0:T(8,128)S(1)}, f32[2,136,128]{2,1,0:T(8,128)S(1)}, u32[]{:S(2)}, u32[]{:S(2)}) %collective-permute-start.25) | collective-permute-done | bytes 139296 | tf_op jit(solution)/shard_map/ppermute | solution.py:512
  82.6 3.4 %collective-permute-done.28.refs_6_ = f32[2,136,128]{2,1,0:T(8,128)S(1)} collective-permute-done((f32[2,136,128]{2,1,0:T(8,128)S(1)}, f32[2,136,128]{2,1,0:T(8,128)S(1)}, u32[]{:S(2)}, u32[]{:S(2)}) %collective-permute-start.28) | collective-permute-done | bytes 139296 | tf_op jit(solution)/shard_map/ppermute | solution.py:512
  86.0 1.9 %collective-permute-done.29.refs_7_ = f32[2,136,128]{2,1,0:T(8,128)S(1)} collective-permute-done((f32[2,136,128]{2,1,0:T(8,128)S(1)}, f32[2,136,128]{2,1,0:T(8,128)S(1)}, u32[]{:S(2)}, u32[]{:S(2)}) %collective-permute-start.29) | collective-permute-done | bytes 139296 | tf_op jit(solution)/shard_map/ppermute | solution.py:512
  87.8 4.6 %shard_map.76 = (f32[128,2048]{1,0:T(8,128)}, f32[8,128]{1,0:T(8,128)}, f32[16,8,128]{2,1,0:T(8,128)S(1)}) custom-call(s32[1,16]{1,0:T(1,128)S(1)} %copy-done.2, s32[1]{0:T(128)} %bitcast.device_ref, f32[2,136,128]{2,1,0:T(8,128)S(1)} %get-tuple-element.120.refs_0_, f32[2,136,128]{2,1,0:T(8,128)S(1)} %collective-permute-done.23.refs_1_, ...), custom_call_target="tpu_custom_call" | custom-call | flops 2000000000 | bytes 4194304 | tf_op jit(solution)/shard_map/pallas_call | solution.py:493
  92.4 11.3 %all_to_all.5 = f32[16,8,128]{2,1,0:T(8,128)S(1)} all-to-all(f32[16,8,128]{2,1,0:T(8,128)S(1)} %get-tuple-element.130), channel_id=1, replica_groups=mesh['maps'=16,'row'=4,'col'=4] {'row','col'}, dimensions={0} | all-to-all | bytes 131072 | tf_op jit(solution)/shard_map/all_to_all | solution.py:505
  (54 shorter events, 26.1 us)
Async XLA Ops:
  2.4 7.6 %collective-permute-start = (f32[128,512]{1,0:T(8,128)S(1)}, f32[128,512]{1,0:T(8,128)S(1)}, u32[]{:S(2)}, u32[]{:S(2)}) collective-permute-start(f32[128,512]{1,0:T(8,128)S(1)} %get-tuple-element.68), channel_id=1, source_target_pairs={{0,3},{1,0},{2,1},{3,2},{4,5},{5,6},{6,7},{7,4},{8,11},{9,8},{10,9... | collective-permute-start | bytes 786440 | tf_op jit(solution)/shard_map/ppermute | solution.py:520
  4.5 11.8 %collective-permute-start.1 = (f32[128,512]{1,0:T(8,128)S(1)}, f32[128,512]{1,0:T(8,128)S(1)}, u32[]{:S(2)}, u32[]{:S(2)}) collective-permute-start(f32[128,512]{1,0:T(8,128)S(1)} %get-tuple-element.69), channel_id=1, source_target_pairs={{0,2},{1,3},{2,0},{3,1},{4,6},{5,7},{6,4},{7,5},{8,10},{9,11},{10,... | collective-permute-start | bytes 786440 | tf_op jit(solution)/shard_map/ppermute | solution.py:520
  6.9 10.8 %collective-permute-start.2 = (f32[128,512]{1,0:T(8,128)S(1)}, f32[128,512]{1,0:T(8,128)S(1)}, u32[]{:S(2)}, u32[]{:S(2)}) collective-permute-start(f32[128,512]{1,0:T(8,128)S(1)} %get-tuple-element.70), channel_id=1, source_target_pairs={{0,1},{1,2},{2,3},{3,0},{4,7},{5,4},{6,5},{7,6},{8,9},{9,10},{10,1... | collective-permute-start | bytes 786440 | tf_op jit(solution)/shard_map/ppermute | solution.py:520
  8.1 16.1 %collective-permute-start.11 = (f32[128,512]{1,0:T(8,128)S(1)}, f32[128,512]{1,0:T(8,128)S(1)}, u32[]{:S(2)}, u32[]{:S(2)}) collective-permute-start(f32[128,512]{1,0:T(8,128)S(1)} %get-tuple-element.102), channel_id=1, source_target_pairs={{0,3},{1,0},{2,1},{3,2},{4,5},{5,6},{6,7},{7,4},{8,11},{9,8},{10,9... | collective-permute-start | bytes 786440 | tf_op jit(solution)/shard_map/ppermute | solution.py:520
  8.4 19.1 %collective-permute-start.12 = (f32[128,512]{1,0:T(8,128)S(1)}, f32[128,512]{1,0:T(8,128)S(1)}, u32[]{:S(2)}, u32[]{:S(2)}) collective-permute-start(f32[128,512]{1,0:T(8,128)S(1)} %get-tuple-element.103), channel_id=1, source_target_pairs={{0,2},{1,3},{2,0},{3,1},{4,6},{5,7},{6,4},{7,5},{8,10},{9,11},{10,... | collective-permute-start | bytes 786440 | tf_op jit(solution)/shard_map/ppermute | solution.py:520
  9.9 19.1 %collective-permute-start.13 = (f32[128,512]{1,0:T(8,128)S(1)}, f32[128,512]{1,0:T(8,128)S(1)}, u32[]{:S(2)}, u32[]{:S(2)}) collective-permute-start(f32[128,512]{1,0:T(8,128)S(1)} %get-tuple-element.104), channel_id=1, source_target_pairs={{0,1},{1,2},{2,3},{3,0},{4,7},{5,4},{6,5},{7,6},{8,9},{9,10},{10,1... | collective-permute-start | bytes 786440 | tf_op jit(solution)/shard_map/ppermute | solution.py:520
  18.9 13.6 %collective-permute-start.3 = (f32[8,128,128]{2,1,0:T(8,128)S(1)}, f32[8,128,128]{2,1,0:T(8,128)S(1)}, u32[]{:S(2)}, u32[]{:S(2)}) collective-permute-start(f32[8,128,128]{2,1,0:T(8,128)S(1)} %get-tuple-element.82), channel_id=1, source_target_pairs={{0,4},{1,5},{2,6},{3,7},{4,0},{5,1},{6,2},{7,3},{8,12},{9,13},{10,... | collective-permute-start | bytes 1572872 | tf_op jit(solution)/shard_map/ppermute | solution.py:508
  32.5 7.2 %collective-permute-start.4 = (f32[2,128,128]{2,1,0:T(8,128)S(1)}, f32[2,128,128]{2,1,0:T(8,128)S(1)}, u32[]{:S(2)}, u32[]{:S(2)}) collective-permute-start(f32[2,128,128]{2,1,0:T(8,128)S(1)} %get-tuple-element.84), channel_id=1, source_target_pairs={{0,1},{1,2},{2,3},{3,0},{4,7},{5,4},{6,5},{7,6},{8,9},{9,10},{10,1... | collective-permute-start | bytes 393224 | tf_op jit(solution)/shard_map/ppermute | solution.py:512
  34.9 9.9 %collective-permute-start.6 = (f32[2,128,128]{2,1,0:T(8,128)S(1)}, f32[2,128,128]{2,1,0:T(8,128)S(1)}, u32[]{:S(2)}, u32[]{:S(2)}) collective-permute-start(f32[2,128,128]{2,1,0:T(8,128)S(1)} %get-tuple-element.86), channel_id=1, source_target_pairs={{0,3},{1,0},{2,1},{3,2},{4,5},{5,6},{6,7},{7,4},{8,11},{9,8},{10,9... | collective-permute-start | bytes 393224 | tf_op jit(solution)/shard_map/ppermute | solution.py:512
  35.2 9.9 %collective-permute-start.7 = (f32[2,128,128]{2,1,0:T(8,128)S(1)}, f32[2,128,128]{2,1,0:T(8,128)S(1)}, u32[]{:S(2)}, u32[]{:S(2)}) collective-permute-start(f32[2,128,128]{2,1,0:T(8,128)S(1)} %get-tuple-element.87), channel_id=1, source_target_pairs={{0,8},{1,9},{2,10},{3,11},{4,12},{5,13},{6,14},{7,15},{8,0},{9,1},... | collective-permute-start | bytes 393224 | tf_op jit(solution)/shard_map/ppermute | solution.py:512
  36.3 10.0 %collective-permute-start.8 = (f32[2,128,128]{2,1,0:T(8,128)S(1)}, f32[2,128,128]{2,1,0:T(8,128)S(1)}, u32[]{:S(2)}, u32[]{:S(2)}) collective-permute-start(f32[2,128,128]{2,1,0:T(8,128)S(1)} %get-tuple-element.88), channel_id=1, source_target_pairs={{0,9},{1,10},{2,11},{3,8},{4,15},{5,12},{6,13},{7,14},{8,1},{9,2},... | collective-permute-start | bytes 393224 | tf_op jit(solution)/shard_map/ppermute | solution.py:512
  39.7 8.8 %collective-permute-start.9 = (f32[2,128,128]{2,1,0:T(8,128)S(1)}, f32[2,128,128]{2,1,0:T(8,128)S(1)}, u32[]{:S(2)}, u32[]{:S(2)}) collective-permute-start(f32[2,128,128]{2,1,0:T(8,128)S(1)} %get-tuple-element.89), channel_id=1, source_target_pairs={{0,10},{1,11},{2,8},{3,9},{4,14},{5,15},{6,12},{7,13},{8,2},{9,3},... | collective-permute-start | bytes 393224 | tf_op jit(solution)/shard_map/ppermute | solution.py:512
  41.6 9.4 %collective-permute-start.10 = (f32[2,128,128]{2,1,0:T(8,128)S(1)}, f32[2,128,128]{2,1,0:T(8,128)S(1)}, u32[]{:S(2)}, u32[]{:S(2)}) collective-permute-start(f32[2,128,128]{2,1,0:T(8,128)S(1)} %get-tuple-element.90), channel_id=1, source_target_pairs={{0,11},{1,8},{2,9},{3,10},{4,13},{5,14},{6,15},{7,12},{8,3},{9,0},... | collective-permute-start | bytes 393224 | tf_op jit(solution)/shard_map/ppermute | solution.py:512
  44.8 8.2 %collective-permute-start.15 = (f32[2,128,128]{2,1,0:T(8,128)S(1)}, f32[2,128,128]{2,1,0:T(8,128)S(1)}, u32[]{:S(2)}, u32[]{:S(2)}) collective-permute-start(f32[2,128,128]{2,1,0:T(8,128)S(1)} %get-tuple-element.108), channel_id=1, source_target_pairs={{0,1},{1,2},{2,3},{3,0},{4,7},{5,4},{6,5},{7,6},{8,9},{9,10},{10,1... | collective-permute-start | bytes 393224 | tf_op jit(solution)/shard_map/ppermute | solution.py:512
  45.0 8.6 %collective-permute-start.16 = (f32[2,128,128]{2,1,0:T(8,128)S(1)}, f32[2,128,128]{2,1,0:T(8,128)S(1)}, u32[]{:S(2)}, u32[]{:S(2)}) collective-permute-start(f32[2,128,128]{2,1,0:T(8,128)S(1)} %get-tuple-element.109), channel_id=1, source_target_pairs={{0,2},{1,3},{2,0},{3,1},{4,6},{5,7},{6,4},{7,5},{8,10},{9,11},{10,... | collective-permute-start | bytes 393224 | tf_op jit(solution)/shard_map/ppermute | solution.py:512
  46.3 10.8 %collective-permute-start.17 = (f32[2,128,128]{2,1,0:T(8,128)S(1)}, f32[2,128,128]{2,1,0:T(8,128)S(1)}, u32[]{:S(2)}, u32[]{:S(2)}) collective-permute-start(f32[2,128,128]{2,1,0:T(8,128)S(1)} %get-tuple-element.110), channel_id=1, source_target_pairs={{0,3},{1,0},{2,1},{3,2},{4,5},{5,6},{6,7},{7,4},{8,11},{9,8},{10,9... | collective-permute-start | bytes 393224 | tf_op jit(solution)/shard_map/ppermute | solution.py:512
  48.5 8.5 %collective-permute-start.18 = (f32[2,128,128]{2,1,0:T(8,128)S(1)}, f32[2,128,128]{2,1,0:T(8,128)S(1)}, u32[]{:S(2)}, u32[]{:S(2)}) collective-permute-start(f32[2,128,128]{2,1,0:T(8,128)S(1)} %get-tuple-element.111), channel_id=1, source_target_pairs={{0,8},{1,9},{2,10},{3,11},{4,12},{5,13},{6,14},{7,15},{8,0},{9,1},... | collective-permute-start | bytes 393224 | tf_op jit(solution)/shard_map/ppermute | solution.py:512
  63.2 7.5 %collective-permute-start.22 = (f32[8,136,128]{2,1,0:T(8,128)S(1)}, f32[8,136,128]{2,1,0:T(8,128)S(1)}, u32[]{:S(2)}, u32[]{:S(2)}) collective-permute-start(f32[8,136,128]{2,1,0:T(8,128)S(1)} %get-tuple-element.119), channel_id=1, source_target_pairs={{0,4},{1,5},{2,6},{3,7},{4,0},{5,1},{6,2},{7,3},{8,12},{9,13},{10,... | collective-permute-start | bytes 1671176 | tf_op jit(solution)/shard_map/ppermute | solution.py:508
  72.0 7.2 %collective-permute-start.24 = (f32[2,136,128]{2,1,0:T(8,128)S(1)}, f32[2,136,128]{2,1,0:T(8,128)S(1)}, u32[]{:S(2)}, u32[]{:S(2)}) collective-permute-start(f32[2,136,128]{2,1,0:T(8,128)S(1)} %get-tuple-element.122), channel_id=1, source_target_pairs={{0,2},{1,3},{2,0},{3,1},{4,6},{5,7},{6,4},{7,5},{8,10},{9,11},{10,... | collective-permute-start | bytes 417800 | tf_op jit(solution)/shard_map/ppermute | solution.py:512
  73.1 9.5 %collective-permute-start.25 = (f32[2,136,128]{2,1,0:T(8,128)S(1)}, f32[2,136,128]{2,1,0:T(8,128)S(1)}, u32[]{:S(2)}, u32[]{:S(2)}) collective-permute-start(f32[2,136,128]{2,1,0:T(8,128)S(1)} %get-tuple-element.123), channel_id=1, source_target_pairs={{0,3},{1,0},{2,1},{3,2},{4,5},{5,6},{6,7},{7,4},{8,11},{9,8},{10,9... | collective-permute-start | bytes 417800 | tf_op jit(solution)/shard_map/ppermute | solution.py:512
  73.1 9.5 %collective-permute-start.26 = (f32[2,136,128]{2,1,0:T(8,128)S(1)}, f32[2,136,128]{2,1,0:T(8,128)S(1)}, u32[]{:S(2)}, u32[]{:S(2)}) collective-permute-start(f32[2,136,128]{2,1,0:T(8,128)S(1)} %get-tuple-element.124), channel_id=1, source_target_pairs={{0,8},{1,9},{2,10},{3,11},{4,12},{5,13},{6,14},{7,15},{8,0},{9,1},... | collective-permute-start | bytes 417800 | tf_op jit(solution)/shard_map/ppermute | solution.py:512
  74.3 8.3 %collective-permute-start.27 = (f32[2,136,128]{2,1,0:T(8,128)S(1)}, f32[2,136,128]{2,1,0:T(8,128)S(1)}, u32[]{:S(2)}, u32[]{:S(2)}) collective-permute-start(f32[2,136,128]{2,1,0:T(8,128)S(1)} %get-tuple-element.125), channel_id=1, source_target_pairs={{0,9},{1,10},{2,11},{3,8},{4,15},{5,12},{6,13},{7,14},{8,1},{9,2},... | collective-permute-start | bytes 417800 | tf_op jit(solution)/shard_map/ppermute | solution.py:512
  77.0 9.0 %collective-permute-start.28 = (f32[2,136,128]{2,1,0:T(8,128)S(1)}, f32[2,136,128]{2,1,0:T(8,128)S(1)}, u32[]{:S(2)}, u32[]{:S(2)}) collective-permute-start(f32[2,136,128]{2,1,0:T(8,128)S(1)} %get-tuple-element.126), channel_id=1, source_target_pairs={{0,10},{1,11},{2,8},{3,9},{4,14},{5,15},{6,12},{7,13},{8,2},{9,3},... | collective-permute-start | bytes 417800 | tf_op jit(solution)/shard_map/ppermute | solution.py:512
  79.2 8.6 %collective-permute-start.29 = (f32[2,136,128]{2,1,0:T(8,128)S(1)}, f32[2,136,128]{2,1,0:T(8,128)S(1)}, u32[]{:S(2)}, u32[]{:S(2)}) collective-permute-start(f32[2,136,128]{2,1,0:T(8,128)S(1)} %get-tuple-element.127), channel_id=1, source_target_pairs={{0,11},{1,8},{2,9},{3,10},{4,13},{5,14},{6,15},{7,12},{8,3},{9,0},... | collective-permute-start | bytes 417800 | tf_op jit(solution)/shard_map/ppermute | solution.py:512
  (9 other events, 94.8 us)

commit v7 on v5

--- a/solution.py
+++ b/solution.py
@@ -25,11 +25,12 @@
 ORDER = (6, 5, 7, 4, 2, 1, 3)
 
 
-def call(kernel, out, scratch, limit, flops, ins):
+def call(kernel, out, scratch, limit, flops, ins, outs=None):
     return pl.pallas_call(
         kernel,
         out_shape=out,
         in_specs=ins,
+        **({} if outs is None else {"out_specs": outs}),
         scratch_shapes=scratch,
         compiler_params=pltpu.CompilerParams(vmem_limit_bytes=limit * MIB),
         cost_estimate=pl.CostEstimate(flops=flops, bytes_accessed=4 * MIB, transcendentals=0),
@@ -391,7 +392,7 @@
 
 def peaks_kernel(bins_ref, device_ref, *refs):
     got, table, offsets_ref, refs = refs[:8], pairs(refs[8:18]), refs[18], refs[19:]
-    snr_ref, heights_ref, counts_ref, field_ref, wide_ref, side_ref, pick_ref, x_ref = refs
+    snr_ref, heights_ref, counts_ref, field_ref, wide_ref, side_ref, pick_ref, x_ref, own_ref, sem = refs
     for index in range(8):
         there = other_chip(device_ref[0], (index & 4) | (-index & 3))
         x_ref[there] = got[index][0]
@@ -412,7 +413,7 @@
     inverse = 1.0 / jnp.sqrt(mean + 1e-06)
     for c, value in enumerate(back(values, 1)):
         cols = pl.ds(INNER * c, INNER)
-        snr_ref[:, cols] = value[0:ROWS] * inverse
+        own_ref[:, cols] = value[0:ROWS] * inverse
         field_ref[8 : ROWS + 8, cols] = value[0:ROWS]
         field_ref[7:8, cols] = value[ROWS : ROWS + 1]
         field_ref[ROWS + 8 : ROWS + 9, cols] = value[ROWS + 1 : ROWS + 2]
@@ -422,7 +423,12 @@
         side = jnp.maximum(pltpu.roll(value, 1, 1), pltpu.roll(value, N - 1, 1))
         wide_ref[start : start + size, :] = jnp.maximum(side, value)
         side_ref[start : start + size, :] = side
-    blocks = iota((LANES, N), 1) // CELL == iota((LANES, N), 0)
+    copies = []
+    for part in range(8):
+        rows = pl.ds(CELL * part, CELL)
+        copies.append(pltpu.make_async_copy(own_ref.at[rows], snr_ref.at[rows], sem.at[part]))
+        copies[-1].start()
+    blocks = lax.shift_right_logical(iota((LANES, N), 1), 4) == iota((LANES, N), 0)
     blocks = jnp.where(blocks, 1.0, 0.0).astype(jnp.bfloat16)
     offsets = offsets_ref[...].astype(jnp.float32).astype(jnp.bfloat16)
     offsets = jnp.concatenate([offsets, offsets], axis=0)
@@ -435,17 +441,20 @@
         below = wide_ref[base + 1 : base + 1 + CELL, :]
         nearest = jnp.maximum(side, jnp.maximum(above, below))
         chosen = spread[p : p + 1, :] == code
-        height = jnp.sum(jnp.where(chosen, value - nearest, 0.0), axis=0, keepdims=True)
-        level = jnp.sum(jnp.where(chosen, value, 0.0), axis=0, keepdims=True)
-        pick_ref[p : p + 1, :] = height
-        pick_ref[8 + p : 9 + p, :] = level
+        height = jnp.where(chosen, value - nearest, 0.0)
+        level = jnp.where(chosen, value, 0.0)
+        pick_ref[8 * p : 8 * p + 8, :] = height[0:8] + height[8:16]
+        pick_ref[HALF + 8 * p : HALF + 8 * p + 8, :] = level[0:8] + level[8:16]
     high, low = split(pick_ref[...])
     gather = partial(
         lax.dot_general,
         dimension_numbers=(((1,), (1,)), ((), ())),
         preferred_element_type=jnp.float32,
     )
-    picked = (gather(high, blocks) + gather(low, blocks)) * inverse
+    both = gather(jnp.concatenate([high, low], axis=0), blocks)
+    both = both[0:LANES] + both[LANES : 2 * LANES]
+    rows = [jnp.sum(both[8 * p : 8 * p + 8], axis=0, keepdims=True) for p in range(16)]
+    picked = jnp.concatenate(rows, axis=0) * inverse
     heights, values = picked[0:8], picked[8:16]
     heights_ref[...] = heights
     weight = jax.nn.sigmoid(heights * 20.0)
@@ -458,6 +467,8 @@
         counts = counts + jnp.where(lane == k, summed, 0.0)
     for s in range(DEV):
         counts_ref[s] = jnp.broadcast_to(counts, (8, LANES))
+    for copy in copies:
+        copy.wait()
 
 
 def peak_pass(thresholds, device, x, table, offsets):
@@ -471,12 +482,32 @@
         pltpu.VMEM((ROWS + 16, N), f32),
         pltpu.VMEM((ROWS + 16, N), f32),
         pltpu.VMEM((ROWS + 16, N), f32),
-        pltpu.VMEM((16, N), f32),
+        pltpu.VMEM((LANES, N), f32),
         pltpu.VMEM((DEV, BLOCK, LANES), f32),
+        pltpu.VMEM((ROWS, N), f32),
+        pltpu.SemaphoreType.DMA((8,)),
     ]
     specs = [pl.BlockSpec(memory_space=pltpu.SMEM)] * 2 + [pl.BlockSpec(memory_space=pltpu.VMEM)] * 19
-    run = call(peaks_kernel, out, scratch, LIMIT[4], 2 * 10**9, specs)
+    places = [pl.BlockSpec(memory_space=pl.ANY)] + [pl.BlockSpec(memory_space=pltpu.VMEM)] * 2
+    run = call(peaks_kernel, out, scratch, LIMIT[4], 2 * 10**9, specs, places)
     return run(thresholds, device, *x, *table, offsets)
+
+
+def finish_kernel(counts_ref, heights_ref, total_ref, out_ref):
+    total = counts_ref[0]
+    for s in range(1, DEV):
+        total = total + counts_ref[s]
+    total_ref[...] = total[0:1, 0:16]
+    out_ref[...] = heights_ref[...]
+
+
+def finish(counts, heights):
+    out = [
+        jax.ShapeDtypeStruct((1, 16), jnp.float32),
+        jax.ShapeDtypeStruct((8, LANES), jnp.float32),
+    ]
+    specs = [pl.BlockSpec(memory_space=pltpu.VMEM)] * 2
+    return call(finish_kernel, out, (), 4, 10**6, specs)(counts, heights)
 
 
 def chip_pairs(index):
@@ -515,8 +546,8 @@
     k = row_pass(device, one, two, sample, frequency, factors)
     out = peak_pass(thresholds, device, scatter(*k), frequency, offsets[0])
     snr, heights, counts = out
-    counts = exchange(counts)
-    return snr[None], heights[None], jnp.sum(counts[:, 0:1, 0:16], axis=0)
+    counts, heights = finish(exchange(counts), heights)
+    return snr[None], heights[None], counts
 
 
 def solution(mesh):

time: 105 us -> 105 us (level)
  no operation moved by 1% of the time
where the time goes in v7:
time: 105 us; the launch traced here: 104 us
  waiting for transfers between devices  41.3 us (39%)
  starting transfers between devices  32.1 us (31%)
  Pallas kernels  15.5 us (15%)
  blocking collectives  12.5 us (12%)
  local copies, waits for them, and re-layouts  1.59 us (2%)
  between operations  1.42 us (1%)
    ppermute x21, waiting for transfers between devices, scatter(): done.append((index, lax.ppermute(blocks[index], group, chip_pairs(index))))  25.3 us
    ppermute x21, starting transfers between devices, scatter(): done.append((index, lax.ppermute(blocks[index], group, chip_pairs(index))))  17.2 us
    ppermute x6, waiting for transfers between devices, body(): got[4 - step] = lax.ppermute(blocks[4 * field + step], 'col', pairs)  14.4 us
    all_to_all x1, blocking collectives, exchange(): return lax.all_to_all(x, group, split_axis=0, concat_axis=0, tiled=True)  12.5 us
    ppermute x6, starting transfers between devices, body(): got[4 - step] = lax.ppermute(blocks[4 * field + step], 'col', pairs)  7.81 us
    ppermute x3, starting transfers between devices, scatter(): got = lax.ppermute(send, group, [(d, d ^ 4) for d in range(DEV)])  7.12 us
    pallas_call x1, Pallas kernels, tables(): call(tables_kernel, out, scratch, LIMIT[0], 10 ** 9, [smem, smem])  4.45 us
    pallas_call x1, Pallas kernels, peak_pass(): return run(thresholds, device, *x, *table, offsets)  4.06 us
  transfers between devices with their start and end apart: 30, of which 15 were waited for; matrix products, arithmetic and copies ran while one was open for 0% of the time, Pallas kernels for 8%

profile of v7, /device:TPU:1, one launch (start us, length us, event | category | flops | bytes accessed | tf_op | source)
XLA Modules:
  0.0 104.4 jit_solution(2445367211085328704)
XLA Ops:
  0.6 1.6 %copy-done = f32[2,1,512,512]{3,2,1,0:T(8,128)S(1)} copy-done((f32[2,1,512,512]{3,2,1,0:T(8,128)S(1)}, f32[2,1,512,512]{3,2,1,0:T(8,128)}, u32[]{:S(2)}) %copy-start) | copy-done | bytes 2097176
  2.4 3.4 %collective-permute-start = (f32[128,512]{1,0:T(8,128)S(1)}, f32[128,512]{1,0:T(8,128)S(1)}, u32[]{:S(2)}, u32[]{:S(2)}) collective-permute-start(f32[128,512]{1,0:T(8,128)S(1)} %get-tuple-element.70), channel_id=1, source_target_pairs={{0,3},{1,0},{2,1},{3,2},{4,7},{5,4},{6,5},{7,6},{8,11},{9,8},{10,9... | collective-permute-start | bytes 786440 | tf_op jit(solution)/shard_map/ppermute | solution.py:538
  6.9 2.1 %collective-permute-start.11 = (f32[128,512]{1,0:T(8,128)S(1)}, f32[128,512]{1,0:T(8,128)S(1)}, u32[]{:S(2)}, u32[]{:S(2)}) collective-permute-start(f32[128,512]{1,0:T(8,128)S(1)} %get-tuple-element.104), channel_id=1, source_target_pairs={{0,3},{1,0},{2,1},{3,2},{4,7},{5,4},{6,5},{7,6},{8,11},{9,8},{10,9... | collective-permute-start | bytes 786440 | tf_op jit(solution)/shard_map/ppermute | solution.py:538
  10.8 2.6 %collective-permute-done.refs_1_ = f32[128,512]{1,0:T(8,128)S(1)} collective-permute-done((f32[128,512]{1,0:T(8,128)S(1)}, f32[128,512]{1,0:T(8,128)S(1)}, u32[]{:S(2)}, u32[]{:S(2)}) %collective-permute-start) | collective-permute-done | bytes 262176 | tf_op jit(solution)/shard_map/ppermute | solution.py:538
  13.4 4.4 %shard_map.68 = (bf16[256,256]{1,0:T(8,128)(2,1)S(1)}, bf16[256,256]{1,0:T(8,128)(2,1)S(1)}, bf16[256,256]{1,0:T(8,128)(2,1)S(1)}, bf16[256,256]{1,0:T(8,128)(2,...) custom-call(f32[1]{0:T(128)S(6)} %copy.7.smooth_ref, ...), custom_call_target="tpu_custom_call" | custom-call | flops 1000000000 | bytes 4194304 | tf_op jit(solution)/shard_map/pallas_call | solution.py:226
  17.9 4.5 %collective-permute-done.2.refs_3_ = f32[128,512]{1,0:T(8,128)S(1)} collective-permute-done((f32[128,512]{1,0:T(8,128)S(1)}, f32[128,512]{1,0:T(8,128)S(1)}, u32[]{:S(2)}, u32[]{:S(2)}) %collective-permute-start.2) | collective-permute-done | bytes 262176 | tf_op jit(solution)/shard_map/ppermute | solution.py:538
  24.9 2.5 %collective-permute-done.11.refs_1_ = f32[128,512]{1,0:T(8,128)S(1)} collective-permute-done((f32[128,512]{1,0:T(8,128)S(1)}, f32[128,512]{1,0:T(8,128)S(1)}, u32[]{:S(2)}, u32[]{:S(2)}) %collective-permute-start.11) | collective-permute-done | bytes 262176 | tf_op jit(solution)/shard_map/ppermute | solution.py:538
  27.4 4.8 %collective-permute-done.13.refs_3_ = f32[128,512]{1,0:T(8,128)S(1)} collective-permute-done((f32[128,512]{1,0:T(8,128)S(1)}, f32[128,512]{1,0:T(8,128)S(1)}, u32[]{:S(2)}, u32[]{:S(2)}) %collective-permute-start.13) | collective-permute-done | bytes 262176 | tf_op jit(solution)/shard_map/ppermute | solution.py:538
  34.3 1.5 %collective-permute-start.5 = (f32[2,128,128]{2,1,0:T(8,128)S(1)}, f32[2,128,128]{2,1,0:T(8,128)S(1)}, u32[]{:S(2)}, u32[]{:S(2)}) collective-permute-start(f32[2,128,128]{2,1,0:T(8,128)S(1)} %get-tuple-element.87), channel_id=1, source_target_pairs={{0,2},{1,3},{2,0},{3,1},{4,6},{5,7},{6,4},{7,5},{8,10},{9,11},{10,... | collective-permute-start | bytes 393224 | tf_op jit(solution)/shard_map/ppermute | solution.py:529
  38.9 4.5 %collective-permute-done.4.refs_1_ = f32[2,128,128]{2,1,0:T(8,128)S(1)} collective-permute-done((f32[2,128,128]{2,1,0:T(8,128)S(1)}, f32[2,128,128]{2,1,0:T(8,128)S(1)}, u32[]{:S(2)}, u32[]{:S(2)}) %collective-permute-start.4) | collective-permute-done | bytes 131104 | tf_op jit(solution)/shard_map/ppermute | solution.py:529
  44.3 1.5 %collective-permute-start.15 = (f32[2,128,128]{2,1,0:T(8,128)S(1)}, f32[2,128,128]{2,1,0:T(8,128)S(1)}, u32[]{:S(2)}, u32[]{:S(2)}) collective-permute-start(f32[2,128,128]{2,1,0:T(8,128)S(1)} %get-tuple-element.110), channel_id=1, source_target_pairs={{0,1},{1,2},{2,3},{3,0},{4,5},{5,6},{6,7},{7,4},{8,9},{9,10},{10,1... | collective-permute-start | bytes 393224 | tf_op jit(solution)/shard_map/ppermute | solution.py:529
  45.9 2.9 %collective-permute-start.16 = (f32[2,128,128]{2,1,0:T(8,128)S(1)}, f32[2,128,128]{2,1,0:T(8,128)S(1)}, u32[]{:S(2)}, u32[]{:S(2)}) collective-permute-start(f32[2,128,128]{2,1,0:T(8,128)S(1)} %get-tuple-element.111), channel_id=1, source_target_pairs={{0,2},{1,3},{2,0},{3,1},{4,6},{5,7},{6,4},{7,5},{8,10},{9,11},{10,... | collective-permute-start | bytes 393224 | tf_op jit(solution)/shard_map/ppermute | solution.py:529
  51.6 3.1 %collective-permute-done.15.refs_1_ = f32[2,128,128]{2,1,0:T(8,128)S(1)} collective-permute-done((f32[2,128,128]{2,1,0:T(8,128)S(1)}, f32[2,128,128]{2,1,0:T(8,128)S(1)}, u32[]{:S(2)}, u32[]{:S(2)}) %collective-permute-start.15) | collective-permute-done | bytes 131104 | tf_op jit(solution)/shard_map/ppermute | solution.py:529
  56.9 2.0 %collective-permute-done.19.refs_5_ = f32[2,128,128]{2,1,0:T(8,128)S(1)} collective-permute-done((f32[2,128,128]{2,1,0:T(8,128)S(1)}, f32[2,128,128]{2,1,0:T(8,128)S(1)}, u32[]{:S(2)}, u32[]{:S(2)}) %collective-permute-start.19) | collective-permute-done | bytes 131104 | tf_op jit(solution)/shard_map/ppermute | solution.py:529
  58.9 3.3 %collective-permute-done.20.refs_6_ = f32[2,128,128]{2,1,0:T(8,128)S(1)} collective-permute-done((f32[2,128,128]{2,1,0:T(8,128)S(1)}, f32[2,128,128]{2,1,0:T(8,128)S(1)}, u32[]{:S(2)}, u32[]{:S(2)}) %collective-permute-start.20) | collective-permute-done | bytes 131104 | tf_op jit(solution)/shard_map/ppermute | solution.py:529
  62.2 2.6 %shard_map.74 = (f32[8,136,128]{2,1,0:T(8,128)S(1)}, f32[8,136,128]{2,1,0:T(8,128)S(1)}) custom-call(s32[1]{0:T(128)} %bitcast.device_ref, f32[2048,128]{1,0:T(8,128)S(1)} %shard_map.71.one_ref, f32[2,128,128]{2,1,0:T(8,128)S(1)} %get-tuple-element.109.refs_0_, f32[2,128,128]{2,1,0:T(8,128)S(1)} %collective-permute-done.15.refs_1_, ...), custom_call_target="tpu_custom_call" | custom-call | flops 3000000000 | bytes 4194304 | tf_op jit(solution)/shard_map/pallas_call | solution.py:390
  64.8 4.9 %collective-permute-start.22 = (f32[8,136,128]{2,1,0:T(8,128)S(1)}, f32[8,136,128]{2,1,0:T(8,128)S(1)}, u32[]{:S(2)}, u32[]{:S(2)}) collective-permute-start(f32[8,136,128]{2,1,0:T(8,128)S(1)} %get-tuple-element.121), channel_id=1, source_target_pairs={{0,4},{1,5},{2,6},{3,7},{4,0},{5,1},{6,2},{7,3},{8,12},{9,13},{10,... | collective-permute-start | bytes 1671176 | tf_op jit(solution)/shard_map/ppermute | solution.py:525
  69.7 1.6 %collective-permute-done.22.got_ref = f32[8,136,128]{2,1,0:T(8,128)S(1)} collective-permute-done((f32[8,136,128]{2,1,0:T(8,128)S(1)}, f32[8,136,128]{2,1,0:T(8,128)S(1)}, u32[]{:S(2)}, u32[]{:S(2)}) %collective-permute-start.22) | collective-permute-done | bytes 557088 | tf_op jit(solution)/shard_map/ppermute | solution.py:525
  72.5 1.5 %collective-permute-start.25 = (f32[2,136,128]{2,1,0:T(8,128)S(1)}, f32[2,136,128]{2,1,0:T(8,128)S(1)}, u32[]{:S(2)}, u32[]{:S(2)}) collective-permute-start(f32[2,136,128]{2,1,0:T(8,128)S(1)} %get-tuple-element.125), channel_id=1, source_target_pairs={{0,3},{1,0},{2,1},{3,2},{4,7},{5,4},{6,5},{7,6},{8,11},{9,8},{10,9... | collective-permute-start | bytes 417800 | tf_op jit(solution)/shard_map/ppermute | solution.py:529
  75.8 4.6 %collective-permute-done.23.refs_1_ = f32[2,136,128]{2,1,0:T(8,128)S(1)} collective-permute-done((f32[2,136,128]{2,1,0:T(8,128)S(1)}, f32[2,136,128]{2,1,0:T(8,128)S(1)}, u32[]{:S(2)}, u32[]{:S(2)}) %collective-permute-start.23) | collective-permute-done | bytes 139296 | tf_op jit(solution)/shard_map/ppermute | solution.py:529
  80.8 3.0 %collective-permute-done.27.refs_5_ = f32[2,136,128]{2,1,0:T(8,128)S(1)} collective-permute-done((f32[2,136,128]{2,1,0:T(8,128)S(1)}, f32[2,136,128]{2,1,0:T(8,128)S(1)}, u32[]{:S(2)}, u32[]{:S(2)}) %collective-permute-start.27) | collective-permute-done | bytes 139296 | tf_op jit(solution)/shard_map/ppermute | solution.py:529
  83.9 3.4 %collective-permute-done.28.refs_6_ = f32[2,136,128]{2,1,0:T(8,128)S(1)} collective-permute-done((f32[2,136,128]{2,1,0:T(8,128)S(1)}, f32[2,136,128]{2,1,0:T(8,128)S(1)}, u32[]{:S(2)}, u32[]{:S(2)}) %collective-permute-start.28) | collective-permute-done | bytes 139296 | tf_op jit(solution)/shard_map/ppermute | solution.py:529
  87.3 4.1 %shard_map.76 = (f32[128,2048]{1,0:T(8,128)}, f32[8,128]{1,0:T(8,128)S(1)}, f32[16,8,128]{2,1,0:T(8,128)S(1)}) custom-call(s32[1,16]{1,0:T(1,128)S(1)} %copy-done.2, s32[1]{0:T(128)} %bitcast.device_ref, f32[2,136,128]{2,1,0:T(8,128)S(1)} %get-tuple-element.122.refs_0_, f32[2,136,128]{2,1,0:T(8,128)S(1)} %collective-permute-done.23.refs_1_, ...), custom_call_target="tpu_custom_call" | custom-call | flops 2000000000 | bytes 4194304 | tf_op jit(solution)/shard_map/pallas_call | solution.py:493
  91.3 12.5 %all_to_all.5.counts_ref = f32[16,8,128]{2,1,0:T(8,128)S(1)} all-to-all(f32[16,8,128]{2,1,0:T(8,128)S(1)} %get-tuple-element.131), channel_id=1, replica_groups=mesh['maps'=16,'row'=4,'col'=4] {'row','col'}, dimensions={0} | all-to-all | bytes 131072 | tf_op jit(solution)/shard_map/all_to_all | solution.py:522
  (54 shorter events, 20.0 us)
Async XLA Ops:
  2.4 11.0 %collective-permute-start = (f32[128,512]{1,0:T(8,128)S(1)}, f32[128,512]{1,0:T(8,128)S(1)}, u32[]{:S(2)}, u32[]{:S(2)}) collective-permute-start(f32[128,512]{1,0:T(8,128)S(1)} %get-tuple-element.70), channel_id=1, source_target_pairs={{0,3},{1,0},{2,1},{3,2},{4,7},{5,4},{6,5},{7,6},{8,11},{9,8},{10,9... | collective-permute-start | bytes 786440 | tf_op jit(solution)/shard_map/ppermute | solution.py:538
  5.7 12.1 %collective-permute-start.1 = (f32[128,512]{1,0:T(8,128)S(1)}, f32[128,512]{1,0:T(8,128)S(1)}, u32[]{:S(2)}, u32[]{:S(2)}) collective-permute-start(f32[128,512]{1,0:T(8,128)S(1)} %get-tuple-element.71), channel_id=1, source_target_pairs={{0,2},{1,3},{2,0},{3,1},{4,6},{5,7},{6,4},{7,5},{8,10},{9,11},{10,... | collective-permute-start | bytes 786440 | tf_op jit(solution)/shard_map/ppermute | solution.py:538
  6.3 16.1 %collective-permute-start.2 = (f32[128,512]{1,0:T(8,128)S(1)}, f32[128,512]{1,0:T(8,128)S(1)}, u32[]{:S(2)}, u32[]{:S(2)}) collective-permute-start(f32[128,512]{1,0:T(8,128)S(1)} %get-tuple-element.72), channel_id=1, source_target_pairs={{0,1},{1,2},{2,3},{3,0},{4,5},{5,6},{6,7},{7,4},{8,9},{9,10},{10,1... | collective-permute-start | bytes 786440 | tf_op jit(solution)/shard_map/ppermute | solution.py:538
  6.9 20.6 %collective-permute-start.11 = (f32[128,512]{1,0:T(8,128)S(1)}, f32[128,512]{1,0:T(8,128)S(1)}, u32[]{:S(2)}, u32[]{:S(2)}) collective-permute-start(f32[128,512]{1,0:T(8,128)S(1)} %get-tuple-element.104), channel_id=1, source_target_pairs={{0,3},{1,0},{2,1},{3,2},{4,7},{5,4},{6,5},{7,6},{8,11},{9,8},{10,9... | collective-permute-start | bytes 786440 | tf_op jit(solution)/shard_map/ppermute | solution.py:538
  8.9 18.5 %collective-permute-start.12 = (f32[128,512]{1,0:T(8,128)S(1)}, f32[128,512]{1,0:T(8,128)S(1)}, u32[]{:S(2)}, u32[]{:S(2)}) collective-permute-start(f32[128,512]{1,0:T(8,128)S(1)} %get-tuple-element.105), channel_id=1, source_target_pairs={{0,2},{1,3},{2,0},{3,1},{4,6},{5,7},{6,4},{7,5},{8,10},{9,11},{10,... | collective-permute-start | bytes 786440 | tf_op jit(solution)/shard_map/ppermute | solution.py:538
  13.4 18.9 %collective-permute-start.13 = (f32[128,512]{1,0:T(8,128)S(1)}, f32[128,512]{1,0:T(8,128)S(1)}, u32[]{:S(2)}, u32[]{:S(2)}) collective-permute-start(f32[128,512]{1,0:T(8,128)S(1)} %get-tuple-element.106), channel_id=1, source_target_pairs={{0,1},{1,2},{2,3},{3,0},{4,5},{5,6},{6,7},{7,4},{8,9},{9,10},{10,1... | collective-permute-start | bytes 786440 | tf_op jit(solution)/shard_map/ppermute | solution.py:538
  23.5 10.7 %collective-permute-start.3 = (f32[8,128,128]{2,1,0:T(8,128)S(1)}, f32[8,128,128]{2,1,0:T(8,128)S(1)}, u32[]{:S(2)}, u32[]{:S(2)}) collective-permute-start(f32[8,128,128]{2,1,0:T(8,128)S(1)} %get-tuple-element.84), channel_id=1, source_target_pairs={{0,4},{1,5},{2,6},{3,7},{4,0},{5,1},{6,2},{7,3},{8,12},{9,13},{10,... | collective-permute-start | bytes 1572872 | tf_op jit(solution)/shard_map/ppermute | solution.py:525
  34.3 9.1 %collective-permute-start.4 = (f32[2,128,128]{2,1,0:T(8,128)S(1)}, f32[2,128,128]{2,1,0:T(8,128)S(1)}, u32[]{:S(2)}, u32[]{:S(2)}) collective-permute-start(f32[2,128,128]{2,1,0:T(8,128)S(1)} %get-tuple-element.86), channel_id=1, source_target_pairs={{0,1},{1,2},{2,3},{3,0},{4,5},{5,6},{6,7},{7,4},{8,9},{9,10},{10,1... | collective-permute-start | bytes 393224 | tf_op jit(solution)/shard_map/ppermute | solution.py:529
  34.3 9.0 %collective-permute-start.5 = (f32[2,128,128]{2,1,0:T(8,128)S(1)}, f32[2,128,128]{2,1,0:T(8,128)S(1)}, u32[]{:S(2)}, u32[]{:S(2)}) collective-permute-start(f32[2,128,128]{2,1,0:T(8,128)S(1)} %get-tuple-element.87), channel_id=1, source_target_pairs={{0,2},{1,3},{2,0},{3,1},{4,6},{5,7},{6,4},{7,5},{8,10},{9,11},{10,... | collective-permute-start | bytes 393224 | tf_op jit(solution)/shard_map/ppermute | solution.py:529
  35.9 8.4 %collective-permute-start.6 = (f32[2,128,128]{2,1,0:T(8,128)S(1)}, f32[2,128,128]{2,1,0:T(8,128)S(1)}, u32[]{:S(2)}, u32[]{:S(2)}) collective-permute-start(f32[2,128,128]{2,1,0:T(8,128)S(1)} %get-tuple-element.88), channel_id=1, source_target_pairs={{0,3},{1,0},{2,1},{3,2},{4,7},{5,4},{6,5},{7,6},{8,11},{9,8},{10,9... | collective-permute-start | bytes 393224 | tf_op jit(solution)/shard_map/ppermute | solution.py:529
  37.0 8.9 %collective-permute-start.7 = (f32[2,128,128]{2,1,0:T(8,128)S(1)}, f32[2,128,128]{2,1,0:T(8,128)S(1)}, u32[]{:S(2)}, u32[]{:S(2)}) collective-permute-start(f32[2,128,128]{2,1,0:T(8,128)S(1)} %get-tuple-element.89), channel_id=1, source_target_pairs={{0,8},{1,9},{2,10},{3,11},{4,12},{5,13},{6,14},{7,15},{8,0},{9,1},... | collective-permute-start | bytes 393224 | tf_op jit(solution)/shard_map/ppermute | solution.py:529
  38.3 10.4 %collective-permute-start.8 = (f32[2,128,128]{2,1,0:T(8,128)S(1)}, f32[2,128,128]{2,1,0:T(8,128)S(1)}, u32[]{:S(2)}, u32[]{:S(2)}) collective-permute-start(f32[2,128,128]{2,1,0:T(8,128)S(1)} %get-tuple-element.90), channel_id=1, source_target_pairs={{0,9},{1,10},{2,11},{3,8},{4,13},{5,14},{6,15},{7,12},{8,1},{9,2},... | collective-permute-start | bytes 393224 | tf_op jit(solution)/shard_map/ppermute | solution.py:529
  43.4 6.9 %collective-permute-start.9 = (f32[2,128,128]{2,1,0:T(8,128)S(1)}, f32[2,128,128]{2,1,0:T(8,128)S(1)}, u32[]{:S(2)}, u32[]{:S(2)}) collective-permute-start(f32[2,128,128]{2,1,0:T(8,128)S(1)} %get-tuple-element.91), channel_id=1, source_target_pairs={{0,10},{1,11},{2,8},{3,9},{4,14},{5,15},{6,12},{7,13},{8,2},{9,3},... | collective-permute-start | bytes 393224 | tf_op jit(solution)/shard_map/ppermute | solution.py:529
  43.4 8.2 %collective-permute-start.10 = (f32[2,128,128]{2,1,0:T(8,128)S(1)}, f32[2,128,128]{2,1,0:T(8,128)S(1)}, u32[]{:S(2)}, u32[]{:S(2)}) collective-permute-start(f32[2,128,128]{2,1,0:T(8,128)S(1)} %get-tuple-element.92), channel_id=1, source_target_pairs={{0,11},{1,8},{2,9},{3,10},{4,15},{5,12},{6,13},{7,14},{8,3},{9,0},... | collective-permute-start | bytes 393224 | tf_op jit(solution)/shard_map/ppermute | solution.py:529
  44.3 10.4 %collective-permute-start.15 = (f32[2,128,128]{2,1,0:T(8,128)S(1)}, f32[2,128,128]{2,1,0:T(8,128)S(1)}, u32[]{:S(2)}, u32[]{:S(2)}) collective-permute-start(f32[2,128,128]{2,1,0:T(8,128)S(1)} %get-tuple-element.110), channel_id=1, source_target_pairs={{0,1},{1,2},{2,3},{3,0},{4,5},{5,6},{6,7},{7,4},{8,9},{9,10},{10,1... | collective-permute-start | bytes 393224 | tf_op jit(solution)/shard_map/ppermute | solution.py:529
  45.9 9.0 %collective-permute-start.16 = (f32[2,128,128]{2,1,0:T(8,128)S(1)}, f32[2,128,128]{2,1,0:T(8,128)S(1)}, u32[]{:S(2)}, u32[]{:S(2)}) collective-permute-start(f32[2,128,128]{2,1,0:T(8,128)S(1)} %get-tuple-element.111), channel_id=1, source_target_pairs={{0,2},{1,3},{2,0},{3,1},{4,6},{5,7},{6,4},{7,5},{8,10},{9,11},{10,... | collective-permute-start | bytes 393224 | tf_op jit(solution)/shard_map/ppermute | solution.py:529
  48.7 8.1 %collective-permute-start.17 = (f32[2,128,128]{2,1,0:T(8,128)S(1)}, f32[2,128,128]{2,1,0:T(8,128)S(1)}, u32[]{:S(2)}, u32[]{:S(2)}) collective-permute-start(f32[2,128,128]{2,1,0:T(8,128)S(1)} %get-tuple-element.112), channel_id=1, source_target_pairs={{0,3},{1,0},{2,1},{3,2},{4,7},{5,4},{6,5},{7,6},{8,11},{9,8},{10,9... | collective-permute-start | bytes 393224 | tf_op jit(solution)/shard_map/ppermute | solution.py:529
  51.6 7.3 %collective-permute-start.19 = (f32[2,128,128]{2,1,0:T(8,128)S(1)}, f32[2,128,128]{2,1,0:T(8,128)S(1)}, u32[]{:S(2)}, u32[]{:S(2)}) collective-permute-start(f32[2,128,128]{2,1,0:T(8,128)S(1)} %get-tuple-element.114), channel_id=1, source_target_pairs={{0,9},{1,10},{2,11},{3,8},{4,13},{5,14},{6,15},{7,12},{8,1},{9,2},... | collective-permute-start | bytes 393224 | tf_op jit(solution)/shard_map/ppermute | solution.py:529
  54.7 7.5 %collective-permute-start.20 = (f32[2,128,128]{2,1,0:T(8,128)S(1)}, f32[2,128,128]{2,1,0:T(8,128)S(1)}, u32[]{:S(2)}, u32[]{:S(2)}) collective-permute-start(f32[2,128,128]{2,1,0:T(8,128)S(1)} %get-tuple-element.115), channel_id=1, source_target_pairs={{0,10},{1,11},{2,8},{3,9},{4,14},{5,15},{6,12},{7,13},{8,2},{9,3},... | collective-permute-start | bytes 393224 | tf_op jit(solution)/shard_map/ppermute | solution.py:529
  54.9 7.3 %collective-permute-start.21 = (f32[2,128,128]{2,1,0:T(8,128)S(1)}, f32[2,128,128]{2,1,0:T(8,128)S(1)}, u32[]{:S(2)}, u32[]{:S(2)}) collective-permute-start(f32[2,128,128]{2,1,0:T(8,128)S(1)} %get-tuple-element.116), channel_id=1, source_target_pairs={{0,11},{1,8},{2,9},{3,10},{4,15},{5,12},{6,13},{7,14},{8,3},{9,0},... | collective-permute-start | bytes 393224 | tf_op jit(solution)/shard_map/ppermute | solution.py:529
  71.3 9.2 %collective-permute-start.23 = (f32[2,136,128]{2,1,0:T(8,128)S(1)}, f32[2,136,128]{2,1,0:T(8,128)S(1)}, u32[]{:S(2)}, u32[]{:S(2)}) collective-permute-start(f32[2,136,128]{2,1,0:T(8,128)S(1)} %get-tuple-element.123), channel_id=1, source_target_pairs={{0,1},{1,2},{2,3},{3,0},{4,5},{5,6},{6,7},{7,4},{8,9},{9,10},{10,1... | collective-permute-start | bytes 417800 | tf_op jit(solution)/shard_map/ppermute | solution.py:529
  71.4 9.1 %collective-permute-start.24 = (f32[2,136,128]{2,1,0:T(8,128)S(1)}, f32[2,136,128]{2,1,0:T(8,128)S(1)}, u32[]{:S(2)}, u32[]{:S(2)}) collective-permute-start(f32[2,136,128]{2,1,0:T(8,128)S(1)} %get-tuple-element.124), channel_id=1, source_target_pairs={{0,2},{1,3},{2,0},{3,1},{4,6},{5,7},{6,4},{7,5},{8,10},{9,11},{10,... | collective-permute-start | bytes 417800 | tf_op jit(solution)/shard_map/ppermute | solution.py:529
  72.5 8.3 %collective-permute-start.25 = (f32[2,136,128]{2,1,0:T(8,128)S(1)}, f32[2,136,128]{2,1,0:T(8,128)S(1)}, u32[]{:S(2)}, u32[]{:S(2)}) collective-permute-start(f32[2,136,128]{2,1,0:T(8,128)S(1)} %get-tuple-element.125), channel_id=1, source_target_pairs={{0,3},{1,0},{2,1},{3,2},{4,7},{5,4},{6,5},{7,6},{8,11},{9,8},{10,9... | collective-permute-start | bytes 417800 | tf_op jit(solution)/shard_map/ppermute | solution.py:529
  74.7 9.2 %collective-permute-start.27 = (f32[2,136,128]{2,1,0:T(8,128)S(1)}, f32[2,136,128]{2,1,0:T(8,128)S(1)}, u32[]{:S(2)}, u32[]{:S(2)}) collective-permute-start(f32[2,136,128]{2,1,0:T(8,128)S(1)} %get-tuple-element.127), channel_id=1, source_target_pairs={{0,9},{1,10},{2,11},{3,8},{4,13},{5,14},{6,15},{7,12},{8,1},{9,2},... | collective-permute-start | bytes 417800 | tf_op jit(solution)/shard_map/ppermute | solution.py:529
  (9 other events, 90.0 us)

commit v8 on v7

--- a/solution.py
+++ b/solution.py
@@ -22,7 +22,7 @@
 ROOT = math.sqrt(0.5)
 MIB = 1 << 20
 LIMIT = (20, 24, 24, 36, 32)
-ORDER = (6, 5, 7, 4, 2, 1, 3)
+ORDER = (4, 5, 7, 2, 1, 3)
 
 
 def call(kernel, out, scratch, limit, flops, ins, outs=None):
@@ -284,12 +284,24 @@
 
 def merge_kernel(keep_ref, got_ref, *outs):
     for index in range(8):
-        outs[index][0] = keep_ref[index]
-        outs[index][1] = got_ref[index]
+        out_ref = outs[(0, 1, 2, 3, 4, 5, 4, 6)[index]]
+        first = 2 if index == 6 else 0
+        out_ref[first] = keep_ref[index]
+        out_ref[first + 1] = got_ref[index]
+
+
+def relay_kernel(x_ref, out_ref):
+    out_ref[...] = x_ref[2:4]
+
+
+def relay(x):
+    out = jax.ShapeDtypeStruct((2,) + x.shape[1:], jnp.float32)
+    return call(relay_kernel, out, (), 8, 10**6, [pl.BlockSpec(memory_space=pltpu.VMEM)])(x)
 
 
 def merge(keep, got):
-    out = [jax.ShapeDtypeStruct((2,) + keep.shape[1:], jnp.float32)] * 8
+    counts = (2, 2, 2, 2, 4, 2, 2)
+    out = [jax.ShapeDtypeStruct((n,) + keep.shape[1:], jnp.float32) for n in counts]
     specs = [pl.BlockSpec(memory_space=pltpu.VMEM)] * 2
     return call(merge_kernel, out, (), 8, 10**8, specs)(keep, got)
 
@@ -524,10 +536,12 @@
     def scatter(keep, send):
         got = lax.ppermute(send, group, [(d, d ^ 4) for d in range(DEV)])
         blocks = merge(keep, got)
-        done = [blocks[0]]
+        done = {0: blocks[0]}
         for index in ORDER:
-            done.append((index, lax.ppermute(blocks[index], group, chip_pairs(index))))
-        return [blocks[0]] + [value for _, value in sorted(done[1:], key=lambda item: item[0])]
+            block = blocks[min(index, 6)]
+            done[index] = lax.ppermute(block, group, chip_pairs(index))
+        done[6] = lax.ppermute(relay(done[4]), group, chip_pairs(2))
+        return [done[index] for index in range(8)]
 
     blocks = pack(device, shear)
     fields = []

time: 105 us -> 109 us (1.038)
  starting transfers between devices: 32.1 us -> 39.2 us
  waiting for transfers between devices: 41.3 us -> 37.7 us
    ppermute x21, starting transfers between devices: 17.2 us -> 26.6 us  [the longest x18 23.7 us: scatter(): done[index] = lax.ppermute(block, group, chip_pairs(index))]
    ppermute x21, waiting for transfers between devices: 25.3 us -> 21.6 us  [the longest x18 19.6 us: scatter(): done[index] = lax.ppermute(block, group, chip_pairs(index))]
    ppermute x3, starting transfers between devices: 7.12 us -> 4.86 us  [scatter(): got = lax.ppermute(send, group, [(d, d ^ 4) for d in range(DEV)])]
  transfers between devices with their start and end apart: 30 -> 30, of which waited for: 15 -> 14; matrix products, arithmetic and copies ran while one was open for 0% -> 0% of each run, Pallas kernels for 8% -> 8%
where the time goes in v8:
time: 109 us; the launch traced here: 108 us
  starting transfers between devices  39.2 us (36%)
  waiting for transfers between devices  37.7 us (35%)
  Pallas kernels  15.5 us (14%)
  blocking collectives  12.9 us (12%)
  local copies, waits for them, and re-layouts  1.59 us (1%)
  between operations  1.44 us (1%)
    ppermute x18, starting transfers between devices, scatter(): done[index] = lax.ppermute(block, group, chip_pairs(index))  23.7 us
    ppermute x18, waiting for transfers between devices, scatter(): done[index] = lax.ppermute(block, group, chip_pairs(index))  19.6 us
    ppermute x6, waiting for transfers between devices, body(): got[4 - step] = lax.ppermute(blocks[4 * field + step], 'col', pairs)  14.4 us
    all_to_all x1, blocking collectives, exchange(): return lax.all_to_all(x, group, split_axis=0, concat_axis=0, tiled=True)  12.9 us
    ppermute x6, starting transfers between devices, body(): got[4 - step] = lax.ppermute(blocks[4 * field + step], 'col', pairs)  7.81 us
    ppermute x3, starting transfers between devices, scatter(): got = lax.ppermute(send, group, [(d, d ^ 4) for d in range(DEV)])  4.86 us
    pallas_call x1, Pallas kernels, tables(): call(tables_kernel, out, scratch, LIMIT[0], 10 ** 9, [smem, smem])  4.45 us
    pallas_call x1, Pallas kernels, peak_pass(): return run(thresholds, device, *x, *table, offsets)  4.04 us
  transfers between devices with their start and end apart: 30, of which 14 were waited for; matrix products, arithmetic and copies ran while one was open for 0% of the time, Pallas kernels for 8%

profile of v8, /device:TPU:1, one launch (start us, length us, event | category | flops | bytes accessed | tf_op | source)
XLA Modules:
  0.0 108.4 jit_solution(17929956736341656528)
XLA Ops:
  0.6 1.6 %copy-done = f32[2,1,512,512]{3,2,1,0:T(8,128)S(1)} copy-done((f32[2,1,512,512]{3,2,1,0:T(8,128)S(1)}, f32[2,1,512,512]{3,2,1,0:T(8,128)}, u32[]{:S(2)}) %copy-start) | copy-done | bytes 2097176
  2.4 3.4 %collective-permute-start = (f32[128,512]{1,0:T(8,128)S(1)}, f32[128,512]{1,0:T(8,128)S(1)}, u32[]{:S(2)}, u32[]{:S(2)}) collective-permute-start(f32[128,512]{1,0:T(8,128)S(1)} %get-tuple-element.67), channel_id=1, source_target_pairs={{0,3},{1,0},{2,1},{3,2},{4,7},{5,4},{6,5},{7,6},{8,11},{9,8},{10,9... | collective-permute-start | bytes 786440 | tf_op jit(solution)/shard_map/ppermute | solution.py:552
  6.9 2.1 %collective-permute-start.11 = (f32[128,512]{1,0:T(8,128)S(1)}, f32[128,512]{1,0:T(8,128)S(1)}, u32[]{:S(2)}, u32[]{:S(2)}) collective-permute-start(f32[128,512]{1,0:T(8,128)S(1)} %get-tuple-element.100), channel_id=1, source_target_pairs={{0,3},{1,0},{2,1},{3,2},{4,7},{5,4},{6,5},{7,6},{8,11},{9,8},{10,9... | collective-permute-start | bytes 786440 | tf_op jit(solution)/shard_map/ppermute | solution.py:552
  10.8 2.6 %collective-permute-done.refs_1_ = f32[128,512]{1,0:T(8,128)S(1)} collective-permute-done((f32[128,512]{1,0:T(8,128)S(1)}, f32[128,512]{1,0:T(8,128)S(1)}, u32[]{:S(2)}, u32[]{:S(2)}) %collective-permute-start) | collective-permute-done | bytes 262176 | tf_op jit(solution)/shard_map/ppermute | solution.py:552
  13.4 4.4 %shard_map.68 = (bf16[256,256]{1,0:T(8,128)(2,1)S(1)}, bf16[256,256]{1,0:T(8,128)(2,1)S(1)}, bf16[256,256]{1,0:T(8,128)(2,1)S(1)}, bf16[256,256]{1,0:T(8,128)(2,...) custom-call(f32[1]{0:T(128)S(6)} %copy.7.smooth_ref, ...), custom_call_target="tpu_custom_call" | custom-call | flops 1000000000 | bytes 4194304 | tf_op jit(solution)/shard_map/pallas_call | solution.py:226
  17.9 4.5 %collective-permute-done.2.refs_3_ = f32[128,512]{1,0:T(8,128)S(1)} collective-permute-done((f32[128,512]{1,0:T(8,128)S(1)}, f32[128,512]{1,0:T(8,128)S(1)}, u32[]{:S(2)}, u32[]{:S(2)}) %collective-permute-start.2) | collective-permute-done | bytes 262176 | tf_op jit(solution)/shard_map/ppermute | solution.py:552
  24.9 2.5 %collective-permute-done.11.refs_1_ = f32[128,512]{1,0:T(8,128)S(1)} collective-permute-done((f32[128,512]{1,0:T(8,128)S(1)}, f32[128,512]{1,0:T(8,128)S(1)}, u32[]{:S(2)}, u32[]{:S(2)}) %collective-permute-start.11) | collective-permute-done | bytes 262176 | tf_op jit(solution)/shard_map/ppermute | solution.py:552
  27.4 4.8 %collective-permute-done.13.refs_3_ = f32[128,512]{1,0:T(8,128)S(1)} collective-permute-done((f32[128,512]{1,0:T(8,128)S(1)}, f32[128,512]{1,0:T(8,128)S(1)}, u32[]{:S(2)}, u32[]{:S(2)}) %collective-permute-start.13) | collective-permute-done | bytes 262176 | tf_op jit(solution)/shard_map/ppermute | solution.py:552
  39.9 6.0 %collective-permute-done.4.refs_1_ = f32[2,128,128]{2,1,0:T(8,128)S(1)} collective-permute-done((f32[2,128,128]{2,1,0:T(8,128)S(1)}, f32[2,128,128]{2,1,0:T(8,128)S(1)}, u32[]{:S(2)}, u32[]{:S(2)}) %collective-permute-start.4) | collective-permute-done | bytes 131104 | tf_op jit(solution)/shard_map/ppermute | solution.py:542
  45.9 3.6 %collective-permute-start.10 = (f32[2,128,128]{2,1,0:T(8,128)S(1)}, f32[2,128,128]{2,1,0:T(8,128)S(1)}, u32[]{:S(2)}, u32[]{:S(2)}) collective-permute-start(f32[2,128,128]{2,1,0:T(8,128)S(1)} %get-tuple-element.88), channel_id=1, source_target_pairs={{0,11},{1,8},{2,9},{3,10},{4,15},{5,12},{6,13},{7,14},{8,3},{9,0},... | collective-permute-start | bytes 393224 | tf_op jit(solution)/shard_map/ppermute | solution.py:542
  49.5 1.6 %collective-permute-start.9 = (f32[2,128,128]{2,1,0:T(8,128)S(1)}, f32[2,128,128]{2,1,0:T(8,128)S(1)}, u32[]{:S(2)}, u32[]{:S(2)}) collective-permute-start(f32[2,128,128]{2,1,0:T(8,128)S(1)} %shard_map.71), channel_id=1, source_target_pairs={{0,2},{1,3},{2,0},{3,1},{4,6},{5,7},{6,4},{7,5},{8,10},{9,11},{10,... | collective-permute-start | bytes 393224 | tf_op jit(solution)/shard_map/ppermute | solution.py:543
  52.9 2.4 %collective-permute-start.17 = (f32[2,128,128]{2,1,0:T(8,128)S(1)}, f32[2,128,128]{2,1,0:T(8,128)S(1)}, u32[]{:S(2)}, u32[]{:S(2)}) collective-permute-start(f32[2,128,128]{2,1,0:T(8,128)S(1)} %get-tuple-element.108), channel_id=1, source_target_pairs={{0,3},{1,0},{2,1},{3,2},{4,7},{5,4},{6,5},{7,6},{8,11},{9,8},{10,9... | collective-permute-start | bytes 393224 | tf_op jit(solution)/shard_map/ppermute | solution.py:542
  56.7 4.1 %collective-permute-done.15.refs_1_ = f32[2,128,128]{2,1,0:T(8,128)S(1)} collective-permute-done((f32[2,128,128]{2,1,0:T(8,128)S(1)}, f32[2,128,128]{2,1,0:T(8,128)S(1)}, u32[]{:S(2)}, u32[]{:S(2)}) %collective-permute-start.15) | collective-permute-done | bytes 131104 | tf_op jit(solution)/shard_map/ppermute | solution.py:542
  62.1 4.2 %collective-permute-done.19.refs_5_ = f32[2,128,128]{2,1,0:T(8,128)S(1)} collective-permute-done((f32[2,128,128]{2,1,0:T(8,128)S(1)}, f32[2,128,128]{2,1,0:T(8,128)S(1)}, u32[]{:S(2)}, u32[]{:S(2)}) %collective-permute-start.19) | collective-permute-done | bytes 131104 | tf_op jit(solution)/shard_map/ppermute | solution.py:542
  67.2 2.6 %shard_map.76 = (f32[8,136,128]{2,1,0:T(8,128)S(1)}, f32[8,136,128]{2,1,0:T(8,128)S(1)}) custom-call(s32[1]{0:T(128)} %bitcast.device_ref, f32[2048,128]{1,0:T(8,128)S(1)} %shard_map.72.one_ref, f32[2,128,128]{2,1,0:T(8,128)S(1)} %get-tuple-element.105.refs_0_, f32[2,128,128]{2,1,0:T(8,128)S(1)} %collective-permute-done.15.refs_1_, ...), custom_call_target="tpu_custom_call" | custom-call | flops 3000000000 | bytes 4194304 | tf_op jit(solution)/shard_map/pallas_call | solution.py:402
  69.8 2.6 %collective-permute-start.22 = (f32[8,136,128]{2,1,0:T(8,128)S(1)}, f32[8,136,128]{2,1,0:T(8,128)S(1)}, u32[]{:S(2)}, u32[]{:S(2)}) collective-permute-start(f32[8,136,128]{2,1,0:T(8,128)S(1)} %get-tuple-element.116), channel_id=1, source_target_pairs={{0,4},{1,5},{2,6},{3,7},{4,0},{5,1},{6,2},{7,3},{8,12},{9,13},{10,... | collective-permute-start | bytes 1671176 | tf_op jit(solution)/shard_map/ppermute | solution.py:537
  72.4 1.6 %collective-permute-done.22.got_ref = f32[8,136,128]{2,1,0:T(8,128)S(1)} collective-permute-done((f32[8,136,128]{2,1,0:T(8,128)S(1)}, f32[8,136,128]{2,1,0:T(8,128)S(1)}, u32[]{:S(2)}, u32[]{:S(2)}) %collective-permute-start.22) | collective-permute-done | bytes 557088 | tf_op jit(solution)/shard_map/ppermute | solution.py:537
  74.9 2.2 %collective-permute-start.23 = (f32[2,136,128]{2,1,0:T(8,128)S(1)}, f32[2,136,128]{2,1,0:T(8,128)S(1)}, u32[]{:S(2)}, u32[]{:S(2)}) collective-permute-start(f32[2,136,128]{2,1,0:T(8,128)S(1)} %get-tuple-element.118), channel_id=1, source_target_pairs={{0,1},{1,2},{2,3},{3,0},{4,5},{5,6},{6,7},{7,4},{8,9},{9,10},{10,1... | collective-permute-start | bytes 417800 | tf_op jit(solution)/shard_map/ppermute | solution.py:542
  77.1 1.9 %collective-permute-start.24 = (f32[2,136,128]{2,1,0:T(8,128)S(1)}, f32[2,136,128]{2,1,0:T(8,128)S(1)}, u32[]{:S(2)}, u32[]{:S(2)}) collective-permute-start(f32[2,136,128]{2,1,0:T(8,128)S(1)} %get-tuple-element.119), channel_id=1, source_target_pairs={{0,2},{1,3},{2,0},{3,1},{4,6},{5,7},{6,4},{7,5},{8,10},{9,11},{10,... | collective-permute-start | bytes 417800 | tf_op jit(solution)/shard_map/ppermute | solution.py:542
  80.2 1.8 %collective-permute-done.26.x_ref.refs_4_ = f32[4,136,128]{2,1,0:T(8,128)S(1)} collective-permute-done((f32[4,136,128]{2,1,0:T(8,128)S(1)}, f32[4,136,128]{2,1,0:T(8,128)S(1)}, u32[]{:S(2)}, u32[]{:S(2)}) %collective-permute-start.26) | collective-permute-done | bytes 278560 | tf_op jit(solution)/shard_map/ppermute | solution.py:542
  82.0 3.3 %collective-permute-start.29 = (f32[2,136,128]{2,1,0:T(8,128)S(1)}, f32[2,136,128]{2,1,0:T(8,128)S(1)}, u32[]{:S(2)}, u32[]{:S(2)}) collective-permute-start(f32[2,136,128]{2,1,0:T(8,128)S(1)} %get-tuple-element.123), channel_id=1, source_target_pairs={{0,11},{1,8},{2,9},{3,10},{4,15},{5,12},{6,13},{7,14},{8,3},{9,0},... | collective-permute-start | bytes 417800 | tf_op jit(solution)/shard_map/ppermute | solution.py:542
  86.6 3.3 %collective-permute-done.27.refs_5_ = f32[2,136,128]{2,1,0:T(8,128)S(1)} collective-permute-done((f32[2,136,128]{2,1,0:T(8,128)S(1)}, f32[2,136,128]{2,1,0:T(8,128)S(1)}, u32[]{:S(2)}, u32[]{:S(2)}) %collective-permute-start.27) | collective-permute-done | bytes 139296 | tf_op jit(solution)/shard_map/ppermute | solution.py:542
  90.9 4.0 %shard_map.79 = (f32[128,2048]{1,0:T(8,128)}, f32[8,128]{1,0:T(8,128)S(1)}, f32[16,8,128]{2,1,0:T(8,128)S(1)}) custom-call(s32[1,16]{1,0:T(1,128)S(1)} %copy-done.2, s32[1]{0:T(128)} %bitcast.device_ref, f32[2,136,128]{2,1,0:T(8,128)S(1)} %get-tuple-element.117.refs_0_, f32[2,136,128]{2,1,0:T(8,128)S(1)} %collective-permute-done.23.refs_1_, ...), custom_call_target="tpu_custom_call" | custom-call | flops 2000000000 | bytes 4194304 | tf_op jit(solution)/shard_map/pallas_call | solution.py:505
  94.9 12.9 %all_to_all.5.counts_ref = f32[16,8,128]{2,1,0:T(8,128)S(1)} all-to-all(f32[16,8,128]{2,1,0:T(8,128)S(1)} %get-tuple-element.125), channel_id=1, replica_groups=mesh['maps'=16,'row'=4,'col'=4] {'row','col'}, dimensions={0} | all-to-all | bytes 131072 | tf_op jit(solution)/shard_map/all_to_all | solution.py:534
  (57 shorter events, 23.0 us)
Async XLA Ops:
  2.4 11.0 %collective-permute-start = (f32[128,512]{1,0:T(8,128)S(1)}, f32[128,512]{1,0:T(8,128)S(1)}, u32[]{:S(2)}, u32[]{:S(2)}) collective-permute-start(f32[128,512]{1,0:T(8,128)S(1)} %get-tuple-element.67), channel_id=1, source_target_pairs={{0,3},{1,0},{2,1},{3,2},{4,7},{5,4},{6,5},{7,6},{8,11},{9,8},{10,9... | collective-permute-start | bytes 786440 | tf_op jit(solution)/shard_map/ppermute | solution.py:552
  5.7 12.1 %collective-permute-start.1 = (f32[128,512]{1,0:T(8,128)S(1)}, f32[128,512]{1,0:T(8,128)S(1)}, u32[]{:S(2)}, u32[]{:S(2)}) collective-permute-start(f32[128,512]{1,0:T(8,128)S(1)} %get-tuple-element.68), channel_id=1, source_target_pairs={{0,2},{1,3},{2,0},{3,1},{4,6},{5,7},{6,4},{7,5},{8,10},{9,11},{10,... | collective-permute-start | bytes 786440 | tf_op jit(solution)/shard_map/ppermute | solution.py:552
  6.3 16.1 %collective-permute-start.2 = (f32[128,512]{1,0:T(8,128)S(1)}, f32[128,512]{1,0:T(8,128)S(1)}, u32[]{:S(2)}, u32[]{:S(2)}) collective-permute-start(f32[128,512]{1,0:T(8,128)S(1)} %get-tuple-element.69), channel_id=1, source_target_pairs={{0,1},{1,2},{2,3},{3,0},{4,5},{5,6},{6,7},{7,4},{8,9},{9,10},{10,1... | collective-permute-start | bytes 786440 | tf_op jit(solution)/shard_map/ppermute | solution.py:552
  6.9 20.6 %collective-permute-start.11 = (f32[128,512]{1,0:T(8,128)S(1)}, f32[128,512]{1,0:T(8,128)S(1)}, u32[]{:S(2)}, u32[]{:S(2)}) collective-permute-start(f32[128,512]{1,0:T(8,128)S(1)} %get-tuple-element.100), channel_id=1, source_target_pairs={{0,3},{1,0},{2,1},{3,2},{4,7},{5,4},{6,5},{7,6},{8,11},{9,8},{10,9... | collective-permute-start | bytes 786440 | tf_op jit(solution)/shard_map/ppermute | solution.py:552
  8.9 18.5 %collective-permute-start.12 = (f32[128,512]{1,0:T(8,128)S(1)}, f32[128,512]{1,0:T(8,128)S(1)}, u32[]{:S(2)}, u32[]{:S(2)}) collective-permute-start(f32[128,512]{1,0:T(8,128)S(1)} %get-tuple-element.101), channel_id=1, source_target_pairs={{0,2},{1,3},{2,0},{3,1},{4,6},{5,7},{6,4},{7,5},{8,10},{9,11},{10,... | collective-permute-start | bytes 786440 | tf_op jit(solution)/shard_map/ppermute | solution.py:552
  13.4 18.9 %collective-permute-start.13 = (f32[128,512]{1,0:T(8,128)S(1)}, f32[128,512]{1,0:T(8,128)S(1)}, u32[]{:S(2)}, u32[]{:S(2)}) collective-permute-start(f32[128,512]{1,0:T(8,128)S(1)} %get-tuple-element.102), channel_id=1, source_target_pairs={{0,1},{1,2},{2,3},{3,0},{4,5},{5,6},{6,7},{7,4},{8,9},{9,10},{10,1... | collective-permute-start | bytes 786440 | tf_op jit(solution)/shard_map/ppermute | solution.py:552
  23.5 10.7 %collective-permute-start.3 = (f32[8,128,128]{2,1,0:T(8,128)S(1)}, f32[8,128,128]{2,1,0:T(8,128)S(1)}, u32[]{:S(2)}, u32[]{:S(2)}) collective-permute-start(f32[8,128,128]{2,1,0:T(8,128)S(1)} %get-tuple-element.81), channel_id=1, source_target_pairs={{0,4},{1,5},{2,6},{3,7},{4,0},{5,1},{6,2},{7,3},{8,12},{9,13},{10,... | collective-permute-start | bytes 1572872 | tf_op jit(solution)/shard_map/ppermute | solution.py:537
  34.3 15.2 %collective-permute-start.7 = (f32[4,128,128]{2,1,0:T(8,128)S(1)}, f32[4,128,128]{2,1,0:T(8,128)S(1)}, u32[]{:S(2)}, u32[]{:S(2)}) collective-permute-start(f32[4,128,128]{2,1,0:T(8,128)S(1)} %get-tuple-element.86), channel_id=1, source_target_pairs={{0,8},{1,9},{2,10},{3,11},{4,12},{5,13},{6,14},{7,15},{8,0},{9,1},... | collective-permute-start | bytes 786440 | tf_op jit(solution)/shard_map/ppermute | solution.py:542
  35.8 13.7 %collective-permute-start.18 = (f32[4,128,128]{2,1,0:T(8,128)S(1)}, f32[4,128,128]{2,1,0:T(8,128)S(1)}, u32[]{:S(2)}, u32[]{:S(2)}) collective-permute-start(f32[4,128,128]{2,1,0:T(8,128)S(1)} %get-tuple-element.109), channel_id=1, source_target_pairs={{0,8},{1,9},{2,10},{3,11},{4,12},{5,13},{6,14},{7,15},{8,0},{9,1},... | collective-permute-start | bytes 786440 | tf_op jit(solution)/shard_map/ppermute | solution.py:542
  37.2 8.7 %collective-permute-start.4 = (f32[2,128,128]{2,1,0:T(8,128)S(1)}, f32[2,128,128]{2,1,0:T(8,128)S(1)}, u32[]{:S(2)}, u32[]{:S(2)}) collective-permute-start(f32[2,128,128]{2,1,0:T(8,128)S(1)} %get-tuple-element.83), channel_id=1, source_target_pairs={{0,1},{1,2},{2,3},{3,0},{4,5},{5,6},{6,7},{7,4},{8,9},{9,10},{10,1... | collective-permute-start | bytes 393224 | tf_op jit(solution)/shard_map/ppermute | solution.py:542
  37.2 8.7 %collective-permute-start.5 = (f32[2,128,128]{2,1,0:T(8,128)S(1)}, f32[2,128,128]{2,1,0:T(8,128)S(1)}, u32[]{:S(2)}, u32[]{:S(2)}) collective-permute-start(f32[2,128,128]{2,1,0:T(8,128)S(1)} %get-tuple-element.84), channel_id=1, source_target_pairs={{0,2},{1,3},{2,0},{3,1},{4,6},{5,7},{6,4},{7,5},{8,10},{9,11},{10,... | collective-permute-start | bytes 393224 | tf_op jit(solution)/shard_map/ppermute | solution.py:542
  38.8 12.4 %collective-permute-start.6 = (f32[2,128,128]{2,1,0:T(8,128)S(1)}, f32[2,128,128]{2,1,0:T(8,128)S(1)}, u32[]{:S(2)}, u32[]{:S(2)}) collective-permute-start(f32[2,128,128]{2,1,0:T(8,128)S(1)} %get-tuple-element.85), channel_id=1, source_target_pairs={{0,3},{1,0},{2,1},{3,2},{4,7},{5,4},{6,5},{7,6},{8,11},{9,8},{10,9... | collective-permute-start | bytes 393224 | tf_op jit(solution)/shard_map/ppermute | solution.py:542
  45.9 9.5 %collective-permute-start.10 = (f32[2,128,128]{2,1,0:T(8,128)S(1)}, f32[2,128,128]{2,1,0:T(8,128)S(1)}, u32[]{:S(2)}, u32[]{:S(2)}) collective-permute-start(f32[2,128,128]{2,1,0:T(8,128)S(1)} %get-tuple-element.88), channel_id=1, source_target_pairs={{0,11},{1,8},{2,9},{3,10},{4,15},{5,12},{6,13},{7,14},{8,3},{9,0},... | collective-permute-start | bytes 393224 | tf_op jit(solution)/shard_map/ppermute | solution.py:542
  49.5 11.3 %collective-permute-start.15 = (f32[2,128,128]{2,1,0:T(8,128)S(1)}, f32[2,128,128]{2,1,0:T(8,128)S(1)}, u32[]{:S(2)}, u32[]{:S(2)}) collective-permute-start(f32[2,128,128]{2,1,0:T(8,128)S(1)} %get-tuple-element.106), channel_id=1, source_target_pairs={{0,1},{1,2},{2,3},{3,0},{4,5},{5,6},{6,7},{7,4},{8,9},{9,10},{10,1... | collective-permute-start | bytes 393224 | tf_op jit(solution)/shard_map/ppermute | solution.py:542
  49.5 11.3 %collective-permute-start.9 = (f32[2,128,128]{2,1,0:T(8,128)S(1)}, f32[2,128,128]{2,1,0:T(8,128)S(1)}, u32[]{:S(2)}, u32[]{:S(2)}) collective-permute-start(f32[2,128,128]{2,1,0:T(8,128)S(1)} %shard_map.71), channel_id=1, source_target_pairs={{0,2},{1,3},{2,0},{3,1},{4,6},{5,7},{6,4},{7,5},{8,10},{9,11},{10,... | collective-permute-start | bytes 393224 | tf_op jit(solution)/shard_map/ppermute | solution.py:543
  51.2 10.9 %collective-permute-start.16 = (f32[2,128,128]{2,1,0:T(8,128)S(1)}, f32[2,128,128]{2,1,0:T(8,128)S(1)}, u32[]{:S(2)}, u32[]{:S(2)}) collective-permute-start(f32[2,128,128]{2,1,0:T(8,128)S(1)} %get-tuple-element.107), channel_id=1, source_target_pairs={{0,2},{1,3},{2,0},{3,1},{4,6},{5,7},{6,4},{7,5},{8,10},{9,11},{10,... | collective-permute-start | bytes 393224 | tf_op jit(solution)/shard_map/ppermute | solution.py:542
  52.9 9.2 %collective-permute-start.17 = (f32[2,128,128]{2,1,0:T(8,128)S(1)}, f32[2,128,128]{2,1,0:T(8,128)S(1)}, u32[]{:S(2)}, u32[]{:S(2)}) collective-permute-start(f32[2,128,128]{2,1,0:T(8,128)S(1)} %get-tuple-element.108), channel_id=1, source_target_pairs={{0,3},{1,0},{2,1},{3,2},{4,7},{5,4},{6,5},{7,6},{8,11},{9,8},{10,9... | collective-permute-start | bytes 393224 | tf_op jit(solution)/shard_map/ppermute | solution.py:542
  55.4 10.9 %collective-permute-start.19 = (f32[2,128,128]{2,1,0:T(8,128)S(1)}, f32[2,128,128]{2,1,0:T(8,128)S(1)}, u32[]{:S(2)}, u32[]{:S(2)}) collective-permute-start(f32[2,128,128]{2,1,0:T(8,128)S(1)} %get-tuple-element.110), channel_id=1, source_target_pairs={{0,9},{1,10},{2,11},{3,8},{4,13},{5,14},{6,15},{7,12},{8,1},{9,2},... | collective-permute-start | bytes 393224 | tf_op jit(solution)/shard_map/ppermute | solution.py:542
  74.1 7.9 %collective-permute-start.26 = (f32[4,136,128]{2,1,0:T(8,128)S(1)}, f32[4,136,128]{2,1,0:T(8,128)S(1)}, u32[]{:S(2)}, u32[]{:S(2)}) collective-permute-start(f32[4,136,128]{2,1,0:T(8,128)S(1)} %get-tuple-element.121), channel_id=1, source_target_pairs={{0,8},{1,9},{2,10},{3,11},{4,12},{5,13},{6,14},{7,15},{8,0},{9,1},... | collective-permute-start | bytes 835592 | tf_op jit(solution)/shard_map/ppermute | solution.py:542
  74.9 10.5 %collective-permute-start.23 = (f32[2,136,128]{2,1,0:T(8,128)S(1)}, f32[2,136,128]{2,1,0:T(8,128)S(1)}, u32[]{:S(2)}, u32[]{:S(2)}) collective-permute-start(f32[2,136,128]{2,1,0:T(8,128)S(1)} %get-tuple-element.118), channel_id=1, source_target_pairs={{0,1},{1,2},{2,3},{3,0},{4,5},{5,6},{6,7},{7,4},{8,9},{9,10},{10,1... | collective-permute-start | bytes 417800 | tf_op jit(solution)/shard_map/ppermute | solution.py:542
  77.1 9.5 %collective-permute-start.24 = (f32[2,136,128]{2,1,0:T(8,128)S(1)}, f32[2,136,128]{2,1,0:T(8,128)S(1)}, u32[]{:S(2)}, u32[]{:S(2)}) collective-permute-start(f32[2,136,128]{2,1,0:T(8,128)S(1)} %get-tuple-element.119), channel_id=1, source_target_pairs={{0,2},{1,3},{2,0},{3,1},{4,6},{5,7},{6,4},{7,5},{8,10},{9,11},{10,... | collective-permute-start | bytes 417800 | tf_op jit(solution)/shard_map/ppermute | solution.py:542
  79.0 7.6 %collective-permute-start.25 = (f32[2,136,128]{2,1,0:T(8,128)S(1)}, f32[2,136,128]{2,1,0:T(8,128)S(1)}, u32[]{:S(2)}, u32[]{:S(2)}) collective-permute-start(f32[2,136,128]{2,1,0:T(8,128)S(1)} %get-tuple-element.120), channel_id=1, source_target_pairs={{0,3},{1,0},{2,1},{3,2},{4,7},{5,4},{6,5},{7,6},{8,11},{9,8},{10,9... | collective-permute-start | bytes 417800 | tf_op jit(solution)/shard_map/ppermute | solution.py:542
  79.5 10.3 %collective-permute-start.27 = (f32[2,136,128]{2,1,0:T(8,128)S(1)}, f32[2,136,128]{2,1,0:T(8,128)S(1)}, u32[]{:S(2)}, u32[]{:S(2)}) collective-permute-start(f32[2,136,128]{2,1,0:T(8,128)S(1)} %get-tuple-element.122), channel_id=1, source_target_pairs={{0,9},{1,10},{2,11},{3,8},{4,13},{5,14},{6,15},{7,12},{8,1},{9,2},... | collective-permute-start | bytes 417800 | tf_op jit(solution)/shard_map/ppermute | solution.py:542
  82.0 7.8 %collective-permute-start.29 = (f32[2,136,128]{2,1,0:T(8,128)S(1)}, f32[2,136,128]{2,1,0:T(8,128)S(1)}, u32[]{:S(2)}, u32[]{:S(2)}) collective-permute-start(f32[2,136,128]{2,1,0:T(8,128)S(1)} %get-tuple-element.123), channel_id=1, source_target_pairs={{0,11},{1,8},{2,9},{3,10},{4,15},{5,12},{6,13},{7,14},{8,3},{9,0},... | collective-permute-start | bytes 417800 | tf_op jit(solution)/shard_map/ppermute | solution.py:542
  (9 other events, 79.9 us)

commit v9 on v8

--- a/solution.py
+++ b/solution.py
@@ -22,7 +22,8 @@
 ROOT = math.sqrt(0.5)
 MIB = 1 << 20
 LIMIT = (20, 24, 24, 36, 32)
-ORDER = (4, 5, 7, 2, 1, 3)
+ORDER = (3, 6, 5, 4, 1, 7)
+PLACES = (0, 1, 2, 2, 3, 4, 5, 6)
 
 
 def call(kernel, out, scratch, limit, flops, ins, outs=None):
@@ -284,8 +285,8 @@
 
 def merge_kernel(keep_ref, got_ref, *outs):
     for index in range(8):
-        out_ref = outs[(0, 1, 2, 3, 4, 5, 4, 6)[index]]
-        first = 2 if index == 6 else 0
+        out_ref = outs[PLACES[index]]
+        first = 2 if index == 2 else 0
         out_ref[first] = keep_ref[index]
         out_ref[first + 1] = got_ref[index]
 
@@ -300,7 +301,7 @@
 
 
 def merge(keep, got):
-    counts = (2, 2, 2, 2, 4, 2, 2)
+    counts = (2, 2, 4, 2, 2, 2, 2)
     out = [jax.ShapeDtypeStruct((n,) + keep.shape[1:], jnp.float32) for n in counts]
     specs = [pl.BlockSpec(memory_space=pltpu.VMEM)] * 2
     return call(merge_kernel, out, (), 8, 10**8, specs)(keep, got)
@@ -538,9 +539,8 @@
         blocks = merge(keep, got)
         done = {0: blocks[0]}
         for index in ORDER:
-            block = blocks[min(index, 6)]
-            done[index] = lax.ppermute(block, group, chip_pairs(index))
-        done[6] = lax.ppermute(relay(done[4]), group, chip_pairs(2))
+            done[index] = lax.ppermute(blocks[PLACES[index]], group, chip_pairs(index))
+        done[2] = lax.ppermute(relay(done[3]), group, chip_pairs(3))
         return [done[index] for index in range(8)]
 
     blocks = pack(device, shear)

time: 109 us -> 109 us (level)
  starting transfers between devices: 39.2 us -> 41.1 us
  waiting for transfers between devices: 37.7 us -> 36.5 us
    ppermute x21, starting transfers between devices: 26.6 us -> 29.4 us  [the longest x18 25.3 us: scatter(): done[index] = lax.ppermute(blocks[PLACES[index]], group, chip_pairs(index))]
    ppermute x21, waiting for transfers between devices: 21.6 us -> 19.5 us  [the longest x18 12.8 us: scatter(): done[index] = lax.ppermute(blocks[PLACES[index]], group, chip_pairs(index))]
  transfers between devices with their start and end apart: 30 -> 30, of which waited for: 14 -> 14; matrix products, arithmetic and copies ran while one was open for 0% -> 0% of each run, Pallas kernels for 8% -> 7%
where the time goes in v9:
time: 109 us
  starting transfers between devices  41.1 us (38%)
  waiting for transfers between devices  36.5 us (33%)
  Pallas kernels  15.5 us (14%)
  blocking collectives  12.6 us (12%)
  local copies, waits for them, and re-layouts  1.59 us (1%)
  between operations  1.46 us (1%)
    ppermute x18, starting transfers between devices, scatter(): done[index] = lax.ppermute(blocks[PLACES[index]], group, chip_pairs(index))  25.3 us
    ppermute x6, waiting for transfers between devices, body(): got[4 - step] = lax.ppermute(blocks[4 * field + step], 'col', pairs)  14.4 us
    ppermute x18, waiting for transfers between devices, scatter(): done[index] = lax.ppermute(blocks[PLACES[index]], group, chip_pairs(index))  12.8 us
    all_to_all x1, blocking collectives, exchange(): return lax.all_to_all(x, group, split_axis=0, concat_axis=0, tiled=True)  12.6 us
    ppermute x6, starting transfers between devices, body(): got[4 - step] = lax.ppermute(blocks[4 * field + step], 'col', pairs)  7.81 us
    ppermute x3, waiting for transfers between devices, scatter(): done[2] = lax.ppermute(relay(done[3]), group, chip_pairs(3))  6.62 us
    pallas_call x1, Pallas kernels, tables(): call(tables_kernel, out, scratch, LIMIT[0], 10 ** 9, [smem, smem])  4.45 us
    ppermute x3, starting transfers between devices, scatter(): done[2] = lax.ppermute(relay(done[3]), group, chip_pairs(3))  4.06 us
  transfers between devices with their start and end apart: 30, of which 14 were waited for; matrix products, arithmetic and copies ran while one was open for 0% of the time, Pallas kernels for 7%

profile of v9, /device:TPU:1, one launch (start us, length us, event | category | flops | bytes accessed | tf_op | source)
XLA Modules:
  0.0 108.7 jit_solution(10456172468034360948)
XLA Ops:
  2.4 3.4 %collective-permute-start = (f32[128,512]{1,0:T(8,128)S(1)}, f32[128,512]{1,0:T(8,128)S(1)}, u32[]{:S(2)}, u32[]{:S(2)}) collective-permute-start(f32[128,512]{1,0:T(8,128)S(1)} %get-tuple-element.67), channel_id=1, source_target_pairs={{0,3},{1,0},{2,1},{3,2},{4,7},{5,4},{6,5},{7,6},{8,11},{9,8},{10,9... | collective-permute-start | bytes 786440 | tf_op jit(solution)/shard_map/ppermute | solution.py:552
  6.9 2.1 %collective-permute-start.11 = (f32[128,512]{1,0:T(8,128)S(1)}, f32[128,512]{1,0:T(8,128)S(1)}, u32[]{:S(2)}, u32[]{:S(2)}) collective-permute-start(f32[128,512]{1,0:T(8,128)S(1)} %get-tuple-element.100), channel_id=1, source_target_pairs={{0,3},{1,0},{2,1},{3,2},{4,7},{5,4},{6,5},{7,6},{8,11},{9,8},{10,9... | collective-permute-start | bytes 786440 | tf_op jit(solution)/shard_map/ppermute | solution.py:552
  10.8 2.6 %collective-permute-done.refs_1_ = f32[128,512]{1,0:T(8,128)S(1)} collective-permute-done((f32[128,512]{1,0:T(8,128)S(1)}, f32[128,512]{1,0:T(8,128)S(1)}, u32[]{:S(2)}, u32[]{:S(2)}) %collective-permute-start) | collective-permute-done | bytes 262176 | tf_op jit(solution)/shard_map/ppermute | solution.py:552
  13.4 4.4 %shard_map.68 = (bf16[256,256]{1,0:T(8,128)(2,1)S(1)}, bf16[256,256]{1,0:T(8,128)(2,1)S(1)}, bf16[256,256]{1,0:T(8,128)(2,1)S(1)}, bf16[256,256]{1,0:T(8,128)(2,...) custom-call(f32[1]{0:T(128)S(6)} %copy.7.smooth_ref, ...), custom_call_target="tpu_custom_call" | custom-call | flops 1000000000 | bytes 4194304 | tf_op jit(solution)/shard_map/pallas_call | solution.py:227
  17.9 4.5 %collective-permute-done.2.refs_3_ = f32[128,512]{1,0:T(8,128)S(1)} collective-permute-done((f32[128,512]{1,0:T(8,128)S(1)}, f32[128,512]{1,0:T(8,128)S(1)}, u32[]{:S(2)}, u32[]{:S(2)}) %collective-permute-start.2) | collective-permute-done | bytes 262176 | tf_op jit(solution)/shard_map/ppermute | solution.py:552
  24.9 2.5 %collective-permute-done.11.refs_1_ = f32[128,512]{1,0:T(8,128)S(1)} collective-permute-done((f32[128,512]{1,0:T(8,128)S(1)}, f32[128,512]{1,0:T(8,128)S(1)}, u32[]{:S(2)}, u32[]{:S(2)}) %collective-permute-start.11) | collective-permute-done | bytes 262176 | tf_op jit(solution)/shard_map/ppermute | solution.py:552
  27.4 4.8 %collective-permute-done.13.refs_3_ = f32[128,512]{1,0:T(8,128)S(1)} collective-permute-done((f32[128,512]{1,0:T(8,128)S(1)}, f32[128,512]{1,0:T(8,128)S(1)}, u32[]{:S(2)}, u32[]{:S(2)}) %collective-permute-start.13) | collective-permute-done | bytes 262176 | tf_op jit(solution)/shard_map/ppermute | solution.py:552
  38.7 3.2 %collective-permute-done.4.refs_1_ = f32[2,128,128]{2,1,0:T(8,128)S(1)} collective-permute-done((f32[2,128,128]{2,1,0:T(8,128)S(1)}, f32[2,128,128]{2,1,0:T(8,128)S(1)}, u32[]{:S(2)}, u32[]{:S(2)}) %collective-permute-start.4) | collective-permute-done | bytes 131104 | tf_op jit(solution)/shard_map/ppermute | solution.py:542
  43.3 3.9 %collective-permute-start.10 = (f32[2,128,128]{2,1,0:T(8,128)S(1)}, f32[2,128,128]{2,1,0:T(8,128)S(1)}, u32[]{:S(2)}, u32[]{:S(2)}) collective-permute-start(f32[2,128,128]{2,1,0:T(8,128)S(1)} %get-tuple-element.88), channel_id=1, source_target_pairs={{0,11},{1,8},{2,9},{3,10},{4,15},{5,12},{6,13},{7,14},{8,3},{9,0},... | collective-permute-start | bytes 393224 | tf_op jit(solution)/shard_map/ppermute | solution.py:542
  47.8 2.1 %collective-permute-start.6 = (f32[2,128,128]{2,1,0:T(8,128)S(1)}, f32[2,128,128]{2,1,0:T(8,128)S(1)}, u32[]{:S(2)}, u32[]{:S(2)}) collective-permute-start(f32[2,128,128]{2,1,0:T(8,128)S(1)} %shard_map.71), channel_id=1, source_target_pairs={{0,3},{1,0},{2,1},{3,2},{4,7},{5,4},{6,5},{7,6},{8,11},{9,8},{10,9... | collective-permute-start | bytes 393224 | tf_op jit(solution)/shard_map/ppermute | solution.py:543
  50.9 3.6 %collective-permute-done.10.refs_7_ = f32[2,128,128]{2,1,0:T(8,128)S(1)} collective-permute-done((f32[2,128,128]{2,1,0:T(8,128)S(1)}, f32[2,128,128]{2,1,0:T(8,128)S(1)}, u32[]{:S(2)}, u32[]{:S(2)}) %collective-permute-start.10) | collective-permute-done | bytes 131104 | tf_op jit(solution)/shard_map/ppermute | solution.py:542
  54.5 1.6 %collective-permute-start.20 = (f32[2,128,128]{2,1,0:T(8,128)S(1)}, f32[2,128,128]{2,1,0:T(8,128)S(1)}, u32[]{:S(2)}, u32[]{:S(2)}) collective-permute-start(f32[2,128,128]{2,1,0:T(8,128)S(1)} %get-tuple-element.110), channel_id=1, source_target_pairs={{0,10},{1,11},{2,8},{3,9},{4,14},{5,15},{6,12},{7,13},{8,2},{9,3},... | collective-permute-start | bytes 393224 | tf_op jit(solution)/shard_map/ppermute | solution.py:542
  57.0 1.9 %collective-permute-start.17 = (f32[2,128,128]{2,1,0:T(8,128)S(1)}, f32[2,128,128]{2,1,0:T(8,128)S(1)}, u32[]{:S(2)}, u32[]{:S(2)}) collective-permute-start(f32[2,128,128]{2,1,0:T(8,128)S(1)} %shard_map.75), channel_id=1, source_target_pairs={{0,3},{1,0},{2,1},{3,2},{4,7},{5,4},{6,5},{7,6},{8,11},{9,8},{10,9... | collective-permute-start | bytes 393224 | tf_op jit(solution)/shard_map/ppermute | solution.py:543
  60.2 2.6 %collective-permute-done.20.refs_6_ = f32[2,128,128]{2,1,0:T(8,128)S(1)} collective-permute-done((f32[2,128,128]{2,1,0:T(8,128)S(1)}, f32[2,128,128]{2,1,0:T(8,128)S(1)}, u32[]{:S(2)}, u32[]{:S(2)}) %collective-permute-start.20) | collective-permute-done | bytes 131104 | tf_op jit(solution)/shard_map/ppermute | solution.py:542
  62.9 3.8 %collective-permute-done.17.refs_2_ = f32[2,128,128]{2,1,0:T(8,128)S(1)} collective-permute-done((f32[2,128,128]{2,1,0:T(8,128)S(1)}, f32[2,128,128]{2,1,0:T(8,128)S(1)}, u32[]{:S(2)}, u32[]{:S(2)}) %collective-permute-start.17) | collective-permute-done | bytes 131104 | tf_op jit(solution)/shard_map/ppermute | solution.py:543
  66.7 2.6 %shard_map.76 = (f32[8,136,128]{2,1,0:T(8,128)S(1)}, f32[8,136,128]{2,1,0:T(8,128)S(1)}) custom-call(s32[1]{0:T(128)} %bitcast.device_ref, f32[2048,128]{1,0:T(8,128)S(1)} %shard_map.72.one_ref, f32[2,128,128]{2,1,0:T(8,128)S(1)} %get-tuple-element.105.refs_0_, f32[2,128,128]{2,1,0:T(8,128)S(1)} %collective-permute-done.15.refs_1_, ...), custom_call_target="tpu_custom_call" | custom-call | flops 3000000000 | bytes 4194304 | tf_op jit(solution)/shard_map/pallas_call | solution.py:403
  69.2 1.6 %collective-permute-start.22 = (f32[8,136,128]{2,1,0:T(8,128)S(1)}, f32[8,136,128]{2,1,0:T(8,128)S(1)}, u32[]{:S(2)}, u32[]{:S(2)}) collective-permute-start(f32[8,136,128]{2,1,0:T(8,128)S(1)} %get-tuple-element.116), channel_id=1, source_target_pairs={{0,4},{1,5},{2,6},{3,7},{4,0},{5,1},{6,2},{7,3},{8,12},{9,13},{10,... | collective-permute-start | bytes 1671176 | tf_op jit(solution)/shard_map/ppermute | solution.py:538
  72.5 1.6 %collective-permute-start.24 = (f32[4,136,128]{2,1,0:T(8,128)S(1)}, f32[4,136,128]{2,1,0:T(8,128)S(1)}, u32[]{:S(2)}, u32[]{:S(2)}) collective-permute-start(f32[4,136,128]{2,1,0:T(8,128)S(1)} %get-tuple-element.119), channel_id=1, source_target_pairs={{0,3},{1,0},{2,1},{3,2},{4,7},{5,4},{6,5},{7,6},{8,11},{9,8},{10,9... | collective-permute-start | bytes 835592 | tf_op jit(solution)/shard_map/ppermute | solution.py:542
  75.2 4.4 %collective-permute-start.28 = (f32[2,136,128]{2,1,0:T(8,128)S(1)}, f32[2,136,128]{2,1,0:T(8,128)S(1)}, u32[]{:S(2)}, u32[]{:S(2)}) collective-permute-start(f32[2,136,128]{2,1,0:T(8,128)S(1)} %get-tuple-element.122), channel_id=1, source_target_pairs={{0,10},{1,11},{2,8},{3,9},{4,14},{5,15},{6,12},{7,13},{8,2},{9,3},... | collective-permute-start | bytes 417800 | tf_op jit(solution)/shard_map/ppermute | solution.py:542
  80.4 6.2 %collective-permute-start.29 = (f32[2,136,128]{2,1,0:T(8,128)S(1)}, f32[2,136,128]{2,1,0:T(8,128)S(1)}, u32[]{:S(2)}, u32[]{:S(2)}) collective-permute-start(f32[2,136,128]{2,1,0:T(8,128)S(1)} %get-tuple-element.123), channel_id=1, source_target_pairs={{0,11},{1,8},{2,9},{3,10},{4,15},{5,12},{6,13},{7,14},{8,3},{9,0},... | collective-permute-start | bytes 417800 | tf_op jit(solution)/shard_map/ppermute | solution.py:542
  86.8 1.9 %collective-permute-done.29.refs_7_ = f32[2,136,128]{2,1,0:T(8,128)S(1)} collective-permute-done((f32[2,136,128]{2,1,0:T(8,128)S(1)}, f32[2,136,128]{2,1,0:T(8,128)S(1)}, u32[]{:S(2)}, u32[]{:S(2)}) %collective-permute-start.29) | collective-permute-done | bytes 139296 | tf_op jit(solution)/shard_map/ppermute | solution.py:542
  88.6 2.9 %collective-permute-done.25.refs_2_ = f32[2,136,128]{2,1,0:T(8,128)S(1)} collective-permute-done((f32[2,136,128]{2,1,0:T(8,128)S(1)}, f32[2,136,128]{2,1,0:T(8,128)S(1)}, u32[]{:S(2)}, u32[]{:S(2)}) %collective-permute-start.25) | collective-permute-done | bytes 139296 | tf_op jit(solution)/shard_map/ppermute | solution.py:543
  91.5 4.0 %shard_map.79 = (f32[128,2048]{1,0:T(8,128)}, f32[8,128]{1,0:T(8,128)S(1)}, f32[16,8,128]{2,1,0:T(8,128)S(1)}) custom-call(s32[1,16]{1,0:T(1,128)S(1)} %copy-done.2, s32[1]{0:T(128)} %bitcast.device_ref, f32[2,136,128]{2,1,0:T(8,128)S(1)} %get-tuple-element.117.refs_0_, f32[2,136,128]{2,1,0:T(8,128)S(1)} %collective-permute-done.23.refs_1_, ...), custom_call_target="tpu_custom_call" | custom-call | flops 2000000000 | bytes 4194304 | tf_op jit(solution)/shard_map/pallas_call | solution.py:506
  95.5 12.6 %all_to_all.5.counts_ref = f32[16,8,128]{2,1,0:T(8,128)S(1)} all-to-all(f32[16,8,128]{2,1,0:T(8,128)S(1)} %get-tuple-element.125), channel_id=1, replica_groups=mesh['maps'=16,'row'=4,'col'=4] {'row','col'}, dimensions={0} | all-to-all | bytes 131072 | tf_op jit(solution)/shard_map/all_to_all | solution.py:535
  (57 shorter events, 22.6 us)
Async XLA Ops:
  2.4 11.0 %collective-permute-start = (f32[128,512]{1,0:T(8,128)S(1)}, f32[128,512]{1,0:T(8,128)S(1)}, u32[]{:S(2)}, u32[]{:S(2)}) collective-permute-start(f32[128,512]{1,0:T(8,128)S(1)} %get-tuple-element.67), channel_id=1, source_target_pairs={{0,3},{1,0},{2,1},{3,2},{4,7},{5,4},{6,5},{7,6},{8,11},{9,8},{10,9... | collective-permute-start | bytes 786440 | tf_op jit(solution)/shard_map/ppermute | solution.py:552
  5.7 12.1 %collective-permute-start.1 = (f32[128,512]{1,0:T(8,128)S(1)}, f32[128,512]{1,0:T(8,128)S(1)}, u32[]{:S(2)}, u32[]{:S(2)}) collective-permute-start(f32[128,512]{1,0:T(8,128)S(1)} %get-tuple-element.68), channel_id=1, source_target_pairs={{0,2},{1,3},{2,0},{3,1},{4,6},{5,7},{6,4},{7,5},{8,10},{9,11},{10,... | collective-permute-start | bytes 786440 | tf_op jit(solution)/shard_map/ppermute | solution.py:552
  6.3 16.1 %collective-permute-start.2 = (f32[128,512]{1,0:T(8,128)S(1)}, f32[128,512]{1,0:T(8,128)S(1)}, u32[]{:S(2)}, u32[]{:S(2)}) collective-permute-start(f32[128,512]{1,0:T(8,128)S(1)} %get-tuple-element.69), channel_id=1, source_target_pairs={{0,1},{1,2},{2,3},{3,0},{4,5},{5,6},{6,7},{7,4},{8,9},{9,10},{10,1... | collective-permute-start | bytes 786440 | tf_op jit(solution)/shard_map/ppermute | solution.py:552
  6.9 20.6 %collective-permute-start.11 = (f32[128,512]{1,0:T(8,128)S(1)}, f32[128,512]{1,0:T(8,128)S(1)}, u32[]{:S(2)}, u32[]{:S(2)}) collective-permute-start(f32[128,512]{1,0:T(8,128)S(1)} %get-tuple-element.100), channel_id=1, source_target_pairs={{0,3},{1,0},{2,1},{3,2},{4,7},{5,4},{6,5},{7,6},{8,11},{9,8},{10,9... | collective-permute-start | bytes 786440 | tf_op jit(solution)/shard_map/ppermute | solution.py:552
  8.9 18.5 %collective-permute-start.12 = (f32[128,512]{1,0:T(8,128)S(1)}, f32[128,512]{1,0:T(8,128)S(1)}, u32[]{:S(2)}, u32[]{:S(2)}) collective-permute-start(f32[128,512]{1,0:T(8,128)S(1)} %get-tuple-element.101), channel_id=1, source_target_pairs={{0,2},{1,3},{2,0},{3,1},{4,6},{5,7},{6,4},{7,5},{8,10},{9,11},{10,... | collective-permute-start | bytes 786440 | tf_op jit(solution)/shard_map/ppermute | solution.py:552
  13.4 18.9 %collective-permute-start.13 = (f32[128,512]{1,0:T(8,128)S(1)}, f32[128,512]{1,0:T(8,128)S(1)}, u32[]{:S(2)}, u32[]{:S(2)}) collective-permute-start(f32[128,512]{1,0:T(8,128)S(1)} %get-tuple-element.102), channel_id=1, source_target_pairs={{0,1},{1,2},{2,3},{3,0},{4,5},{5,6},{6,7},{7,4},{8,9},{9,10},{10,1... | collective-permute-start | bytes 786440 | tf_op jit(solution)/shard_map/ppermute | solution.py:552
  23.5 10.7 %collective-permute-start.3 = (f32[8,128,128]{2,1,0:T(8,128)S(1)}, f32[8,128,128]{2,1,0:T(8,128)S(1)}, u32[]{:S(2)}, u32[]{:S(2)}) collective-permute-start(f32[8,128,128]{2,1,0:T(8,128)S(1)} %get-tuple-element.81), channel_id=1, source_target_pairs={{0,4},{1,5},{2,6},{3,7},{4,0},{5,1},{6,2},{7,3},{8,12},{9,13},{10,... | collective-permute-start | bytes 1572872 | tf_op jit(solution)/shard_map/ppermute | solution.py:538
  34.3 12.8 %collective-permute-start.5 = (f32[4,128,128]{2,1,0:T(8,128)S(1)}, f32[4,128,128]{2,1,0:T(8,128)S(1)}, u32[]{:S(2)}, u32[]{:S(2)}) collective-permute-start(f32[4,128,128]{2,1,0:T(8,128)S(1)} %get-tuple-element.84), channel_id=1, source_target_pairs={{0,3},{1,0},{2,1},{3,2},{4,7},{5,4},{6,5},{7,6},{8,11},{9,8},{10,9... | collective-permute-start | bytes 786440 | tf_op jit(solution)/shard_map/ppermute | solution.py:542
  35.8 12.0 %collective-permute-start.16 = (f32[4,128,128]{2,1,0:T(8,128)S(1)}, f32[4,128,128]{2,1,0:T(8,128)S(1)}, u32[]{:S(2)}, u32[]{:S(2)}) collective-permute-start(f32[4,128,128]{2,1,0:T(8,128)S(1)} %get-tuple-element.107), channel_id=1, source_target_pairs={{0,3},{1,0},{2,1},{3,2},{4,7},{5,4},{6,5},{7,6},{8,11},{9,8},{10,9... | collective-permute-start | bytes 786440 | tf_op jit(solution)/shard_map/ppermute | solution.py:542
  38.7 11.3 %collective-permute-start.8 = (f32[2,128,128]{2,1,0:T(8,128)S(1)}, f32[2,128,128]{2,1,0:T(8,128)S(1)}, u32[]{:S(2)}, u32[]{:S(2)}) collective-permute-start(f32[2,128,128]{2,1,0:T(8,128)S(1)} %get-tuple-element.86), channel_id=1, source_target_pairs={{0,9},{1,10},{2,11},{3,8},{4,13},{5,14},{6,15},{7,12},{8,1},{9,2},... | collective-permute-start | bytes 393224 | tf_op jit(solution)/shard_map/ppermute | solution.py:542
  41.9 8.9 %collective-permute-start.9 = (f32[2,128,128]{2,1,0:T(8,128)S(1)}, f32[2,128,128]{2,1,0:T(8,128)S(1)}, u32[]{:S(2)}, u32[]{:S(2)}) collective-permute-start(f32[2,128,128]{2,1,0:T(8,128)S(1)} %get-tuple-element.87), channel_id=1, source_target_pairs={{0,10},{1,11},{2,8},{3,9},{4,14},{5,15},{6,12},{7,13},{8,2},{9,3},... | collective-permute-start | bytes 393224 | tf_op jit(solution)/shard_map/ppermute | solution.py:542
  43.3 11.3 %collective-permute-start.10 = (f32[2,128,128]{2,1,0:T(8,128)S(1)}, f32[2,128,128]{2,1,0:T(8,128)S(1)}, u32[]{:S(2)}, u32[]{:S(2)}) collective-permute-start(f32[2,128,128]{2,1,0:T(8,128)S(1)} %get-tuple-element.88), channel_id=1, source_target_pairs={{0,11},{1,8},{2,9},{3,10},{4,15},{5,12},{6,13},{7,14},{8,3},{9,0},... | collective-permute-start | bytes 393224 | tf_op jit(solution)/shard_map/ppermute | solution.py:542
  47.1 9.0 %collective-permute-start.15 = (f32[2,128,128]{2,1,0:T(8,128)S(1)}, f32[2,128,128]{2,1,0:T(8,128)S(1)}, u32[]{:S(2)}, u32[]{:S(2)}) collective-permute-start(f32[2,128,128]{2,1,0:T(8,128)S(1)} %get-tuple-element.106), channel_id=1, source_target_pairs={{0,1},{1,2},{2,3},{3,0},{4,5},{5,6},{6,7},{7,4},{8,9},{9,10},{10,1... | collective-permute-start | bytes 393224 | tf_op jit(solution)/shard_map/ppermute | solution.py:542
  47.8 9.2 %collective-permute-start.6 = (f32[2,128,128]{2,1,0:T(8,128)S(1)}, f32[2,128,128]{2,1,0:T(8,128)S(1)}, u32[]{:S(2)}, u32[]{:S(2)}) collective-permute-start(f32[2,128,128]{2,1,0:T(8,128)S(1)} %shard_map.71), channel_id=1, source_target_pairs={{0,3},{1,0},{2,1},{3,2},{4,7},{5,4},{6,5},{7,6},{8,11},{9,8},{10,9... | collective-permute-start | bytes 393224 | tf_op jit(solution)/shard_map/ppermute | solution.py:543
  49.9 10.3 %collective-permute-start.18 = (f32[2,128,128]{2,1,0:T(8,128)S(1)}, f32[2,128,128]{2,1,0:T(8,128)S(1)}, u32[]{:S(2)}, u32[]{:S(2)}) collective-permute-start(f32[2,128,128]{2,1,0:T(8,128)S(1)} %get-tuple-element.108), channel_id=1, source_target_pairs={{0,8},{1,9},{2,10},{3,11},{4,12},{5,13},{6,14},{7,15},{8,0},{9,1},... | collective-permute-start | bytes 393224 | tf_op jit(solution)/shard_map/ppermute | solution.py:542
  50.8 9.4 %collective-permute-start.19 = (f32[2,128,128]{2,1,0:T(8,128)S(1)}, f32[2,128,128]{2,1,0:T(8,128)S(1)}, u32[]{:S(2)}, u32[]{:S(2)}) collective-permute-start(f32[2,128,128]{2,1,0:T(8,128)S(1)} %get-tuple-element.109), channel_id=1, source_target_pairs={{0,9},{1,10},{2,11},{3,8},{4,13},{5,14},{6,15},{7,12},{8,1},{9,2},... | collective-permute-start | bytes 393224 | tf_op jit(solution)/shard_map/ppermute | solution.py:542
  54.5 8.4 %collective-permute-start.20 = (f32[2,128,128]{2,1,0:T(8,128)S(1)}, f32[2,128,128]{2,1,0:T(8,128)S(1)}, u32[]{:S(2)}, u32[]{:S(2)}) collective-permute-start(f32[2,128,128]{2,1,0:T(8,128)S(1)} %get-tuple-element.110), channel_id=1, source_target_pairs={{0,10},{1,11},{2,8},{3,9},{4,14},{5,15},{6,12},{7,13},{8,2},{9,3},... | collective-permute-start | bytes 393224 | tf_op jit(solution)/shard_map/ppermute | solution.py:542
  57.0 9.6 %collective-permute-start.17 = (f32[2,128,128]{2,1,0:T(8,128)S(1)}, f32[2,128,128]{2,1,0:T(8,128)S(1)}, u32[]{:S(2)}, u32[]{:S(2)}) collective-permute-start(f32[2,128,128]{2,1,0:T(8,128)S(1)} %shard_map.75), channel_id=1, source_target_pairs={{0,3},{1,0},{2,1},{3,2},{4,7},{5,4},{6,5},{7,6},{8,11},{9,8},{10,9... | collective-permute-start | bytes 393224 | tf_op jit(solution)/shard_map/ppermute | solution.py:543
  72.5 7.9 %collective-permute-start.24 = (f32[4,136,128]{2,1,0:T(8,128)S(1)}, f32[4,136,128]{2,1,0:T(8,128)S(1)}, u32[]{:S(2)}, u32[]{:S(2)}) collective-permute-start(f32[4,136,128]{2,1,0:T(8,128)S(1)} %get-tuple-element.119), channel_id=1, source_target_pairs={{0,3},{1,0},{2,1},{3,2},{4,7},{5,4},{6,5},{7,6},{8,11},{9,8},{10,9... | collective-permute-start | bytes 835592 | tf_op jit(solution)/shard_map/ppermute | solution.py:542
  74.1 12.5 %collective-permute-start.23 = (f32[2,136,128]{2,1,0:T(8,128)S(1)}, f32[2,136,128]{2,1,0:T(8,128)S(1)}, u32[]{:S(2)}, u32[]{:S(2)}) collective-permute-start(f32[2,136,128]{2,1,0:T(8,128)S(1)} %get-tuple-element.118), channel_id=1, source_target_pairs={{0,1},{1,2},{2,3},{3,0},{4,5},{5,6},{6,7},{7,4},{8,9},{9,10},{10,1... | collective-permute-start | bytes 417800 | tf_op jit(solution)/shard_map/ppermute | solution.py:542
  74.1 12.6 %collective-permute-start.26 = (f32[2,136,128]{2,1,0:T(8,128)S(1)}, f32[2,136,128]{2,1,0:T(8,128)S(1)}, u32[]{:S(2)}, u32[]{:S(2)}) collective-permute-start(f32[2,136,128]{2,1,0:T(8,128)S(1)} %get-tuple-element.120), channel_id=1, source_target_pairs={{0,8},{1,9},{2,10},{3,11},{4,12},{5,13},{6,14},{7,15},{8,0},{9,1},... | collective-permute-start | bytes 417800 | tf_op jit(solution)/shard_map/ppermute | solution.py:542
  74.9 11.9 %collective-permute-start.27 = (f32[2,136,128]{2,1,0:T(8,128)S(1)}, f32[2,136,128]{2,1,0:T(8,128)S(1)}, u32[]{:S(2)}, u32[]{:S(2)}) collective-permute-start(f32[2,136,128]{2,1,0:T(8,128)S(1)} %get-tuple-element.121), channel_id=1, source_target_pairs={{0,9},{1,10},{2,11},{3,8},{4,13},{5,14},{6,15},{7,12},{8,1},{9,2},... | collective-permute-start | bytes 417800 | tf_op jit(solution)/shard_map/ppermute | solution.py:542
  75.2 11.5 %collective-permute-start.28 = (f32[2,136,128]{2,1,0:T(8,128)S(1)}, f32[2,136,128]{2,1,0:T(8,128)S(1)}, u32[]{:S(2)}, u32[]{:S(2)}) collective-permute-start(f32[2,136,128]{2,1,0:T(8,128)S(1)} %get-tuple-element.122), channel_id=1, source_target_pairs={{0,10},{1,11},{2,8},{3,9},{4,14},{5,15},{6,12},{7,13},{8,2},{9,3},... | collective-permute-start | bytes 417800 | tf_op jit(solution)/shard_map/ppermute | solution.py:542
  80.4 8.2 %collective-permute-start.29 = (f32[2,136,128]{2,1,0:T(8,128)S(1)}, f32[2,136,128]{2,1,0:T(8,128)S(1)}, u32[]{:S(2)}, u32[]{:S(2)}) collective-permute-start(f32[2,136,128]{2,1,0:T(8,128)S(1)} %get-tuple-element.123), channel_id=1, source_target_pairs={{0,11},{1,8},{2,9},{3,10},{4,15},{5,12},{6,13},{7,14},{8,3},{9,0},... | collective-permute-start | bytes 417800 | tf_op jit(solution)/shard_map/ppermute | solution.py:542
  (9 other events, 79.9 us)
